TPU v7x, 512 devices: a 8x2x16 block of a 8x8x16 slice. The times are simulated.
512 devices in a mesh: rep: 2 (over y), exp: 16 (over x, core), tp: 16 (over z).
Axes of the slice: x: 8, y: 2, z: 16, core: 2. Of those that a mesh axis runs over, the one named last changes fastest.
The devices are a block of a 8x8x16 slice.
Arguments:
- tokens: bfloat16 [1024, 6144], P(('rep', 'exp'), 'tp'), parts along dimension 0, may hold values from -6 to 6
- expert_ids: int32 [1024, 2], P(('rep', 'exp')), parts along dimension 0, may hold values from 0 to 3, all different within a row; in each aligned block of 32 rows (0 to 31, 32 to 63, ...) at most 20 rows name the same one
- route_logits: float32 [1024, 2], P(('rep', 'exp')), parts along dimension 0, may hold values from -6 to 6
- gate_weight: bfloat16 [6144, 32768], P(None, ('exp', 'tp')), may hold values from -0.078125 to 0.078125
- up_weight: bfloat16 [6144, 32768], P(None, ('exp', 'tp')), may hold values from -0.078125 to 0.078125
- down_weight: bfloat16 [32768, 6144], P(('exp', 'tp')), may hold values from -0.0625 to 0.0625
Outputs:
- moe_out: bfloat16 [1024, 6144], P(('rep', 'exp'), 'tp'), parts along dimension 0
There are 2 independent parts, one for each index of `rep`. A program takes and returns all parts, laid end to end along the dimension named above; an argument that names none is the same for every part. Nothing has to cross between parts.
Inputs may be any that keep to these rules, and one draw needn't show every extreme that they name: `expert_ids`: each token names two different experts. In each aligned block of 32 tokens no expert is named by more than 20 tokens, a bound that some block reaches.
All inputs are finite; a program needn't handle non-finite values.
Results may differ from a plain program's by a relative error of at most 0.019.
Values may be sent and summed in bfloat16 or wider, within the bound.
No kernel may reach another device: no remote copies, remote signals or barrier semaphores. Data moves between devices by JAX's collectives and lax.ppermute only.
A program may use at most 64 MiB of HBM per device.

v0:
```python
import jax
import jax.numpy as jnp
from jax import lax
from jax.sharding import PartitionSpec as P

D = 6144
EXPERTS = 4
CAP = 20


def cut_along(x, dim, devices):
    shape = x.shape
    blocks = x.reshape(*shape[:dim], devices, shape[dim] // devices, *shape[dim + 1 :])
    return jnp.moveaxis(blocks, dim, 0)


def sum_at_owner(x, axis, dim):
    devices = lax.axis_size(axis)
    blocks = lax.all_to_all(cut_along(x, dim, devices), axis, 0, 0, tiled=True)
    return jnp.sum(blocks.astype(jnp.float32), axis=0)


def slot_tables(expert_ids, route_logits):
    chosen = (expert_ids[:, :, None] == jnp.arange(EXPERTS, dtype=jnp.int32)[None, None, :]).astype(
        jnp.int32
    )
    per_token = jnp.sum(chosen, axis=1)
    before = jnp.cumsum(per_token, axis=0) - per_token
    position = jnp.sum(chosen * before[:, None, :], axis=2)
    at_slot = (position[:, :, None] == jnp.arange(CAP, dtype=jnp.int32)[None, None, :]).astype(
        jnp.float32
    )
    chosen_f = chosen.astype(jnp.float32)
    diff = route_logits[:, 0] - route_logits[:, 1]
    shares = jnp.stack([jax.nn.sigmoid(diff), jax.nn.sigmoid(-diff)], axis=1)
    placement = jnp.einsum("tke,tkc->ect", chosen_f, at_slot)
    mixing = jnp.einsum("tk,tke,tkc->tec", shares, chosen_f, at_slot)
    return (placement.astype(jnp.bfloat16), mixing)


def on_device(tokens, expert_ids, route_logits, gate_weight, up_weight, down_weight):
    exp_count = lax.axis_size("exp")
    groups = exp_count // EXPERTS
    placement, mixing = slot_tables(expert_ids, route_logits)
    slots = jnp.einsum("ect,td->ecd", placement, tokens, preferred_element_type=jnp.float32).astype(
        jnp.bfloat16
    )
    outgoing = jnp.repeat(slots, groups, axis=0)
    incoming = lax.all_to_all(outgoing, "exp", split_axis=0, concat_axis=0, tiled=True)
    gathered = lax.all_gather(incoming, "tp", axis=2, tiled=True)
    slot_rows = gathered.reshape(exp_count * CAP, D)
    gate_act = jnp.dot(slot_rows, gate_weight, preferred_element_type=jnp.float32)
    up_act = jnp.dot(slot_rows, up_weight, preferred_element_type=jnp.float32)
    hidden = (jax.nn.silu(gate_act) * up_act).astype(jnp.bfloat16)
    partial_value = jnp.dot(hidden, down_weight, preferred_element_type=jnp.float32).astype(
        jnp.bfloat16
    )
    partial_value = lax.optimization_barrier(partial_value).reshape(exp_count, CAP, D)
    returned = lax.all_to_all(partial_value, "exp", split_axis=0, concat_axis=0, tiled=True)
    summed = jnp.sum(returned.astype(jnp.float32).reshape(EXPERTS, groups, CAP, D), axis=1)
    combined = jnp.einsum("tec,ecd->td", mixing, summed)
    moe_out = sum_at_owner(combined.astype(jnp.bfloat16), "tp", 1).astype(jnp.bfloat16)
    return moe_out


def solution(mesh):
    return jax.shard_map(
        on_device,
        mesh=mesh,
        in_specs=(
            P(("rep", "exp"), "tp"),
            P(("rep", "exp"), None),
            P(("rep", "exp"), None),
            P(None, ("exp", "tp")),
            P(None, ("exp", "tp")),
            P(("exp", "tp"), None),
        ),
        out_specs=P(("rep", "exp"), "tp"),
        check_vma=False,
    )
```

profile of v0, /device:TPU:80, one launch (start us, length us, event | category | flops | bytes accessed | tf_op | source)
XLA Modules:
  0.0 320.6 jit_solution(2993547651281507378)
XLA Ops:
  6.6 0.0 all-gather.2.cloned.1.call-start
  6.6 0.9 copy.12
  7.4 0.1 convert_reduce_fusion.1
  7.6 0.1 reduce_window_sum.11
  7.6 0.7 select_reduce_fusion
  8.3 0.4 fusion.2
  8.7 0.9 convolution_convert_fusion.1
  9.7 19.1 %all_to_all.15 = bf16[16,20,384]{2,1,0:T(8,128)(2,1)} all-to-all(bf16[16,20,384]{2,1,0:T(8,128)(2,1)S(1)} %bitcast.28), channel_id=1, replica_groups=mesh['rep'=2,'exp'=16,'tp'=16] {'exp'}, dimensions={0} | all-to-all | bytes 491520 | tf_op jit(solution)/shard_map/all_to_all | solution.py:49
  28.8 0.1 all-gather.2.cloned.1.call-update
  28.8 0.0 copy-start.1
  28.8 112.3 %all-gather.2.cloned.1.call-done = bf16[16,20,6144]{2,1,0:T(8,128)(2,1)} async-done(((bf16[16,20,384]{2,1,0:T(8,128)(2,1)}), bf16[16,20,6144]{2,1,0:T(8,128)(2,1)}) %all-gather.2.cloned.1.call-update) | async-done | bytes 3932176 | tf_op jit(solution)/shard_map/all_gather | solution.py:50
  141.1 7.0 %reshape.30 = bf16[320,6144]{1,0:T(8,128)(2,1)} reshape(bf16[16,20,6144]{2,1,0:T(8,128)(2,1)} %all-gather.2.cloned.1.call-done) | data formatting | bytes 7864320 | tf_op jit(solution)/shard_map/reshape | solution.py:51
  148.1 3.3 %fusion.21 = f32[320,128]{1,0:T(8,128)S(1)} fusion(bf16[320,6144]{1,0:T(8,128)(2,1)} %reshape.30, bf16[6144,128]{1,0:T(8,128)(2,1)S(1)} %copy-done.1), kind=kOutput, calls=%fused_computation.36 | convolution fusion | flops 503316480 | bytes 5668864 | tf_op jit(solution)/shard_map/dot_general | solution.py:52
  151.4 8.7 %convolution_convert_fusion = bf16[320,6144]{1,0:T(8,128)(2,1)} fusion(bf16[128,6144]{1,0:T(8,128)(2,1)S(1)} %copy-done, bf16[320,6144]{1,0:T(8,128)(2,1)} %reshape.30, bf16[6144,128]{1,0:T(8,128)(2,1)} %param.10, f32[320,128]{1,0:T(8,128)S(1)} %fusion.21), kind=kOutput, calls=%fused_computation.1 | convolution fusion | flops 1008844800 | bytes 11173888 | tf_op jit(solution)/shard_map/dot_general | solution.py:55
  160.1 6.9 %reshape.31 = bf16[16,20,6144]{2,1,0:T(8,128)(2,1)} reshape(bf16[320,6144]{1,0:T(8,128)(2,1)} %convolution_convert_fusion) | data formatting | bytes 7864320 | tf_op jit(solution)/shard_map/reshape | solution.py:58
  167.0 7.1 %all-to-all-start.1 = ((bf16[16,20,6144]{2,1,0:T(8,128)(2,1)}), bf16[16,20,6144]{2,1,0:T(8,128)(2,1)}, u32[]{:S(2)}, u32[]{:S(2)}) async-start(bf16[16,20,6144]{2,1,0:T(8,128)(2,1)} %reshape.31), calls=%async_computation.1 | async-start | bytes 9437184 | tf_op jit(solution)/shard_map/all_to_all | solution.py:59
  174.2 0.1 copy.11
  174.3 0.4 fusion.11
  174.7 104.8 %all-to-all-done.1 = bf16[16,20,6144]{2,1,0:T(8,128)(2,1)} async-done(((bf16[16,20,6144]{2,1,0:T(8,128)(2,1)}), bf16[16,20,6144]{2,1,0:T(8,128)(2,1)}, u32[]{:S(2)}, u32[]{:S(2)}) %all-to-all-start.1) | async-done | bytes 3932192 | tf_op jit(solution)/shard_map/all_to_all | solution.py:59
  279.5 3.2 %convert_reduce_fusion = bf16[4,20,6144]{2,1,0:T(8,128)(2,1)S(1)} fusion(bf16[16,20,6144]{2,1,0:T(8,128)(2,1)} %all-to-all-done.1), kind=kLoop, calls=%fused_computation | loop fusion | flops 3440640 | bytes 4915200 | tf_op jit(solution)/shard_map/reduce_sum | solution.py:60
  282.8 0.5 fusion
  283.3 0.1 copy.22
  283.3 29.7 %all_to_all.16 = bf16[16,32,384]{2,1,0:T(8,128)(2,1)S(1)} all-to-all(bf16[16,32,384]{2,1,0:T(8,128)(2,1)S(1)} %bitcast.26), channel_id=1, replica_groups=mesh['rep'=2,'exp'=16,'tp'=16] {'tp'}, dimensions={0} | all-to-all | bytes 786432 | tf_op jit(solution)/shard_map/all_to_all | solution.py:19
  313.1 0.7 reduce_sum.42
  (9 shorter events, 0.1 us)
Async XLA Ops:
  6.5 144.8 %copy-start = (bf16[128,6144]{1,0:T(8,128)(2,1)S(1)}, bf16[128,6144]{1,0:T(8,128)(2,1)}, u32[]{:S(2)}) copy-start(bf16[128,6144]{1,0:T(8,128)(2,1)} %param.11) | copy-start | bytes 4718596
  6.6 134.5 %all-gather.2.cloned.1.call-start = ((), (), s32[]{:S(2)}) async-start(), calls=%async_computation.3 | async-start | bytes 5013504 | tf_op jit(solution)/shard_map/all_gather | solution.py:50
  28.8 119.2 %copy-start.1 = (bf16[6144,128]{1,0:T(8,128)(2,1)S(1)}, bf16[6144,128]{1,0:T(8,128)(2,1)}, u32[]{:S(2)}) copy-start(bf16[6144,128]{1,0:T(8,128)(2,1)} %param.9) | copy-start | bytes 4718596
  167.0 7.2 %copy-start.2 = (f32[32,2]{0,1:T(2,128)S(1)}, f32[32,2]{0,1:T(2,128)}, u32[]{:S(2)}) copy-start(f32[32,2]{0,1:T(2,128)} %param.8) | copy-start | bytes 772
  167.0 112.6 %all-to-all-start.1 = ((bf16[16,20,6144]{2,1,0:T(8,128)(2,1)}), bf16[16,20,6144]{2,1,0:T(8,128)(2,1)}, u32[]{:S(2)}, u32[]{:S(2)}) async-start(bf16[16,20,6144]{2,1,0:T(8,128)(2,1)} %reshape.31), calls=%async_computation.1 | async-start | bytes 9437184 | tf_op jit(solution)/shard_map/all_to_all | solution.py:59
Sparse Core Ops, SparseCore 0:
  28.9 112.1 all-gather.1
where the time goes:
time: 323 us; the launch traced here: 321 us
  waiting for transfers between devices  217 us (67%)
  blocking collectives  48.8 us (15%)
  local copies, waits for them, and re-layouts  14.9 us (5%)
  matrix products  14.3 us (4%)
  between operations  13.5 us (4%)
  starting transfers between devices  7.15 us (2%)
  other arithmetic  4.76 us (1%)
    all_gather x1, waiting for transfers between devices, on_device(): gathered = lax.all_gather(incoming, 'tp', axis=2, tiled=True)  112 us
    all_to_all x1, waiting for transfers between devices, on_device(): lax.all_to_all(partial_value, 'exp', split_axis=0, concat_axis=0, tiled=T...  105 us
    all_to_all x1, blocking collectives, sum_at_owner(): blocks = lax.all_to_all(cut_along(x, dim, devices), axis, 0, 0, tiled=True)  29.7 us
    all_to_all x1, blocking collectives, on_device(): lax.all_to_all(outgoing, 'exp', split_axis=0, concat_axis=0, tiled=True)  19.1 us
    dot_general x1, matrix products, on_device(): jnp.dot(hidden, down_weight, preferred_element_type=jnp.float32)  8.73 us
    all_to_all x1, starting transfers between devices, on_device(): lax.all_to_all(partial_value, 'exp', split_axis=0, concat_axis=0, tiled=T...  7.15 us
    reshape x1, local copies, waits for them, and re-layouts, on_device(): slot_rows = gathered.reshape(exp_count * CAP, D)  6.97 us
    reshape x1, local copies, waits for them, and re-layouts, on_device(): lax.optimization_barrier(partial_value).reshape(exp_count, CAP, D)  6.87 us
  transfers between devices with their start and end apart: 2, of which 2 were waited for; matrix products, arithmetic and copies ran while one was open for 0% of the time, Pallas kernels for 0%

commit v1 on v0

v1 whole, which is shorter than its diff:
```python
import functools

import jax
import jax.numpy as jnp
from jax import lax
from jax.experimental import pallas as pl
from jax.experimental.pallas import tpu as pltpu
from jax.sharding import Mesh, PartitionSpec as P

EXPERTS = 4
CAP = 20
QUARTERS = 4
CORES = 2


def cost(flops, nbytes):
    return pl.CostEstimate(flops=flops, bytes_accessed=nbytes, transcendentals=0)


def count_at_least(index, width, parts):
    total = jnp.zeros_like(index)
    for k in range(1, parts):
        total = total + (index >= k * width).astype(jnp.int32)
    return total


def placed(ids, expert, slot, before):
    chosen = ((ids[0:1, :] == expert) | (ids[1:2, :] == expert)).astype(jnp.float32)
    position = jnp.dot(chosen, before, preferred_element_type=jnp.float32)
    return chosen * (position == slot.astype(jnp.float32)).astype(jnp.float32)


def dispatch_kernel(chips, ids_ref, tokens_ref, out_ref):
    count = tokens_ref.shape[0]
    rows = EXPERTS * CAP
    row = lax.broadcasted_iota(jnp.int32, (rows, count), 0)
    expert = count_at_least(row, CAP, EXPERTS)
    slot = row - CAP * expert
    first = lax.broadcasted_iota(jnp.int32, (count, count), 0)
    second = lax.broadcasted_iota(jnp.int32, (count, count), 1)
    before = (first < second).astype(jnp.float32)
    placement = placed(ids_ref[...], expert, slot, before).astype(jnp.bfloat16)
    slots = jnp.dot(placement, tokens_ref[...], preferred_element_type=jnp.float32).astype(
        jnp.bfloat16
    )
    per_expert = chips // EXPERTS
    for chip in range(chips):
        e = chip // per_expert
        out_ref[chip] = slots[e * CAP : (e + 1) * CAP]


def dispatch(ids, tokens, chips):
    features = tokens.shape[1]
    return pl.pallas_call(
        functools.partial(dispatch_kernel, chips),
        out_shape=jax.ShapeDtypeStruct((chips, CAP, features), jnp.bfloat16),
        cost_estimate=cost(2 * 80 * 32 * features, 200000),
        compiler_params=pltpu.CompilerParams(vmem_limit_bytes=4 << 20),
        name="dispatch",
    )(ids, tokens)


def mixing_kernel(chips, count, ids_ref, logits_ref, out_ref):
    lanes = ids_ref.shape[1]
    rows = chips * QUARTERS * CAP
    row = lax.broadcasted_iota(jnp.int32, (rows, lanes), 0)
    chip = count_at_least(row, QUARTERS * CAP, chips)
    rest = row - QUARTERS * CAP * chip
    quarter = count_at_least(rest, CAP, QUARTERS)
    slot = rest - CAP * quarter
    expert = count_at_least(chip, chips // EXPERTS, EXPERTS)
    lane = lax.broadcasted_iota(jnp.int32, (rows, lanes), 1)
    own = (count_at_least(lane, count, QUARTERS) == quarter).astype(jnp.float32)
    first = lax.broadcasted_iota(jnp.int32, (lanes, lanes), 0)
    second = lax.broadcasted_iota(jnp.int32, (lanes, lanes), 1)
    same = count_at_least(first, count, QUARTERS) == count_at_least(second, count, QUARTERS)
    before = ((first < second) & same).astype(jnp.float32)
    ids = ids_ref[...]
    diff = logits_ref[0:1, :] - logits_ref[1:2, :]
    share = jnp.where(ids[0:1, :] == expert, jax.nn.sigmoid(diff), jax.nn.sigmoid(-diff))
    out_ref[...] = (placed(ids, expert, slot, before) * share * own).astype(jnp.bfloat16)


def mixing(ids, logits, chips):
    count = ids.shape[1]
    rows = chips * QUARTERS * CAP
    return pl.pallas_call(
        functools.partial(mixing_kernel, chips, count),
        out_shape=jax.ShapeDtypeStruct((rows, QUARTERS * count), jnp.bfloat16),
        cost_estimate=cost(2 * rows * 128 * 128, 200000),
        compiler_params=pltpu.CompilerParams(vmem_limit_bytes=8 << 20),
        name="mixing",
    )(jnp.tile(ids, (1, QUARTERS)), jnp.tile(logits, (1, QUARTERS)))


def ffn_kernel(
    steps, chips, low_ref, high_ref, gate_ref, gate2_ref, up_ref, up2_ref, down_ref, down2_ref, out_ref, total, hidden
):
    step = pl.program_id(0)
    half = low_ref.shape[1]
    depth = low_ref.shape[2]
    blocks = low_ref.shape[0]

    @pl.when(step == 0)
    def _():
        total[...] = jnp.zeros_like(total)

    @pl.when(step < steps)
    def _():
        for part, ref in enumerate((low_ref, high_ref)):
            rows = slice(part * half, (part + 1) * half)
            added = total[rows]
            for b in range(blocks):
                k = slice(b * depth, (b + 1) * depth)
                weight = jnp.concatenate(
                    [gate_ref[k], gate2_ref[k], up_ref[k], up2_ref[k]], axis=1
                )
                added = added + jnp.dot(ref[b], weight, preferred_element_type=jnp.float32)
            total[rows] = added

    @pl.when(step == steps - 1)
    def _():
        width = total.shape[1] // 2
        gate = total[:, :width]
        hidden[...] = (gate * jax.nn.sigmoid(gate) * total[:, width:]).astype(jnp.bfloat16)

    for q in range(QUARTERS):

        @pl.when(step == steps + q)
        def _(q=q):
            weight = jnp.concatenate([down_ref[...], down2_ref[...]], axis=0)
            partial = jnp.dot(hidden[...], weight, preferred_element_type=jnp.float32)
            for chip in range(chips):
                out_ref[chip, q * CAP : (q + 1) * CAP, :] = partial[
                    chip * CAP : (chip + 1) * CAP
                ].astype(jnp.bfloat16)


def ffn(low, high, gate, gate2, up, up2, down, down2, chips):
    parts, half, depth = low.shape
    model, width = gate.shape
    steps = 4
    blocks = parts // steps
    quarter = model // QUARTERS
    rows = 2 * half
    into = lambda i: (jnp.minimum(i, steps - 1), 0, 0)
    weights = pl.BlockSpec((blocks * depth, width), lambda i: (jnp.minimum(i, steps - 1), 0))
    downs = pl.BlockSpec((width, quarter), lambda i: (0, jnp.maximum(i - steps, 0)))
    tokens_in = pl.BlockSpec((blocks, half, depth), into)
    return pl.pallas_call(
        functools.partial(ffn_kernel, steps, chips),
        grid=(steps + QUARTERS,),
        in_specs=[tokens_in, tokens_in, weights, weights, weights, weights, downs, downs],
        out_specs=pl.BlockSpec((chips, QUARTERS * CAP, quarter), lambda i: (0, 0, 0)),
        out_shape=jax.ShapeDtypeStruct((chips, QUARTERS * CAP, quarter), jnp.bfloat16),
        scratch_shapes=[
            pltpu.VMEM((rows, 4 * width), jnp.float32),
            pltpu.VMEM((rows, 2 * width), jnp.bfloat16),
        ],
        cost_estimate=cost(2 * rows * model * width * 6, 14000000),
        compiler_params=pltpu.CompilerParams(vmem_limit_bytes=24 << 20),
        name="ffn",
    )(low, high, gate, gate2, up, up2, down, down2)


def combine_kernel(mix_ref, back_ref, out_ref):
    blocks, count, depth = out_ref.shape
    per_quarter = blocks // QUARTERS
    summed = lax.dot_general(
        mix_ref[...], back_ref[...], (((0,), (0,)), ((), ())), preferred_element_type=jnp.float32
    ).astype(jnp.bfloat16)
    for q in range(QUARTERS):
        for s in range(per_quarter):
            out_ref[q * per_quarter + s] = summed[
                q * count : (q + 1) * count, s * depth : (s + 1) * depth
            ]


def combine(mix, back, count, blocks):
    rows, quarter = back.shape
    depth = QUARTERS * quarter // blocks
    return pl.pallas_call(
        combine_kernel,
        out_shape=jax.ShapeDtypeStruct((blocks, count, depth), jnp.bfloat16),
        cost_estimate=cost(2 * rows * quarter * 128, 2400000),
        compiler_params=pltpu.CompilerParams(vmem_limit_bytes=12 << 20),
        name="combine",
    )(mix, back)


def on_device(tokens, expert_ids, route_logits, gate_weight, up_weight, down_weight):
    chips = lax.axis_size("x")
    parts = lax.axis_size("tp")
    count, depth = tokens.shape
    swap = [(0, 1), (1, 0)]
    ids = expert_ids.T
    outgoing = dispatch(ids, tokens, chips)
    incoming = lax.all_to_all(outgoing, "x", 0, 0, tiled=True)
    gate2 = lax.ppermute(gate_weight, "core", swap)
    up2 = lax.ppermute(up_weight, "core", swap)
    down2 = lax.ppermute(down_weight, "core", swap)
    rows = incoming.reshape(2, chips * CAP // 2, depth)
    low = lax.all_gather(rows[0], "tp")
    high = lax.all_gather(rows[1], "tp")
    partial_value = ffn(low, high, gate_weight, gate2, up_weight, up2, down_weight, down2, chips)
    returned = lax.all_to_all(partial_value, "x", 0, 0, tiled=True)
    mix = mixing(ids, route_logits.T, chips)
    back = returned.reshape(chips * QUARTERS * CAP, parts * depth // QUARTERS)
    combined = combine(mix, back, count, parts)
    blocks = lax.all_to_all(combined, "tp", 0, 0, tiled=True)
    return jnp.sum(blocks.astype(jnp.float32), axis=0).astype(jnp.bfloat16)


def solution(mesh):
    sizes = [mesh.shape[axis] for axis in ("rep", "exp", "tp")]
    devices = mesh.devices.reshape(sizes[0], sizes[1] // CORES, CORES, sizes[2])
    split = Mesh(devices, ("rep", "x", "core", "tp"))
    tokens = ("rep", "x", "core")
    hidden = ("x", "core", "tp")
    return jax.shard_map(
        on_device,
        mesh=split,
        in_specs=(
            P(tokens, "tp"),
            P(tokens, None),
            P(tokens, None),
            P(None, hidden),
            P(None, hidden),
            P(hidden, None),
        ),
        out_specs=P(tokens, "tp"),
        check_vma=False,
    )
```

time: 323 us -> 202 us (0.63)
  waiting for transfers between devices: 217 us -> 34.3 us
  blocking collectives: 48.8 us -> 142 us
  matrix products: 14.3 us -> 0 us
  between operations: 13.5 us -> 0.12 us
  local copies, waits for them, and re-layouts: 14.9 us -> 4.45 us
  Pallas kernels: 0 us -> 9.36 us
  other arithmetic: 4.76 us -> 0.67 us
  starting transfers between devices: 7.15 us -> 10.4 us
    all_gather x1 -> x0, waiting for transfers between devices: 112 us -> none  [on_device(): gathered = lax.all_gather(incoming, 'tp', axis=2, tiled=True)]
    all_gather x0 -> x2, blocking collectives: none -> 106 us  [the longest x1 74.8 us: on_device(): low = lax.all_gather(rows[0], 'tp')]
    all_to_all x1, waiting for transfers between devices: 105 us -> 34.3 us  [on_device(): returned = lax.all_to_all(partial_value, 'x', 0, 0, tiled=True)]
    dot_general x6 -> x0, matrix products: 14.3 us -> none  [the longest x1 8.73 us: on_device(): jnp.dot(hidden, down_weight, preferred_element_type=jnp.float32)]
    reshape x3 -> x0, local copies, waits for them, and re-layouts: 13.9 us -> none  [the longest x1 6.97 us: on_device(): slot_rows = gathered.reshape(exp_count * CAP, D)]
    all_to_all x2, blocking collectives: 48.8 us -> 35.8 us  [the longest x1 18.6 us: on_device(): blocks = lax.all_to_all(combined, 'tp', 0, 0, tiled=True)]
    pallas_call x0 -> x4, Pallas kernels: none -> 9.36 us  [the longest x1 8.38 us: ffn(): pl.pallas_call(functools.partial(ffn_kernel, steps, chips), grid=(steps +...]
    ppermute x0 -> x3, starting transfers between devices: none -> 6.47 us  [the longest x1 2.44 us: on_device(): up2 = lax.ppermute(up_weight, 'core', swap)]
  transfers between devices with their start and end apart: 2 -> 4, of which waited for: 2 -> 1; matrix products, arithmetic and copies ran while one was open for 0% -> 0% of each run, Pallas kernels for 0% -> 0%
where the time goes in v1:
time: 202 us
  blocking collectives  142 us (70%)
  waiting for transfers between devices  34.3 us (17%)
  starting transfers between devices  10.4 us (5%)
  Pallas kernels  9.36 us (5%)
  local copies, waits for them, and re-layouts  4.45 us (2%)
    all_gather x1, blocking collectives, on_device(): low = lax.all_gather(rows[0], 'tp')  74.8 us
    all_to_all x1, waiting for transfers between devices, on_device(): returned = lax.all_to_all(partial_value, 'x', 0, 0, tiled=True)  34.3 us
    all_gather x1, blocking collectives, on_device(): high = lax.all_gather(rows[1], 'tp')  31.7 us
    all_to_all x1, blocking collectives, on_device(): blocks = lax.all_to_all(combined, 'tp', 0, 0, tiled=True)  18.6 us
    all_to_all x1, blocking collectives, on_device(): incoming = lax.all_to_all(outgoing, 'x', 0, 0, tiled=True)  17.2 us
    pallas_call x1, Pallas kernels, ffn(): pl.pallas_call(functools.partial(ffn_kernel, steps, chips), grid=(steps +...  8.38 us
    unnamed x14, local copies, waits for them, and re-layouts  4.23 us
  transfers between devices with their start and end apart: 4, of which 1 were waited for; matrix products, arithmetic and copies ran while one was open for 0% of the time, Pallas kernels for 0%

profile of v1, /device:TPU:80, one launch (start us, length us, event | category | flops | bytes accessed | tf_op | source)
XLA Modules:
  0.0 201.6 jit_solution(9820341821593830653)
XLA Ops:
  0.0 2.1 %collective-permute-start = (bf16[6144,128]{1,0:T(8,128)(2,1)}, bf16[6144,128]{1,0:T(8,128)(2,1)S(1)}, u32[]{:S(2)}, u32[]{:S(2)}) collective-permute-start(bf16[6144,128]{1,0:T(8,128)(2,1)} %gate_ref.1), channel_id=1, source_target_pairs={{0,16},{16,0},{1,17},{17,1},{2,18},{18,2},{3,19},{19,3},{4,20},{20... | collective-permute-start | bytes 4718600 | tf_op jit(solution)/shard_map/ppermute | solution.py:199
  2.1 2.4 %collective-permute-start.1 = (bf16[6144,128]{1,0:T(8,128)(2,1)}, bf16[6144,128]{1,0:T(8,128)(2,1)}, u32[]{:S(2)}, u32[]{:S(2)}) collective-permute-start(bf16[6144,128]{1,0:T(8,128)(2,1)} %up_ref.1), channel_id=1, source_target_pairs={{0,16},{16,0},{1,17},{17,1},{2,18},{18,2},{3,19},{19,3},{4,20},{20... | collective-permute-start | bytes 4718600 | tf_op jit(solution)/shard_map/ppermute | solution.py:200
  4.5 2.0 collective-permute-start.2
  6.5 0.7 copy-done.3
  7.2 0.7 copy-done.4
  7.9 0.3 dispatch.1
  8.2 17.2 %all_to_all.15 = bf16[8,20,384]{2,1,0:T(8,128)(2,1)S(1)} all-to-all(bf16[8,20,384]{2,1,0:T(8,128)(2,1)S(1)} %dispatch.1), channel_id=1, replica_groups=mesh['rep'=2,'x'=8,'core'=2,'tp'=16] {'x'}, dimensions={0} | all-to-all | bytes 245760 | tf_op jit(solution)/shard_map/all_to_all | solution.py:198
  25.4 74.8 %all_gather.6.low_ref = bf16[16,80,384]{2,1,0:T(8,128)(2,1)S(1)} all-gather(bf16[1,80,384]{2,1,0:T(8,128)(2,1)S(1)} %slice.13), channel_id=1, replica_groups=mesh['rep'=2,'x'=8,'core'=2,'tp'=16] {'tp'}, dimensions={0}, use_global_device_ids=true | all-gather | bytes 1044480 | tf_op jit(solution)/shard_map/all_gather | solution.py:203
  100.2 31.7 %all_gather.7.high_ref = bf16[16,80,384]{2,1,0:T(8,128)(2,1)S(1)} all-gather(bf16[1,80,384]{2,1,0:T(8,128)(2,1)S(1)} %slice.15), channel_id=1, replica_groups=mesh['rep'=2,'x'=8,'core'=2,'tp'=16] {'tp'}, dimensions={0}, use_global_device_ids=true | all-gather | bytes 1044480 | tf_op jit(solution)/shard_map/all_gather | solution.py:204
  131.9 0.0 collective-permute-done.gate2_ref
  131.9 0.0 collective-permute-done.1.up2_ref
  131.9 0.0 collective-permute-done.2.down2_ref
  131.9 0.0 copy-start.1
  132.0 1.4 copy-done.1
  133.4 1.4 copy-done.2
  134.8 8.4 %ffn.1 = bf16[8,80,1536]{2,1,0:T(8,128)(2,1)} custom-call(bf16[16,80,384]{2,1,0:T(8,128)(2,1)S(1)} %all_gather.6.low_ref, bf16[16,80,384]{2,1,0:T(8,128)(2,1)S(1)} %all_gather.7.high_ref, bf16[6144,128]{1,0:T(8,128)(2,1)S(1)} %copy-done, bf16[6144,128]{1,0:T(8,128)(2,1)S(1)} %collective-permute-done.gate2_ref, bf16[6144,128]{1,0:T(8,128)(2,1)S(1)} %copy-done.1, ...), custom_call_target="tpu_custom_call" | custom-call | flops 1509949440 | bytes 14000000 | tf_op jit(solution)/shard_map/ffn/pallas_call | solution.py:150
  143.1 3.9 %all-to-all-start.1 = ((bf16[8,80,1536]{2,1,0:T(8,128)(2,1)}), bf16[8,80,1536]{2,1,0:T(8,128)(2,1)S(1)}, u32[]{:S(2)}, u32[]{:S(2)}) async-start(bf16[8,80,1536]{2,1,0:T(8,128)(2,1)} %ffn.1), calls=%async_computation.1 | async-start | bytes 3932160 | tf_op jit(solution)/shard_map/all_to_all | solution.py:206
  147.1 0.1 tile.9.ids_ref
  147.2 0.1 tile.21.logits_ref
  147.3 0.2 mixing.1.mix_ref
  147.5 34.3 %all-to-all-done.1 = bf16[8,80,1536]{2,1,0:T(8,128)(2,1)S(1)} async-done(((bf16[8,80,1536]{2,1,0:T(8,128)(2,1)}), bf16[8,80,1536]{2,1,0:T(8,128)(2,1)S(1)}, u32[]{:S(2)}, u32[]{:S(2)}) %all-to-all-start.1) | async-done | bytes 1966112 | tf_op jit(solution)/shard_map/all_to_all | solution.py:206
  181.8 0.5 combine.1
  182.3 18.6 %all_to_all.16 = bf16[16,32,384]{2,1,0:T(8,128)(2,1)S(1)} all-to-all(bf16[16,32,384]{2,1,0:T(8,128)(2,1)S(1)} %combine.1), channel_id=1, replica_groups=mesh['rep'=2,'x'=8,'core'=2,'tp'=16] {'tp'}, dimensions={0} | all-to-all | bytes 786432 | tf_op jit(solution)/shard_map/all_to_all | solution.py:210
  200.9 0.7 reduce_sum.12
  (14 shorter events, 0.1 us)
Async XLA Ops:
  0.0 131.9 %copy-start = (bf16[6144,128]{1,0:T(8,128)(2,1)S(1)}, bf16[6144,128]{1,0:T(8,128)(2,1)}, u32[]{:S(2)}) copy-start(bf16[6144,128]{1,0:T(8,128)(2,1)} %gate_ref.1) | copy-start | bytes 4718596
  0.0 131.9 %collective-permute-start = (bf16[6144,128]{1,0:T(8,128)(2,1)}, bf16[6144,128]{1,0:T(8,128)(2,1)S(1)}, u32[]{:S(2)}, u32[]{:S(2)}) collective-permute-start(bf16[6144,128]{1,0:T(8,128)(2,1)} %gate_ref.1), channel_id=1, source_target_pairs={{0,16},{16,0},{1,17},{17,1},{2,18},{18,2},{3,19},{19,3},{4,20},{20... | collective-permute-start | bytes 4718600 | tf_op jit(solution)/shard_map/ppermute | solution.py:199
  2.1 129.8 %collective-permute-start.1 = (bf16[6144,128]{1,0:T(8,128)(2,1)}, bf16[6144,128]{1,0:T(8,128)(2,1)}, u32[]{:S(2)}, u32[]{:S(2)}) collective-permute-start(bf16[6144,128]{1,0:T(8,128)(2,1)} %up_ref.1), channel_id=1, source_target_pairs={{0,16},{16,0},{1,17},{17,1},{2,18},{18,2},{3,19},{19,3},{4,20},{20... | collective-permute-start | bytes 4718600 | tf_op jit(solution)/shard_map/ppermute | solution.py:200
  4.5 127.4 %collective-permute-start.2 = (bf16[128,6144]{1,0:T(8,128)(2,1)}, bf16[128,6144]{1,0:T(8,128)(2,1)}, u32[]{:S(2)}, u32[]{:S(2)}) collective-permute-start(bf16[128,6144]{1,0:T(8,128)(2,1)} %down_ref.1), channel_id=1, source_target_pairs={{0,16},{16,0},{1,17},{17,1},{2,18},{18,2},{3,19},{19,3},{4,20},{20... | collective-permute-start | bytes 4718600 | tf_op jit(solution)/shard_map/ppermute | solution.py:201
  6.5 0.7 copy-start.3
  7.2 0.7 copy-start.4
  131.9 1.4 copy-start.1
  133.4 1.4 copy-start.2
  143.1 3.9 %copy-start.5 = (s32[32,2]{0,1:T(2,128)S(1)}, s32[32,2]{0,1:T(2,128)}, u32[]{:S(2)}) copy-start(s32[32,2]{0,1:T(2,128)} %param.7) | copy-start | bytes 772
  143.1 4.0 %copy-start.6 = (f32[32,2]{0,1:T(2,128)S(1)}, f32[32,2]{0,1:T(2,128)}, u32[]{:S(2)}) copy-start(f32[32,2]{0,1:T(2,128)} %param.8) | copy-start | bytes 772
  143.1 38.7 %all-to-all-start.1 = ((bf16[8,80,1536]{2,1,0:T(8,128)(2,1)}), bf16[8,80,1536]{2,1,0:T(8,128)(2,1)S(1)}, u32[]{:S(2)}, u32[]{:S(2)}) async-start(bf16[8,80,1536]{2,1,0:T(8,128)(2,1)} %ffn.1), calls=%async_computation.1 | async-start | bytes 3932160 | tf_op jit(solution)/shard_map/all_to_all | solution.py:206

commit v2 on v1

v2 whole, which is shorter than its diff:
```python
import functools

import jax
import jax.numpy as jnp
from jax import lax
from jax.experimental import pallas as pl
from jax.experimental.pallas import tpu as pltpu
from jax.sharding import Mesh, PartitionSpec as P

EXPERTS = 4
CAP = 20
MAIN = 16
TAIL = CAP - MAIN
QUARTERS = 4
CORES = 2


def cost(flops, nbytes):
    return pl.CostEstimate(flops=flops, bytes_accessed=nbytes, transcendentals=0)


def count_at_least(index, width, parts):
    total = jnp.zeros_like(index)
    for k in range(1, parts):
        total = total + (index >= k * width).astype(jnp.int32)
    return total


def placed(ids, expert, slot, before):
    chosen = ((ids[0:1, :] == expert) | (ids[1:2, :] == expert)).astype(jnp.float32)
    position = jnp.dot(chosen, before, preferred_element_type=jnp.float32)
    return chosen * (position == slot.astype(jnp.float32)).astype(jnp.float32)


def grouped(row, groups):
    later = row >= groups * MAIN
    rest = row - groups * MAIN
    main = count_at_least(row, MAIN, groups)
    tail = count_at_least(rest, TAIL, groups)
    group = jnp.where(later, tail, main)
    slot = jnp.where(later, MAIN + rest - TAIL * tail, row - MAIN * main)
    return group, slot


def dispatch_kernel(chips, ids_ref, tokens_ref, out_ref, image, sems):
    blocks, count, depth = tokens_ref.shape
    per_quarter = blocks // QUARTERS
    per_expert = chips // EXPERTS
    row = lax.broadcasted_iota(jnp.int32, (EXPERTS * CAP, count), 0)
    expert, slot = grouped(row, EXPERTS)
    first = lax.broadcasted_iota(jnp.int32, (count, count), 0)
    second = lax.broadcasted_iota(jnp.int32, (count, count), 1)
    before = (first < second).astype(jnp.float32)
    placement = placed(ids_ref[...], expert, slot, before).astype(jnp.bfloat16)
    for b in range(blocks):
        q, s = b // per_quarter, b % per_quarter
        lanes = slice(s * depth, (s + 1) * depth)
        slots = jnp.dot(placement, tokens_ref[b], preferred_element_type=jnp.float32).astype(
            jnp.bfloat16
        )
        for e in range(EXPERTS):
            image[e, q * MAIN : (q + 1) * MAIN, lanes] = slots[e * MAIN : (e + 1) * MAIN]
            to, at = QUARTERS * MAIN + q * TAIL, EXPERTS * MAIN + e * TAIL
            image[e, to : to + TAIL, lanes] = slots[at : at + TAIL]
    copies = [
        pltpu.make_async_copy(image.at[chip // per_expert], out_ref.at[chip], sems.at[chip])
        for chip in range(chips)
    ]
    for copy in copies:
        copy.start()
    for copy in copies:
        copy.wait()


def dispatch(ids, tokens, chips):
    blocks, count, depth = tokens.shape
    quarter = blocks * depth // QUARTERS
    return pl.pallas_call(
        functools.partial(dispatch_kernel, chips),
        out_shape=jax.ShapeDtypeStruct((chips, QUARTERS * CAP, quarter), jnp.bfloat16),
        out_specs=pl.BlockSpec(memory_space=pltpu.HBM),
        scratch_shapes=[
            pltpu.VMEM((EXPERTS, QUARTERS * CAP, quarter), jnp.bfloat16),
            pltpu.SemaphoreType.DMA((chips,)),
        ],
        cost_estimate=cost(2 * 80 * count * blocks * depth, 2400000),
        compiler_params=pltpu.CompilerParams(vmem_limit_bytes=60 << 20),
        name="dispatch",
    )(ids, tokens)


def mixing_kernel(chips, count, ids_ref, logits_ref, out_ref):
    lanes = ids_ref.shape[1]
    rows = chips * QUARTERS * CAP
    row = lax.broadcasted_iota(jnp.int32, (rows, lanes), 0)
    chip = count_at_least(row, QUARTERS * CAP, chips)
    quarter, slot = grouped(row - QUARTERS * CAP * chip, QUARTERS)
    expert = count_at_least(chip, chips // EXPERTS, EXPERTS)
    lane = lax.broadcasted_iota(jnp.int32, (rows, lanes), 1)
    own = (count_at_least(lane, count, QUARTERS) == quarter).astype(jnp.float32)
    first = lax.broadcasted_iota(jnp.int32, (lanes, lanes), 0)
    second = lax.broadcasted_iota(jnp.int32, (lanes, lanes), 1)
    same = count_at_least(first, count, QUARTERS) == count_at_least(second, count, QUARTERS)
    before = ((first < second) & same).astype(jnp.float32)
    ids = ids_ref[...]
    diff = logits_ref[0:1, :] - logits_ref[1:2, :]
    share = jnp.where(ids[0:1, :] == expert, jax.nn.sigmoid(diff), jax.nn.sigmoid(-diff))
    out_ref[...] = (placed(ids, expert, slot, before) * share * own).astype(jnp.bfloat16)


def mixing(ids, logits, chips):
    count = ids.shape[1]
    rows = chips * QUARTERS * CAP
    return pl.pallas_call(
        functools.partial(mixing_kernel, chips, count),
        out_shape=jax.ShapeDtypeStruct((rows, QUARTERS * count), jnp.bfloat16),
        cost_estimate=cost(2 * rows * 128 * 128, 200000),
        compiler_params=pltpu.CompilerParams(vmem_limit_bytes=8 << 20),
        name="mixing",
    )(jnp.tile(ids, (1, QUARTERS)), jnp.tile(logits, (1, QUARTERS)))


def ffn_kernel(
    slots_ref, gate_ref, gate2_ref, up_ref, up2_ref, down_ref, down2_ref, out_ref, slots, ins, downs, outs, slot_sem, in_sems, out_sems
):
    chips, _, quarter = slots_ref.shape
    width = gate_ref.shape[1]
    mains = QUARTERS * MAIN
    arrival = pltpu.make_async_copy(slots_ref, slots, slot_sem)
    arrival.start()
    first, second = [], []
    for q in range(QUARTERS):
        k = pl.ds(q * quarter, quarter)
        first.append(
            [
                pltpu.make_async_copy(
                    ref.at[k], ins.at[q, :, pl.ds(i * width, width)], in_sems.at[q, i]
                )
                for i, ref in enumerate((gate_ref, gate2_ref, up_ref, up2_ref))
            ]
        )
        second.append(
            [
                pltpu.make_async_copy(
                    ref.at[:, k], downs.at[q, pl.ds(i * width, width)], in_sems.at[q, 4 + i]
                )
                for i, ref in enumerate((down_ref, down2_ref))
            ]
        )
    for group in first + second:
        for copy in group:
            copy.start()
    arrival.wait()
    total = None
    for q in range(QUARTERS):
        at = mains + q * TAIL
        rows = jnp.concatenate(
            [slots[chip, q * MAIN : (q + 1) * MAIN] for chip in range(chips)]
            + [slots[chip, at : at + TAIL] for chip in range(chips)],
            axis=0,
        )
        for copy in first[q]:
            copy.wait()
        added = jnp.dot(rows, ins[q], preferred_element_type=jnp.float32)
        total = added if total is None else total + added
    gate = total[:, : 2 * width]
    hidden = (gate * jax.nn.sigmoid(gate) * total[:, 2 * width :]).astype(jnp.bfloat16)
    for q in range(QUARTERS):
        at = mains + q * TAIL
        for copy in second[q]:
            copy.wait()
        partial = jnp.dot(hidden, downs[q], preferred_element_type=jnp.float32).astype(
            jnp.bfloat16
        )
        for chip in range(chips):
            outs[chip, q * MAIN : (q + 1) * MAIN] = partial[chip * MAIN : (chip + 1) * MAIN]
            tail = chips * MAIN + chip * TAIL
            outs[chip, at : at + TAIL] = partial[tail : tail + TAIL]
    copies = [
        pltpu.make_async_copy(outs.at[chip], out_ref.at[chip], out_sems.at[chip])
        for chip in range(chips)
    ]
    for copy in copies:
        copy.start()
    for copy in copies:
        copy.wait()


def ffn(slots, *weights):
    model, width = weights[0].shape
    chips = slots.shape[0]
    quarter = model // QUARTERS
    hbm = pl.BlockSpec(memory_space=pltpu.HBM)
    return pl.pallas_call(
        ffn_kernel,
        in_specs=[hbm] * 7,
        out_specs=hbm,
        out_shape=jax.ShapeDtypeStruct(slots.shape, jnp.bfloat16),
        scratch_shapes=[
            pltpu.VMEM(slots.shape, jnp.bfloat16),
            pltpu.VMEM((QUARTERS, quarter, 4 * width), jnp.bfloat16),
            pltpu.VMEM((QUARTERS, 2 * width, quarter), jnp.bfloat16),
            pltpu.VMEM(slots.shape, jnp.bfloat16),
            pltpu.SemaphoreType.DMA,
            pltpu.SemaphoreType.DMA((QUARTERS, 6)),
            pltpu.SemaphoreType.DMA((chips,)),
        ],
        cost_estimate=cost(2 * chips * CAP * model * width * 6, 14000000),
        compiler_params=pltpu.CompilerParams(vmem_limit_bytes=60 << 20),
        name="ffn",
    )(slots, *weights)


def combine_kernel(mix_ref, back_ref, out_ref):
    blocks, count, depth = out_ref.shape
    per_quarter = blocks // QUARTERS
    summed = lax.dot_general(
        mix_ref[...], back_ref[...], (((0,), (0,)), ((), ())), preferred_element_type=jnp.float32
    ).astype(jnp.bfloat16)
    for q in range(QUARTERS):
        for s in range(per_quarter):
            out_ref[q * per_quarter + s] = summed[
                q * count : (q + 1) * count, s * depth : (s + 1) * depth
            ]


def combine(mix, back, count, blocks):
    rows, quarter = back.shape
    depth = QUARTERS * quarter // blocks
    return pl.pallas_call(
        combine_kernel,
        out_shape=jax.ShapeDtypeStruct((blocks, count, depth), jnp.bfloat16),
        cost_estimate=cost(2 * rows * quarter * 128, 2400000),
        compiler_params=pltpu.CompilerParams(vmem_limit_bytes=12 << 20),
        name="combine",
    )(mix, back)


def on_device(tokens, expert_ids, route_logits, gate_weight, up_weight, down_weight):
    chips = lax.axis_size("x")
    parts = lax.axis_size("tp")
    count, depth = tokens.shape
    swap = [(0, 1), (1, 0)]
    ids = expert_ids.T
    gathered = lax.all_gather(tokens, "tp")
    outgoing = dispatch(ids, gathered, chips)
    gate, up, down, outgoing = lax.optimization_barrier(
        (gate_weight, up_weight, down_weight, outgoing)
    )
    incoming = lax.all_to_all(outgoing, "x", 0, 0, tiled=True)
    gate2 = lax.ppermute(gate, "core", swap)
    up2 = lax.ppermute(up, "core", swap)
    down2 = lax.ppermute(down, "core", swap)
    partial_value = ffn(incoming, gate, gate2, up, up2, down, down2)
    returned = lax.all_to_all(partial_value, "x", 0, 0, tiled=True)
    mix = mixing(ids, route_logits.T, chips)
    back = returned.reshape(chips * QUARTERS * CAP, parts * depth // QUARTERS)
    combined = combine(mix, back, count, parts)
    blocks = lax.all_to_all(combined, "tp", 0, 0, tiled=True)
    return jnp.sum(blocks.astype(jnp.float32), axis=0).astype(jnp.bfloat16)


def solution(mesh):
    sizes = [mesh.shape[axis] for axis in ("rep", "exp", "tp")]
    devices = mesh.devices.reshape(sizes[0], sizes[1] // CORES, CORES, sizes[2])
    split = Mesh(devices, ("rep", "x", "core", "tp"))
    tokens = ("rep", "x", "core")
    hidden = ("x", "core", "tp")
    return jax.shard_map(
        on_device,
        mesh=split,
        in_specs=(
            P(tokens, "tp"),
            P(tokens, None),
            P(tokens, None),
            P(None, hidden),
            P(None, hidden),
            P(hidden, None),
        ),
        out_specs=P(tokens, "tp"),
        check_vma=False,
    )
```

time: 202 us -> 206 us (1.020)
  blocking collectives: 142 us -> 95.6 us
  waiting for transfers between devices: 34.3 us -> 76.7 us
  starting transfers between devices: 10.4 us -> 17.6 us
  Pallas kernels: 9.36 us -> 12.3 us
    all_gather x2 -> x1, blocking collectives: 106 us -> 72.6 us  [on_device(): gathered = lax.all_gather(tokens, 'tp')]
    all_to_all x0 -> x1, waiting for transfers between devices: none -> 31.6 us  [on_device(): incoming = lax.all_to_all(outgoing, 'x', 0, 0, tiled=True)]
    all_to_all x1 -> x0, blocking collectives: 17.2 us -> none  [on_device(): incoming = lax.all_to_all(outgoing, 'x', 0, 0, tiled=True)]
    all_to_all x1, waiting for transfers between devices: 34.3 us -> 42.5 us  [on_device(): returned = lax.all_to_all(partial_value, 'x', 0, 0, tiled=True)]
    all_to_all x0 -> x1, starting transfers between devices: none -> 7.47 us  [on_device(): incoming = lax.all_to_all(outgoing, 'x', 0, 0, tiled=True)]
    all_to_all x1, blocking collectives: 18.6 us -> 22.9 us  [on_device(): blocks = lax.all_to_all(combined, 'tp', 0, 0, tiled=True)]
    pallas_call x1, Pallas kernels: 0.27 us -> 2.97 us  [dispatch(): pl.pallas_call(functools.partial(dispatch_kernel, chips), out_shape=jax.S...]
    ppermute x3, waiting for transfers between devices: 0.01 us -> 2.53 us  [the longest x1 1.29 us: on_device(): down2 = lax.ppermute(down, 'core', swap)]
  transfers between devices with their start and end apart: 4 -> 5, of which waited for: 1 -> 4; matrix products, arithmetic and copies ran while one was open for 0% -> 0% of each run, Pallas kernels for 0% -> 0%
where the time goes in v2:
time: 206 us
  blocking collectives  95.6 us (46%)
  waiting for transfers between devices  76.7 us (37%)
  starting transfers between devices  17.6 us (9%)
  Pallas kernels  12.3 us (6%)
  local copies, waits for them, and re-layouts  2.66 us (1%)
    all_gather x1, blocking collectives, on_device(): gathered = lax.all_gather(tokens, 'tp')  72.6 us
    all_to_all x1, waiting for transfers between devices, on_device(): returned = lax.all_to_all(partial_value, 'x', 0, 0, tiled=True)  42.5 us
    all_to_all x1, waiting for transfers between devices, on_device(): incoming = lax.all_to_all(outgoing, 'x', 0, 0, tiled=True)  31.6 us
    all_to_all x1, blocking collectives, on_device(): blocks = lax.all_to_all(combined, 'tp', 0, 0, tiled=True)  22.9 us
    pallas_call x1, Pallas kernels, ffn(): pl.pallas_call(ffn_kernel, in_specs=[hbm] * 7, out_specs=hbm, out_shape=j...  8.63 us
    all_to_all x1, starting transfers between devices, on_device(): incoming = lax.all_to_all(outgoing, 'x', 0, 0, tiled=True)  7.47 us
  transfers between devices with their start and end apart: 5, of which 4 were waited for; matrix products, arithmetic and copies ran while one was open for 0% of the time, Pallas kernels for 0%

profile of v2, /device:TPU:80, one launch (start us, length us, event | category | flops | bytes accessed | tf_op | source)
XLA Modules:
  0.0 205.7 jit_solution(5666779089934666224)
XLA Ops:
  0.0 72.6 %all-gather = bf16[512,384]{1,0:T(8,128)(2,1)} all-gather(bf16[32,384]{1,0:T(8,128)(2,1)} %param.6), channel_id=2, replica_groups=mesh['rep'=2,'x'=8,'core'=2,'tp'=16] {'tp'}, dimensions={0}, use_global_device_ids=true | all-gather | bytes 417792 | tf_op jit(solution)/shard_map/all_gather | solution.py:245
  72.6 3.0 %dispatch.1 = bf16[8,80,1536]{2,1,0:T(8,128)(2,1)} custom-call(s32[2,32]{1,0:T(2,128)} %bitcast.6, bf16[16,32,384]{2,1,0:T(8,128)(2,1)} %bitcast.5), custom_call_target="tpu_custom_call" | custom-call | flops 31457280 | bytes 2400000 | tf_op jit(solution)/shard_map/dispatch/pallas_call | solution.py:78
  75.6 0.0 copy-start.1
  75.6 7.5 %all-to-all-start = ((bf16[8,80,1536]{2,1,0:T(8,128)(2,1)}), bf16[8,80,1536]{2,1,0:T(8,128)(2,1)S(1)}, u32[]{:S(2)}, u32[]{:S(2)}) async-start(bf16[8,80,1536]{2,1,0:T(8,128)(2,1)} %dispatch.1), calls=%async_computation | async-start | bytes 3932160 | tf_op jit(solution)/shard_map/all_to_all | solution.py:250
  83.1 2.0 collective-permute-start
  85.1 2.4 %collective-permute-start.1 = (bf16[6144,128]{1,0:T(8,128)(2,1)}, bf16[6144,128]{1,0:T(8,128)(2,1)S(1)}, u32[]{:S(2)}, u32[]{:S(2)}) collective-permute-start(bf16[6144,128]{1,0:T(8,128)(2,1)} %up_ref), channel_id=1, source_target_pairs={{0,16},{16,0},{1,17},{17,1},{2,18},{18,2},{3,19},{19,3},{4,20},{20... | collective-permute-start | bytes 4718600 | tf_op jit(solution)/shard_map/ppermute | solution.py:252
  87.5 2.0 collective-permute-start.2
  89.5 0.0 collective-permute-done.gate2_ref
  89.5 1.2 collective-permute-done.1.up2_ref
  90.7 1.2 copy-done.3
  91.9 1.3 collective-permute-done.2.down2_ref
  93.2 31.6 %all-to-all-done.slots_ref = bf16[8,80,1536]{2,1,0:T(8,128)(2,1)S(1)} async-done(((bf16[8,80,1536]{2,1,0:T(8,128)(2,1)}), bf16[8,80,1536]{2,1,0:T(8,128)(2,1)S(1)}, u32[]{:S(2)}, u32[]{:S(2)}) %all-to-all-start) | async-done | bytes 1966112 | tf_op jit(solution)/shard_map/all_to_all | solution.py:250
  124.8 1.3 copy-done
  126.1 8.6 %ffn.1 = bf16[8,80,1536]{2,1,0:T(8,128)(2,1)} custom-call(bf16[8,80,1536]{2,1,0:T(8,128)(2,1)} %copy-done, bf16[6144,128]{1,0:T(8,128)(2,1)} %gate_ref, bf16[6144,128]{1,0:T(8,128)(2,1)} %copy-done.2, bf16[6144,128]{1,0:T(8,128)(2,1)} %up_ref, bf16[6144,128]{1,0:T(8,128)(2,1)} %copy-done.3, bf16[128,6144]{1,0:T(8,128)(2,1)} %down_ref, ...), custom_call_target="tpu_custom_call" | custom-call | flops 1509949440 | bytes 14000000 | tf_op jit(solution)/shard_map/ffn/pallas_call | solution.py:194
  134.8 0.0 copy-start.4
  134.8 0.0 copy-start.5
  134.8 3.8 %all-to-all-start.1 = ((bf16[8,80,1536]{2,1,0:T(8,128)(2,1)}), bf16[8,80,1536]{2,1,0:T(8,128)(2,1)S(1)}, u32[]{:S(2)}, u32[]{:S(2)}) async-start(bf16[8,80,1536]{2,1,0:T(8,128)(2,1)} %ffn.1), calls=%async_computation.1 | async-start | bytes 3932160 | tf_op jit(solution)/shard_map/all_to_all | solution.py:255
  138.6 0.1 tile.9.ids_ref
  138.7 0.1 tile.21.logits_ref
  138.8 0.2 mixing.1.mix_ref
  139.0 42.5 %all-to-all-done.1 = bf16[8,80,1536]{2,1,0:T(8,128)(2,1)S(1)} async-done(((bf16[8,80,1536]{2,1,0:T(8,128)(2,1)}), bf16[8,80,1536]{2,1,0:T(8,128)(2,1)S(1)}, u32[]{:S(2)}, u32[]{:S(2)}) %all-to-all-start.1) | async-done | bytes 1966112 | tf_op jit(solution)/shard_map/all_to_all | solution.py:255
  181.5 0.5 combine.1
  182.0 22.9 %all_to_all.15 = bf16[16,32,384]{2,1,0:T(8,128)(2,1)S(1)} all-to-all(bf16[16,32,384]{2,1,0:T(8,128)(2,1)S(1)} %combine.1), channel_id=1, replica_groups=mesh['rep'=2,'x'=8,'core'=2,'tp'=16] {'tp'}, dimensions={0} | all-to-all | bytes 786432 | tf_op jit(solution)/shard_map/all_to_all | solution.py:259
  205.0 0.7 reduce_sum.12
  (9 shorter events, 0.0 us)
Async XLA Ops:
  75.6 7.5 %copy-start.1 = (bf16[6144,128]{1,0:T(8,128)(2,1)S(1)}, bf16[6144,128]{1,0:T(8,128)(2,1)}, u32[]{:S(2)}) copy-start(bf16[6144,128]{1,0:T(8,128)(2,1)} %gate_ref) | copy-start | bytes 4718596
  75.6 49.2 %all-to-all-start = ((bf16[8,80,1536]{2,1,0:T(8,128)(2,1)}), bf16[8,80,1536]{2,1,0:T(8,128)(2,1)S(1)}, u32[]{:S(2)}, u32[]{:S(2)}) async-start(bf16[8,80,1536]{2,1,0:T(8,128)(2,1)} %dispatch.1), calls=%async_computation | async-start | bytes 3932160 | tf_op jit(solution)/shard_map/all_to_all | solution.py:250
  83.1 6.4 %collective-permute-start = (bf16[6144,128]{1,0:T(8,128)(2,1)S(1)}, bf16[6144,128]{1,0:T(8,128)(2,1)S(1)}, u32[]{:S(2)}, u32[]{:S(2)}) collective-permute-start(bf16[6144,128]{1,0:T(8,128)(2,1)S(1)} %copy-done.1), channel_id=1, source_target_pairs={{0,16},{16,0},{1,17},{17,1},{2,18},{18,2},{3,19},{19,3},{4,20},{20... | collective-permute-start | bytes 4718600 | tf_op jit(solution)/shard_map/ppermute | solution.py:251
  85.1 5.7 %collective-permute-start.1 = (bf16[6144,128]{1,0:T(8,128)(2,1)}, bf16[6144,128]{1,0:T(8,128)(2,1)S(1)}, u32[]{:S(2)}, u32[]{:S(2)}) collective-permute-start(bf16[6144,128]{1,0:T(8,128)(2,1)} %up_ref), channel_id=1, source_target_pairs={{0,16},{16,0},{1,17},{17,1},{2,18},{18,2},{3,19},{19,3},{4,20},{20... | collective-permute-start | bytes 4718600 | tf_op jit(solution)/shard_map/ppermute | solution.py:252
  87.5 5.7 %collective-permute-start.2 = (bf16[128,6144]{1,0:T(8,128)(2,1)}, bf16[128,6144]{1,0:T(8,128)(2,1)}, u32[]{:S(2)}, u32[]{:S(2)}) collective-permute-start(bf16[128,6144]{1,0:T(8,128)(2,1)} %down_ref), channel_id=1, source_target_pairs={{0,16},{16,0},{1,17},{17,1},{2,18},{18,2},{3,19},{19,3},{4,20},{20... | collective-permute-start | bytes 4718600 | tf_op jit(solution)/shard_map/ppermute | solution.py:253
  89.5 1.3 copy-start.2
  90.7 1.2 copy-start.3
  124.8 1.3 copy-start
  134.8 3.8 %copy-start.4 = (s32[32,2]{0,1:T(2,128)S(1)}, s32[32,2]{0,1:T(2,128)}, u32[]{:S(2)}) copy-start(s32[32,2]{0,1:T(2,128)} %param.7) | copy-start | bytes 772
  134.8 3.9 %copy-start.5 = (f32[32,2]{0,1:T(2,128)S(1)}, f32[32,2]{0,1:T(2,128)}, u32[]{:S(2)}) copy-start(f32[32,2]{0,1:T(2,128)} %param.8) | copy-start | bytes 772
  134.8 46.7 %all-to-all-start.1 = ((bf16[8,80,1536]{2,1,0:T(8,128)(2,1)}), bf16[8,80,1536]{2,1,0:T(8,128)(2,1)S(1)}, u32[]{:S(2)}, u32[]{:S(2)}) async-start(bf16[8,80,1536]{2,1,0:T(8,128)(2,1)} %ffn.1), calls=%async_computation.1 | async-start | bytes 3932160 | tf_op jit(solution)/shard_map/all_to_all | solution.py:255

commit v3 on v2

v3 whole, which is shorter than its diff:
```python
import functools

import jax
import jax.numpy as jnp
from jax import lax
from jax.experimental import pallas as pl
from jax.experimental.pallas import tpu as pltpu
from jax.sharding import Mesh, PartitionSpec as P


EXPERTS = 4
CAP = 20
MAIN = 16
TAIL = CAP - MAIN
QUARTERS = 4
CORES = 2


def cost(flops, nbytes):
    return pl.CostEstimate(flops=flops, bytes_accessed=nbytes, transcendentals=0)


def count_at_least(index, width, parts):
    total = jnp.zeros_like(index)
    for k in range(1, parts):
        total = total + (index >= k * width).astype(jnp.int32)
    return total


def placed(ids, expert, slot, before):
    chosen = ((ids[0:1, :] == expert) | (ids[1:2, :] == expert)).astype(jnp.float32)
    position = jnp.dot(chosen, before, preferred_element_type=jnp.float32)
    return chosen * (position == slot.astype(jnp.float32)).astype(jnp.float32)


def grouped(row, groups):
    later = row >= groups * MAIN
    rest = row - groups * MAIN
    main = count_at_least(row, MAIN, groups)
    tail = count_at_least(rest, TAIL, groups)
    group = jnp.where(later, tail, main)
    slot = jnp.where(later, MAIN + rest - TAIL * tail, row - MAIN * main)
    return group, slot


def dispatch_kernel(chips, ids_ref, tokens_ref, out_ref):
    count = tokens_ref.shape[0]
    row = lax.broadcasted_iota(jnp.int32, (EXPERTS * CAP, count), 0)
    expert = count_at_least(row, CAP, EXPERTS)
    slot = row - CAP * expert
    first = lax.broadcasted_iota(jnp.int32, (count, count), 0)
    second = lax.broadcasted_iota(jnp.int32, (count, count), 1)
    before = (first < second).astype(jnp.float32)
    placement = placed(ids_ref[...], expert, slot, before).astype(jnp.bfloat16)
    slots = jnp.dot(placement, tokens_ref[...], preferred_element_type=jnp.float32).astype(
        jnp.bfloat16
    )
    per_expert = chips // EXPERTS
    for chip in range(chips):
        e = chip // per_expert
        out_ref[chip] = slots[e * CAP : (e + 1) * CAP]


def dispatch(ids, tokens, chips):
    count, features = tokens.shape
    return pl.pallas_call(
        functools.partial(dispatch_kernel, chips),
        out_shape=jax.ShapeDtypeStruct((chips, CAP, features), jnp.bfloat16),
        cost_estimate=cost(2 * EXPERTS * CAP * count * features, 200000),
        compiler_params=pltpu.CompilerParams(vmem_limit_bytes=4 << 20),
        name="dispatch",
    )(ids, tokens)


def gather_rows_kernel(in_ref, out_ref):
    chips = in_ref.shape[0]
    for chip in range(chips):
        out_ref[chip * MAIN : (chip + 1) * MAIN] = in_ref[chip, :MAIN]
        at = chips * MAIN + chip * TAIL
        out_ref[at : at + TAIL] = in_ref[chip, MAIN:]


def gather_rows(slots):
    chips, _, depth = slots.shape
    return pl.pallas_call(
        gather_rows_kernel,
        out_shape=jax.ShapeDtypeStruct((chips * CAP, depth), jnp.bfloat16),
        cost_estimate=cost(1000, 250000),
        compiler_params=pltpu.CompilerParams(vmem_limit_bytes=4 << 20),
        name="gather_rows",
    )(slots)


def mixing_kernel(chips, count, ids_ref, logits_ref, out_ref):
    lanes = ids_ref.shape[1]
    rows = chips * QUARTERS * CAP
    row = lax.broadcasted_iota(jnp.int32, (rows, lanes), 0)
    chip = count_at_least(row, QUARTERS * CAP, chips)
    quarter, slot = grouped(row - QUARTERS * CAP * chip, QUARTERS)
    expert = count_at_least(chip, chips // EXPERTS, EXPERTS)
    lane = lax.broadcasted_iota(jnp.int32, (rows, lanes), 1)
    own = (count_at_least(lane, count, QUARTERS) == quarter).astype(jnp.float32)
    first = lax.broadcasted_iota(jnp.int32, (lanes, lanes), 0)
    second = lax.broadcasted_iota(jnp.int32, (lanes, lanes), 1)
    same = count_at_least(first, count, QUARTERS) == count_at_least(second, count, QUARTERS)
    before = ((first < second) & same).astype(jnp.float32)
    ids = ids_ref[...]
    diff = logits_ref[0:1, :] - logits_ref[1:2, :]
    share = jnp.where(ids[0:1, :] == expert, jax.nn.sigmoid(diff), jax.nn.sigmoid(-diff))
    out_ref[...] = (placed(ids, expert, slot, before) * share * own).astype(jnp.bfloat16)


def mixing(ids, logits, chips):
    count = ids.shape[1]
    rows = chips * QUARTERS * CAP
    return pl.pallas_call(
        functools.partial(mixing_kernel, chips, count),
        out_shape=jax.ShapeDtypeStruct((rows, QUARTERS * count), jnp.bfloat16),
        cost_estimate=cost(2 * rows * 128 * 128, 200000),
        compiler_params=pltpu.CompilerParams(vmem_limit_bytes=8 << 20),
        name="mixing",
    )(jnp.tile(ids, (1, QUARTERS)), jnp.tile(logits, (1, QUARTERS)))


def multiply(total, tokens, first, weights, start, number):
    for b in range(0, number, 2):
        rows = jnp.concatenate([tokens[first + b], tokens[first + b + 1]], axis=1)
        weight = jnp.concatenate([weights[start + b], weights[start + b + 1]], axis=0)
        added = jnp.dot(rows, weight, preferred_element_type=jnp.float32)
        total = added if total is None else total + added
    return total


def own_kernel(slots_ref, gate_ref, gate2_ref, up_ref, up2_ref, out_ref, ins, sems):
    pairs = slots_ref.shape[0]
    parity = lax.axis_index("odd")
    width = gate_ref.shape[-1]
    half = pairs // 2
    refs = (gate_ref, gate2_ref, up_ref, up2_ref)
    groups = [
        [
            pltpu.make_async_copy(
                ref.at[pl.ds(g * half, half), parity],
                ins.at[pl.ds(g * half, half), :, pl.ds(i * width, width)],
                sems.at[g, i],
            )
            for i, ref in enumerate(refs)
        ]
        for g in range(2)
    ]
    for group in groups:
        for copy in group:
            copy.start()
    total = None
    for g, group in enumerate(groups):
        for copy in group:
            copy.wait()
        total = multiply(total, slots_ref, g * half, ins, g * half, half)
    out_ref[...] = total


def own_part(slots, *weights):
    pairs, rows, depth = slots.shape
    width = weights[0].shape[-1]
    hbm = pl.BlockSpec(memory_space=pltpu.HBM)
    return pl.pallas_call(
        own_kernel,
        in_specs=[pl.BlockSpec(memory_space=pltpu.VMEM)] + [hbm] * 4,
        out_specs=pl.BlockSpec(memory_space=pltpu.VMEM),
        out_shape=jax.ShapeDtypeStruct((rows, 4 * width), jnp.float32),
        scratch_shapes=[
            pltpu.VMEM((pairs, depth, 4 * width), jnp.bfloat16),
            pltpu.SemaphoreType.DMA((2, 4)),
        ],
        cost_estimate=cost(2 * pairs * rows * depth * 4 * width, 4200000),
        compiler_params=pltpu.CompilerParams(vmem_limit_bytes=60 << 20),
        name="own_part",
    )(slots, *weights)


def ffn_kernel(
    total_ref, left_ref, right_ref, gate_ref, gate2_ref, up_ref, up2_ref, down_ref, down2_ref, out_ref, ins, downs, outs, in_sems, down_sems, out_sems
):
    half = left_ref.shape[0]
    chips, _, quarter = out_ref.shape
    parity = 1 - lax.axis_index("odd")
    width = gate_ref.shape[-1]
    refs = (gate_ref, gate2_ref, up_ref, up2_ref)
    groups = [
        [
            pltpu.make_async_copy(
                ref.at[pl.ds(g * half, half), parity],
                ins.at[pl.ds(g * half, half), :, pl.ds(i * width, width)],
                in_sems.at[g, i],
            )
            for i, ref in enumerate(refs)
        ]
        for g in range(2)
    ]
    second = [
        [
            pltpu.make_async_copy(
                ref.at[:, pl.ds(q * quarter, quarter)],
                downs.at[q, pl.ds(i * width, width)],
                down_sems.at[q, i],
            )
            for i, ref in enumerate((down_ref, down2_ref))
        ]
        for q in range(QUARTERS)
    ]
    for group in groups + second:
        for copy in group:
            copy.start()
    total = total_ref[...]
    for g, group in enumerate(groups):
        for copy in group:
            copy.wait()
        total = multiply(total, (left_ref, right_ref)[g], 0, ins, g * half, half)
    gate = total[:, : 2 * width]
    hidden = (gate * jax.nn.sigmoid(gate) * total[:, 2 * width :]).astype(jnp.bfloat16)
    for q in range(QUARTERS):
        at = QUARTERS * MAIN + q * TAIL
        for copy in second[q]:
            copy.wait()
        partial = jnp.dot(hidden, downs[q], preferred_element_type=jnp.float32).astype(
            jnp.bfloat16
        )
        for chip in range(chips):
            outs[chip, q * MAIN : (q + 1) * MAIN] = partial[chip * MAIN : (chip + 1) * MAIN]
            tail = chips * MAIN + chip * TAIL
            outs[chip, at : at + TAIL] = partial[tail : tail + TAIL]
    copies = [
        pltpu.make_async_copy(outs.at[chip], out_ref.at[chip], out_sems.at[chip])
        for chip in range(chips)
    ]
    for copy in copies:
        copy.start()
    for copy in copies:
        copy.wait()


def ffn(total, left, right, chips, *weights):
    half, rows, depth = left.shape
    width, model = weights[-1].shape
    quarter = model // QUARTERS
    hbm = pl.BlockSpec(memory_space=pltpu.HBM)
    vmem = pl.BlockSpec(memory_space=pltpu.VMEM)
    out = (chips, QUARTERS * CAP, quarter)
    return pl.pallas_call(
        ffn_kernel,
        in_specs=[vmem] * 3 + [hbm] * 6,
        out_specs=hbm,
        out_shape=jax.ShapeDtypeStruct(out, jnp.bfloat16),
        scratch_shapes=[
            pltpu.VMEM((2 * half, depth, 4 * width), jnp.bfloat16),
            pltpu.VMEM((QUARTERS, 2 * width, quarter), jnp.bfloat16),
            pltpu.VMEM(out, jnp.bfloat16),
            pltpu.SemaphoreType.DMA((2, 4)),
            pltpu.SemaphoreType.DMA((QUARTERS, 2)),
            pltpu.SemaphoreType.DMA((chips,)),
        ],
        cost_estimate=cost(2 * rows * model * width * 4, 9000000),
        compiler_params=pltpu.CompilerParams(vmem_limit_bytes=60 << 20),
        name="ffn",
    )(total, left, right, *weights)


def combine_kernel(mix_ref, back_ref, out_ref):
    blocks, count, depth = out_ref.shape
    per_quarter = blocks // QUARTERS
    summed = lax.dot_general(
        mix_ref[...], back_ref[...], (((0,), (0,)), ((), ())), preferred_element_type=jnp.float32
    ).astype(jnp.bfloat16)
    for q in range(QUARTERS):
        for s in range(per_quarter):
            out_ref[q * per_quarter + s] = summed[
                q * count : (q + 1) * count, s * depth : (s + 1) * depth
            ]


def combine(mix, back, count, blocks):
    rows, quarter = back.shape
    depth = QUARTERS * quarter // blocks
    return pl.pallas_call(
        combine_kernel,
        out_shape=jax.ShapeDtypeStruct((blocks, count, depth), jnp.bfloat16),
        cost_estimate=cost(2 * rows * quarter * 128, 2400000),
        compiler_params=pltpu.CompilerParams(vmem_limit_bytes=12 << 20),
        name="combine",
    )(mix, back)


def on_device(tokens, expert_ids, route_logits, gate_weight, up_weight, down_weight):
    chips = lax.axis_size("x")
    pairs = lax.axis_size("pair")
    parts = 2 * pairs
    count, depth = tokens.shape
    swap = [(0, 1), (1, 0)]
    along = ("pair", "odd")
    ids = expert_ids.T
    outgoing = dispatch(ids, tokens, chips)
    incoming = lax.all_to_all(outgoing, "x", 0, 0, tiled=True)
    own = lax.all_gather(gather_rows(incoming), "pair")
    gate, up, down, own = lax.optimization_barrier((gate_weight, up_weight, down_weight, own))
    up_z = [(i, (i + 1) % parts) for i in range(parts)]
    down_z = [((i + 1) % parts, i) for i in range(parts)]
    left = lax.ppermute(own[: pairs // 2], along, up_z)
    right = lax.ppermute(own[pairs // 2 :], along, down_z)
    gate2 = lax.ppermute(gate, "core", swap)
    up2 = lax.ppermute(up, "core", swap)
    down2 = lax.ppermute(down, "core", swap)
    blocks = [w.reshape(pairs, 2, depth, w.shape[1]) for w in (gate, gate2, up, up2)]
    total = own_part(own, *blocks)
    partial_value = ffn(total, left, right, chips, *blocks, down, down2)
    returned = lax.all_to_all(partial_value, "x", 0, 0, tiled=True)
    mix = mixing(ids, route_logits.T, chips)
    back = returned.reshape(chips * QUARTERS * CAP, parts * depth // QUARTERS)
    combined = combine(mix, back, count, parts)
    blocks = lax.all_to_all(combined, along, 0, 0, tiled=True)
    return jnp.sum(blocks.astype(jnp.float32), axis=0).astype(jnp.bfloat16)


def solution(mesh):
    sizes = [mesh.shape[axis] for axis in ("rep", "exp", "tp")]
    devices = mesh.devices.reshape(sizes[0], sizes[1] // CORES, CORES, sizes[2] // 2, 2)
    split = Mesh(devices, ("rep", "x", "core", "pair", "odd"))
    tokens = ("rep", "x", "core")
    features = ("pair", "odd")
    hidden = ("x", "core", "pair", "odd")
    return jax.shard_map(
        on_device,
        mesh=split,
        in_specs=(
            P(tokens, features),
            P(tokens, None),
            P(tokens, None),
            P(None, hidden),
            P(None, hidden),
            P(hidden, None),
        ),
        out_specs=P(tokens, features),
        check_vma=False,
    )
```

time: 206 us -> 208 us (level)
  waiting for transfers between devices: 76.7 us -> 53.8 us
  blocking collectives: 95.6 us -> 118 us
    all_to_all x1 -> x0, waiting for transfers between devices: 31.6 us -> none  [on_device(): incoming = lax.all_to_all(outgoing, 'x', 0, 0, tiled=True)]
    all_to_all x1 -> x2, blocking collectives: 22.9 us -> 48.3 us  [the longest x1 31.6 us: on_device(): blocks = lax.all_to_all(combined, along, 0, 0, tiled=True)]
    ppermute x0 -> x2, starting transfers between devices: none -> 9.44 us  [the longest x1 5.09 us: on_device(): left = lax.ppermute(own[:pairs // 2], along, up_z)]
    all_to_all x1 -> x0, starting transfers between devices: 7.47 us -> none  [on_device(): incoming = lax.all_to_all(outgoing, 'x', 0, 0, tiled=True)]
    ppermute x0 -> x2, waiting for transfers between devices: none -> 5.94 us  [the longest x1 4.73 us: on_device(): left = lax.ppermute(own[:pairs // 2], along, up_z)]
    all_to_all x1, waiting for transfers between devices: 42.5 us -> 47.9 us  [on_device(): returned = lax.all_to_all(partial_value, 'x', 0, 0, tiled=True)]
    all_gather x1, blocking collectives: 72.6 us -> 69.3 us  [on_device(): own = lax.all_gather(gather_rows(incoming), 'pair')]
    pallas_call x1, Pallas kernels: 2.97 us -> 0.26 us  [dispatch(): pl.pallas_call(functools.partial(dispatch_kernel, chips), out_shape=jax.S...]
  transfers between devices with their start and end apart: 5 -> 6, of which waited for: 4 -> 3; matrix products, arithmetic and copies ran while one was open for 0% -> 1% of each run, Pallas kernels for 0% -> 2%
where the time goes in v3:
time: 208 us; the launch traced here: 207 us
  blocking collectives  118 us (57%)
  waiting for transfers between devices  53.8 us (26%)
  starting transfers between devices  19.6 us (9%)
  Pallas kernels  11.5 us (6%)
  local copies, waits for them, and re-layouts  3.88 us (2%)
    all_gather x1, blocking collectives, on_device(): own = lax.all_gather(gather_rows(incoming), 'pair')  69.3 us
    all_to_all x1, waiting for transfers between devices, on_device(): returned = lax.all_to_all(partial_value, 'x', 0, 0, tiled=True)  47.9 us
    all_to_all x1, blocking collectives, on_device(): blocks = lax.all_to_all(combined, along, 0, 0, tiled=True)  31.6 us
    all_to_all x1, blocking collectives, on_device(): incoming = lax.all_to_all(outgoing, 'x', 0, 0, tiled=True)  16.7 us
    pallas_call x1, Pallas kernels, ffn(): pl.pallas_call(ffn_kernel, in_specs=[vmem] * 3 + [hbm] * 6, out_specs=hbm...  6.25 us
    ppermute x1, starting transfers between devices, on_device(): left = lax.ppermute(own[:pairs // 2], along, up_z)  5.09 us
    ppermute x1, waiting for transfers between devices, on_device(): left = lax.ppermute(own[:pairs // 2], along, up_z)  4.73 us
    ppermute x1, starting transfers between devices, on_device(): right = lax.ppermute(own[pairs // 2:], along, down_z)  4.34 us
  transfers between devices with their start and end apart: 6, of which 3 were waited for; matrix products, arithmetic and copies ran while one was open for 1% of the time, Pallas kernels for 2%

profile of v3, /device:TPU:80, one launch (start us, length us, event | category | flops | bytes accessed | tf_op | source)
XLA Modules:
  0.0 207.3 jit_solution(18164812113406630667)
XLA Ops:
  0.0 0.7 copy-done
  0.7 0.7 copy-done.1
  1.4 0.3 dispatch.1
  1.7 16.7 %all_to_all.15.in_ref = bf16[8,20,384]{2,1,0:T(8,128)(2,1)S(1)} all-to-all(bf16[8,20,384]{2,1,0:T(8,128)(2,1)S(1)} %dispatch.1), channel_id=1, replica_groups=mesh['rep'=2,'x'=8,'core'=2,'pair'=8,'odd'=2] {'x'}, dimensions={0} | all-to-all | bytes 245760 | tf_op jit(solution)/shard_map/all_to_all | solution.py:302
  18.4 69.3 %all-gather = bf16[1280,384]{1,0:T(8,128)(2,1)S(1)} all-gather(bf16[160,384]{1,0:T(8,128)(2,1)S(1)} %gather_rows.1), channel_id=2, replica_groups=mesh['rep'=2,'x'=8,'core'=2,'pair'=8,'odd'=2] {'pair'}, dimensions={0}, use_global_device_ids=true | all-gather | bytes 1105920 | tf_op jit(solution)/shard_map/all_gather | solution.py:303
  87.8 1.9 collective-permute-start
  89.7 2.4 %collective-permute-start.1 = (bf16[6144,128]{1,0:T(8,128)(2,1)}, bf16[6144,128]{1,0:T(8,128)(2,1)}, u32[]{:S(2)}, u32[]{:S(2)}) collective-permute-start(bf16[6144,128]{1,0:T(8,128)(2,1)} %param.10), channel_id=1, source_target_pairs={{0,16},{16,0},{1,17},{17,1},{2,18},{18,2},{3,19},{19,3},{4,20},{20... | collective-permute-start | bytes 4718600 | tf_op jit(solution)/shard_map/ppermute | solution.py:310
  92.2 2.0 collective-permute-start.4
  94.1 1.1 fusion
  95.2 5.1 %collective-permute-start.2 = (bf16[4,160,384]{2,1,0:T(8,128)(2,1)}, bf16[4,160,384]{2,1,0:T(8,128)(2,1)}, u32[]{:S(2)}, u32[]{:S(2)}) collective-permute-start(bf16[4,160,384]{2,1,0:T(8,128)(2,1)} %get-tuple-element.14), channel_id=1, source_target_pairs={{0,1},{1,2},{2,3},{3,4},{4,5},{5,6},{6,7},{7,8},{8,9},{9,10},{10,1... | collective-permute-start | bytes 1474568 | tf_op jit(solution)/shard_map/ppermute | solution.py:307
  100.3 4.3 %collective-permute-start.3 = (bf16[4,160,384]{2,1,0:T(8,128)(2,1)}, bf16[4,160,384]{2,1,0:T(8,128)(2,1)}, u32[]{:S(2)}, u32[]{:S(2)}) collective-permute-start(bf16[4,160,384]{2,1,0:T(8,128)(2,1)} %get-tuple-element.13), channel_id=1, source_target_pairs={{1,0},{2,1},{3,2},{4,3},{5,4},{6,5},{7,6},{8,7},{9,8},{10,9},{11,1... | collective-permute-start | bytes 1474568 | tf_op jit(solution)/shard_map/ppermute | solution.py:308
  104.7 1.2 copy-done.5
  105.9 4.3 %own_part.1.total_ref = f32[160,512]{1,0:T(8,128)} custom-call(bf16[8,160,384]{2,1,0:T(8,128)(2,1)} %bitcast.12, bf16[8,2,384,128]{3,2,1,0:T(8,128)(2,1)} %bitcast.13, bf16[8,2,384,128]{3,2,1,0:T(8,128)(2,1)} %bitcast.17, bf16[8,2,384,128]{3,2,1,0:T(8,128)(2,1)} %bitcast.15, bf16[8,2,384,128]{3,2,1,0:T(8,128)(2,1)} %bitcast.6.up2_ref), custom_call_target="tpu_custom_call" | custom-call | flops 503316480 | bytes 4200000 | tf_op jit(solution)/shard_map/own_part/pallas_call | solution.py:166
  110.2 4.7 %collective-permute-done.2.left_ref = bf16[4,160,384]{2,1,0:T(8,128)(2,1)} collective-permute-done((bf16[4,160,384]{2,1,0:T(8,128)(2,1)}, bf16[4,160,384]{2,1,0:T(8,128)(2,1)}, u32[]{:S(2)}, u32[]{:S(2)}) %collective-permute-start.2) | collective-permute-done | bytes 491552 | tf_op jit(solution)/shard_map/ppermute | solution.py:307
  114.9 1.2 collective-permute-done.3.right_ref
  116.1 6.3 %ffn.1 = bf16[8,80,1536]{2,1,0:T(8,128)(2,1)} custom-call(f32[160,512]{1,0:T(8,128)} %own_part.1.total_ref, bf16[4,160,384]{2,1,0:T(8,128)(2,1)} %collective-permute-done.2.left_ref, bf16[4,160,384]{2,1,0:T(8,128)(2,1)} %collective-permute-done.3.right_ref, bf16[8,2,384,128]{3,2,1,0:T(8,128)(2,1)} %bitcast.14, bf16[8,2,384,128]{3,2,1,0:T(8,128)(2,1)} %bitcast.18, ...), custom_call_target="tpu_custom_call" | custom-call | flops 1006632960 | bytes 9000000 | tf_op jit(solution)/shard_map/ffn/pallas_call | solution.py:249
  122.4 3.8 %all-to-all-start.1 = ((bf16[8,80,1536]{2,1,0:T(8,128)(2,1)}), bf16[8,80,1536]{2,1,0:T(8,128)(2,1)S(1)}, u32[]{:S(2)}, u32[]{:S(2)}) async-start(bf16[8,80,1536]{2,1,0:T(8,128)(2,1)} %ffn.1), calls=%async_computation.1 | async-start | bytes 3932160 | tf_op jit(solution)/shard_map/all_to_all | solution.py:315
  126.3 0.1 tile.9.ids_ref
  126.3 0.1 tile.21.logits_ref
  126.4 0.2 mixing.1.mix_ref
  126.7 47.9 %all-to-all-done.1 = bf16[8,80,1536]{2,1,0:T(8,128)(2,1)S(1)} async-done(((bf16[8,80,1536]{2,1,0:T(8,128)(2,1)}), bf16[8,80,1536]{2,1,0:T(8,128)(2,1)S(1)}, u32[]{:S(2)}, u32[]{:S(2)}) %all-to-all-start.1) | async-done | bytes 1966112 | tf_op jit(solution)/shard_map/all_to_all | solution.py:315
  174.5 0.5 combine.1
  175.0 31.6 %all_to_all.16 = bf16[16,32,384]{2,1,0:T(8,128)(2,1)S(1)} all-to-all(bf16[16,32,384]{2,1,0:T(8,128)(2,1)S(1)} %combine.1), channel_id=1, replica_groups=mesh['rep'=2,'x'=8,'core'=2,'pair'=8,'odd'=2] {'pair','odd'}, dimensions={0} | all-to-all | bytes 786432 | tf_op jit(solution)/shard_map/all_to_all | solution.py:319
  206.6 0.7 reduce_sum.12
  (17 shorter events, 0.1 us)
Async XLA Ops:
  0.0 0.7 copy-start
  0.7 0.7 copy-start.1
  1.4 86.4 %copy-start.4 = (bf16[6144,128]{1,0:T(8,128)(2,1)S(1)}, bf16[6144,128]{1,0:T(8,128)(2,1)}, u32[]{:S(2)}) copy-start(bf16[6144,128]{1,0:T(8,128)(2,1)} %param.9) | copy-start | bytes 4718596
  87.8 16.9 %copy-start.3 = (bf16[1280,384]{1,0:T(8,128)(2,1)}, bf16[1280,384]{1,0:T(8,128)(2,1)S(1)}, u32[]{:S(2)}) copy-start(bf16[1280,384]{1,0:T(8,128)(2,1)S(1)} %all-gather) | copy-start | bytes 2949124
  87.8 16.9 %collective-permute-start = (bf16[6144,128]{1,0:T(8,128)(2,1)S(1)}, bf16[6144,128]{1,0:T(8,128)(2,1)S(1)}, u32[]{:S(2)}, u32[]{:S(2)}) collective-permute-start(bf16[6144,128]{1,0:T(8,128)(2,1)S(1)} %copy-done.4), channel_id=1, source_target_pairs={{0,16},{16,0},{1,17},{17,1},{2,18},{18,2},{3,19},{19,3},{4,20},{20... | collective-permute-start | bytes 4718600 | tf_op jit(solution)/shard_map/ppermute | solution.py:309
  89.7 15.0 %collective-permute-start.1 = (bf16[6144,128]{1,0:T(8,128)(2,1)}, bf16[6144,128]{1,0:T(8,128)(2,1)}, u32[]{:S(2)}, u32[]{:S(2)}) collective-permute-start(bf16[6144,128]{1,0:T(8,128)(2,1)} %param.10), channel_id=1, source_target_pairs={{0,16},{16,0},{1,17},{17,1},{2,18},{18,2},{3,19},{19,3},{4,20},{20... | collective-permute-start | bytes 4718600 | tf_op jit(solution)/shard_map/ppermute | solution.py:310
  92.2 23.9 %collective-permute-start.4 = (bf16[128,6144]{1,0:T(8,128)(2,1)}, bf16[128,6144]{1,0:T(8,128)(2,1)}, u32[]{:S(2)}, u32[]{:S(2)}) collective-permute-start(bf16[128,6144]{1,0:T(8,128)(2,1)} %down_ref), channel_id=1, source_target_pairs={{0,16},{16,0},{1,17},{17,1},{2,18},{18,2},{3,19},{19,3},{4,20},{20... | collective-permute-start | bytes 4718600 | tf_op jit(solution)/shard_map/ppermute | solution.py:311
  95.2 19.7 %collective-permute-start.2 = (bf16[4,160,384]{2,1,0:T(8,128)(2,1)}, bf16[4,160,384]{2,1,0:T(8,128)(2,1)}, u32[]{:S(2)}, u32[]{:S(2)}) collective-permute-start(bf16[4,160,384]{2,1,0:T(8,128)(2,1)} %get-tuple-element.14), channel_id=1, source_target_pairs={{0,1},{1,2},{2,3},{3,4},{4,5},{5,6},{6,7},{7,8},{8,9},{9,10},{10,1... | collective-permute-start | bytes 1474568 | tf_op jit(solution)/shard_map/ppermute | solution.py:307
  100.3 15.8 %collective-permute-start.3 = (bf16[4,160,384]{2,1,0:T(8,128)(2,1)}, bf16[4,160,384]{2,1,0:T(8,128)(2,1)}, u32[]{:S(2)}, u32[]{:S(2)}) collective-permute-start(bf16[4,160,384]{2,1,0:T(8,128)(2,1)} %get-tuple-element.13), channel_id=1, source_target_pairs={{1,0},{2,1},{3,2},{4,3},{5,4},{6,5},{7,6},{8,7},{9,8},{10,9},{11,1... | collective-permute-start | bytes 1474568 | tf_op jit(solution)/shard_map/ppermute | solution.py:308
  104.7 1.2 copy-start.5
  122.4 3.8 %copy-start.2 = (s32[32,2]{0,1:T(2,128)S(1)}, s32[32,2]{0,1:T(2,128)}, u32[]{:S(2)}) copy-start(s32[32,2]{0,1:T(2,128)} %param.7) | copy-start | bytes 772
  122.4 3.9 %copy-start.6 = (f32[32,2]{0,1:T(2,128)S(1)}, f32[32,2]{0,1:T(2,128)}, u32[]{:S(2)}) copy-start(f32[32,2]{0,1:T(2,128)} %param.8) | copy-start | bytes 772
  122.4 52.1 %all-to-all-start.1 = ((bf16[8,80,1536]{2,1,0:T(8,128)(2,1)}), bf16[8,80,1536]{2,1,0:T(8,128)(2,1)S(1)}, u32[]{:S(2)}, u32[]{:S(2)}) async-start(bf16[8,80,1536]{2,1,0:T(8,128)(2,1)} %ffn.1), calls=%async_computation.1 | async-start | bytes 3932160 | tf_op jit(solution)/shard_map/all_to_all | solution.py:315

commit v4 on v3

--- a/solution.py
+++ b/solution.py
@@ -178,11 +178,33 @@
     )(slots, *weights)
 
 
+def down_copies(refs, scratch, sems, parity):
+    pairs, _, depth = scratch.shape
+    width = refs[0].shape[0]
+    return [
+        [
+            pltpu.make_async_copy(
+                ref.at[:, pl.ds(pl.multiple_of((2 * b + parity) * depth, 128), depth)],
+                scratch.at[b, pl.ds(i * width, width)],
+                sems.at[b, i],
+            )
+            for i, ref in enumerate(refs)
+        ]
+        for b in range(pairs)
+    ]
+
+
+def down_pair(hidden, scratch, copies, b):
+    for copy in copies[b] + copies[b + 1]:
+        copy.wait()
+    weight = jnp.concatenate([scratch[b], scratch[b + 1]], axis=1)
+    return jnp.dot(hidden, weight, preferred_element_type=jnp.float32)
+
+
 def ffn_kernel(
-    total_ref, left_ref, right_ref, gate_ref, gate2_ref, up_ref, up2_ref, down_ref, down2_ref, out_ref, ins, downs, outs, in_sems, down_sems, out_sems
+    total_ref, left_ref, right_ref, gate_ref, gate2_ref, up_ref, up2_ref, down_ref, down2_ref, hidden_ref, to_right_ref, to_left_ref, ins, downs, in_sems, down_sems
 ):
-    half = left_ref.shape[0]
-    chips, _, quarter = out_ref.shape
+    half, _, depth = left_ref.shape
     parity = 1 - lax.axis_index("odd")
     width = gate_ref.shape[-1]
     refs = (gate_ref, gate2_ref, up_ref, up2_ref)
@@ -197,17 +219,7 @@
         ]
         for g in range(2)
     ]
-    second = [
-        [
-            pltpu.make_async_copy(
-                ref.at[:, pl.ds(q * quarter, quarter)],
-                downs.at[q, pl.ds(i * width, width)],
-                down_sems.at[q, i],
-            )
-            for i, ref in enumerate((down_ref, down2_ref))
-        ]
-        for q in range(QUARTERS)
-    ]
+    second = down_copies((down_ref, down2_ref), downs, down_sems, parity)
     for group in groups + second:
         for copy in group:
             copy.start()
@@ -218,51 +230,92 @@
         total = multiply(total, (left_ref, right_ref)[g], 0, ins, g * half, half)
     gate = total[:, : 2 * width]
     hidden = (gate * jax.nn.sigmoid(gate) * total[:, 2 * width :]).astype(jnp.bfloat16)
-    for q in range(QUARTERS):
-        at = QUARTERS * MAIN + q * TAIL
-        for copy in second[q]:
-            copy.wait()
-        partial = jnp.dot(hidden, downs[q], preferred_element_type=jnp.float32).astype(
-            jnp.bfloat16
-        )
-        for chip in range(chips):
-            outs[chip, q * MAIN : (q + 1) * MAIN] = partial[chip * MAIN : (chip + 1) * MAIN]
-            tail = chips * MAIN + chip * TAIL
-            outs[chip, at : at + TAIL] = partial[tail : tail + TAIL]
-    copies = [
-        pltpu.make_async_copy(outs.at[chip], out_ref.at[chip], out_sems.at[chip])
-        for chip in range(chips)
-    ]
-    for copy in copies:
-        copy.start()
-    for copy in copies:
-        copy.wait()
-
-
-def ffn(total, left, right, chips, *weights):
+    hidden_ref[...] = hidden
+    for b in range(0, 2 * half, 2):
+        partial = down_pair(hidden, downs, second, b).astype(jnp.bfloat16)
+        out_ref, at = (to_right_ref, b) if b < half else (to_left_ref, b - half)
+        out_ref[at] = partial[:, :depth]
+        out_ref[at + 1] = partial[:, depth:]
+
+
+def ffn(total, left, right, *weights):
     half, rows, depth = left.shape
     width, model = weights[-1].shape
-    quarter = model // QUARTERS
     hbm = pl.BlockSpec(memory_space=pltpu.HBM)
     vmem = pl.BlockSpec(memory_space=pltpu.VMEM)
-    out = (chips, QUARTERS * CAP, quarter)
+    sent = jax.ShapeDtypeStruct(left.shape, jnp.bfloat16)
     return pl.pallas_call(
         ffn_kernel,
         in_specs=[vmem] * 3 + [hbm] * 6,
-        out_specs=hbm,
-        out_shape=jax.ShapeDtypeStruct(out, jnp.bfloat16),
+        out_specs=(vmem, vmem, vmem),
+        out_shape=(jax.ShapeDtypeStruct((rows, 2 * width), jnp.bfloat16), sent, sent),
         scratch_shapes=[
             pltpu.VMEM((2 * half, depth, 4 * width), jnp.bfloat16),
-            pltpu.VMEM((QUARTERS, 2 * width, quarter), jnp.bfloat16),
-            pltpu.VMEM(out, jnp.bfloat16),
+            pltpu.VMEM((2 * half, 2 * width, depth), jnp.bfloat16),
             pltpu.SemaphoreType.DMA((2, 4)),
-            pltpu.SemaphoreType.DMA((QUARTERS, 2)),
-            pltpu.SemaphoreType.DMA((chips,)),
+            pltpu.SemaphoreType.DMA((2 * half, 2)),
         ],
-        cost_estimate=cost(2 * rows * model * width * 4, 9000000),
+        cost_estimate=cost(2 * rows * model * width * 3, 7000000),
         compiler_params=pltpu.CompilerParams(vmem_limit_bytes=60 << 20),
         name="ffn",
     )(total, left, right, *weights)
+
+
+def own_down_kernel(hidden_ref, down_ref, down2_ref, out_ref):
+    pairs, _, depth = out_ref.shape
+    parity = lax.axis_index("odd")
+
+    def block(b):
+        lanes = pl.ds(pl.multiple_of((2 * b + parity) * depth, 128), depth)
+        return jnp.concatenate([down_ref[:, lanes], down2_ref[:, lanes]], axis=0)
+
+    for b in range(0, pairs, 2):
+        weight = jnp.concatenate([block(b), block(b + 1)], axis=1)
+        partial = jnp.dot(hidden_ref[...], weight, preferred_element_type=jnp.float32)
+        out_ref[b] = partial[:, :depth]
+        out_ref[b + 1] = partial[:, depth:]
+
+
+def own_down(hidden, down, down2, pairs):
+    rows = hidden.shape[0]
+    width, model = down.shape
+    depth = model // (2 * pairs)
+    return pl.pallas_call(
+        own_down_kernel,
+        out_shape=jax.ShapeDtypeStruct((pairs, rows, depth), jnp.float32),
+        cost_estimate=cost(2 * rows * model * width, 4000000),
+        compiler_params=pltpu.CompilerParams(vmem_limit_bytes=16 << 20),
+        name="own_down",
+    )(hidden, down, down2)
+
+
+def join_kernel(own_ref, left_ref, right_ref, out_ref):
+    pairs, _, depth = own_ref.shape
+    chips = out_ref.shape[0]
+    half = pairs // 2
+    per_quarter = pairs // QUARTERS
+    for b in range(pairs):
+        other = left_ref[b] if b < half else right_ref[b - half]
+        both = (own_ref[b] + other.astype(jnp.float32)).astype(jnp.bfloat16)
+        q, s = b // per_quarter, b % per_quarter
+        at = QUARTERS * MAIN + q * TAIL
+        lanes = slice(s * depth, (s + 1) * depth)
+        for chip in range(chips):
+            tail = chips * MAIN + chip * TAIL
+            out_ref[chip, q * MAIN : (q + 1) * MAIN, lanes] = both[chip * MAIN : (chip + 1) * MAIN]
+            out_ref[chip, at : at + TAIL, lanes] = both[tail : tail + TAIL]
+
+
+def join(own, left, right, chips):
+    pairs, rows, depth = own.shape
+    out = (chips, QUARTERS * CAP, pairs * depth // QUARTERS)
+    return pl.pallas_call(
+        join_kernel,
+        out_shape=jax.ShapeDtypeStruct(out, jnp.bfloat16),
+        cost_estimate=cost(pairs * rows * depth, 8 * pairs * rows * depth),
+        compiler_params=pltpu.CompilerParams(vmem_limit_bytes=16 << 20),
+        name="join",
+    )(own, left, right)
 
 
 def combine_kernel(mix_ref, back_ref, out_ref):
@@ -298,25 +351,30 @@
     swap = [(0, 1), (1, 0)]
     along = ("pair", "odd")
     ids = expert_ids.T
-    outgoing = dispatch(ids, tokens, chips)
-    incoming = lax.all_to_all(outgoing, "x", 0, 0, tiled=True)
-    own = lax.all_gather(gather_rows(incoming), "pair")
-    gate, up, down, own = lax.optimization_barrier((gate_weight, up_weight, down_weight, own))
     up_z = [(i, (i + 1) % parts) for i in range(parts)]
     down_z = [((i + 1) % parts, i) for i in range(parts)]
-    left = lax.ppermute(own[: pairs // 2], along, up_z)
-    right = lax.ppermute(own[pairs // 2 :], along, down_z)
+    outgoing = dispatch(ids, tokens, chips)
+    gate, up, down, outgoing = lax.optimization_barrier(
+        (gate_weight, up_weight, down_weight, outgoing)
+    )
+    incoming = lax.all_to_all(outgoing, "x", 0, 0, tiled=True)
     gate2 = lax.ppermute(gate, "core", swap)
     up2 = lax.ppermute(up, "core", swap)
     down2 = lax.ppermute(down, "core", swap)
+    own = lax.all_gather(gather_rows(incoming), "pair")
+    left = lax.ppermute(own[: pairs // 2], along, up_z)
+    right = lax.ppermute(own[pairs // 2 :], along, down_z)
     blocks = [w.reshape(pairs, 2, depth, w.shape[1]) for w in (gate, gate2, up, up2)]
     total = own_part(own, *blocks)
-    partial_value = ffn(total, left, right, chips, *blocks, down, down2)
+    hidden, to_right, to_left = ffn(total, left, right, *blocks, down, down2)
+    from_left = lax.ppermute(to_right, along, up_z)
+    from_right = lax.ppermute(to_left, along, down_z)
+    partial_value = join(own_down(hidden, down, down2, pairs), from_left, from_right, chips)
     returned = lax.all_to_all(partial_value, "x", 0, 0, tiled=True)
     mix = mixing(ids, route_logits.T, chips)
-    back = returned.reshape(chips * QUARTERS * CAP, parts * depth // QUARTERS)
-    combined = combine(mix, back, count, parts)
-    blocks = lax.all_to_all(combined, along, 0, 0, tiled=True)
+    back = returned.reshape(chips * QUARTERS * CAP, pairs * depth // QUARTERS)
+    combined = combine(mix, back, count, pairs)
+    blocks = lax.all_to_all(combined, "pair", 0, 0, tiled=True)
     return jnp.sum(blocks.astype(jnp.float32), axis=0).astype(jnp.bfloat16)
 
 

time: 208 us -> 183 us (0.88)
  waiting for transfers between devices: 53.8 us -> 26.3 us
  starting transfers between devices: 19.6 us -> 29.3 us
  blocking collectives: 118 us -> 109 us
    all_to_all x1, waiting for transfers between devices: 47.9 us -> 19.6 us  [on_device(): returned = lax.all_to_all(partial_value, 'x', 0, 0, tiled=True)]
    all_to_all x1, blocking collectives: 31.6 us -> 22.8 us  [on_device(): blocks = lax.all_to_all(combined, 'pair', 0, 0, tiled=True)]
    ppermute x0 -> x2, starting transfers between devices: none -> 7.69 us  [the longest x1 4.2 us: on_device(): from_left = lax.ppermute(to_right, along, up_z)]
    ppermute x0 -> x2, waiting for transfers between devices: none -> 4.72 us  [the longest x1 2.42 us: on_device(): from_right = lax.ppermute(to_left, along, down_z)]
    ppermute x1, waiting for transfers between devices: 4.73 us -> 0.64 us  [on_device(): left = lax.ppermute(own[:pairs // 2], along, up_z)]
    unnamed x14 -> x18, local copies, waits for them, and re-layouts: 2.62 us -> 4.88 us
    pallas_call x1 -> x3, Pallas kernels: 6.25 us -> 7.14 us  [the longest x1 5.58 us: ffn(): pl.pallas_call(ffn_kernel, in_specs=[vmem] * 3 + [hbm] * 6, out_specs=(vm...]
  transfers between devices with their start and end apart: 6 -> 8, of which waited for: 3 -> 5; matrix products, arithmetic and copies ran while one was open for 1% -> 0% of each run, Pallas kernels for 2% -> 3%
where the time goes in v4:
time: 183 us; the launch traced here: 182 us
  blocking collectives  109 us (60%)
  starting transfers between devices  29.3 us (16%)
  waiting for transfers between devices  26.3 us (14%)
  Pallas kernels  12.3 us (7%)
  local copies, waits for them, and re-layouts  5.15 us (3%)
    all_gather x1, blocking collectives, on_device(): own = lax.all_gather(gather_rows(incoming), 'pair')  68.6 us
    all_to_all x1, blocking collectives, on_device(): blocks = lax.all_to_all(combined, 'pair', 0, 0, tiled=True)  22.8 us
    all_to_all x1, waiting for transfers between devices, on_device(): returned = lax.all_to_all(partial_value, 'x', 0, 0, tiled=True)  19.6 us
    all_to_all x1, blocking collectives, on_device(): incoming = lax.all_to_all(outgoing, 'x', 0, 0, tiled=True)  17.2 us
    ppermute x1, starting transfers between devices, on_device(): left = lax.ppermute(own[:pairs // 2], along, up_z)  6.28 us
    pallas_call x1, Pallas kernels, ffn(): pl.pallas_call(ffn_kernel, in_specs=[vmem] * 3 + [hbm] * 6, out_specs=(vm...  5.58 us
    ppermute x1, starting transfers between devices, on_device(): right = lax.ppermute(own[pairs // 2:], along, down_z)  5.06 us
    unnamed x18, local copies, waits for them, and re-layouts  4.88 us
  transfers between devices with their start and end apart: 8, of which 5 were waited for; matrix products, arithmetic and copies ran while one was open for 0% of the time, Pallas kernels for 3%

profile of v4, /device:TPU:80, one launch (start us, length us, event | category | flops | bytes accessed | tf_op | source)
XLA Modules:
  0.0 182.4 jit_solution(12991524027968864190)
XLA Ops:
  0.0 0.7 copy-done.4
  0.7 0.7 copy-done.5
  1.7 2.0 %collective-permute-start = (bf16[6144,128]{1,0:T(8,128)(2,1)}, bf16[6144,128]{1,0:T(8,128)(2,1)}, u32[]{:S(2)}, u32[]{:S(2)}) collective-permute-start(bf16[6144,128]{1,0:T(8,128)(2,1)} %param.9), channel_id=1, source_target_pairs={{0,16},{16,0},{1,17},{17,1},{2,18},{18,2},{3,19},{19,3},{4,20},{20... | collective-permute-start | bytes 4718600 | tf_op jit(solution)/shard_map/ppermute | solution.py:361
  3.6 2.4 %collective-permute-start.1 = (bf16[6144,128]{1,0:T(8,128)(2,1)}, bf16[6144,128]{1,0:T(8,128)(2,1)}, u32[]{:S(2)}, u32[]{:S(2)}) collective-permute-start(bf16[6144,128]{1,0:T(8,128)(2,1)} %param.10), channel_id=1, source_target_pairs={{0,16},{16,0},{1,17},{17,1},{2,18},{18,2},{3,19},{19,3},{4,20},{20... | collective-permute-start | bytes 4718600 | tf_op jit(solution)/shard_map/ppermute | solution.py:362
  6.1 2.0 %collective-permute-start.4 = (bf16[128,6144]{1,0:T(8,128)(2,1)}, bf16[128,6144]{1,0:T(8,128)(2,1)S(1)}, u32[]{:S(2)}, u32[]{:S(2)}) collective-permute-start(bf16[128,6144]{1,0:T(8,128)(2,1)} %down_ref.1), channel_id=1, source_target_pairs={{0,16},{16,0},{1,17},{17,1},{2,18},{18,2},{3,19},{19,3},{4,20},{20... | collective-permute-start | bytes 4718600 | tf_op jit(solution)/shard_map/ppermute | solution.py:363
  8.1 17.2 %all_to_all.15.in_ref = bf16[8,20,384]{2,1,0:T(8,128)(2,1)S(1)} all-to-all(bf16[8,20,384]{2,1,0:T(8,128)(2,1)S(1)} %dispatch.1), channel_id=1, replica_groups=mesh['rep'=2,'x'=8,'core'=2,'pair'=8,'odd'=2] {'x'}, dimensions={0} | all-to-all | bytes 245760 | tf_op jit(solution)/shard_map/all_to_all | solution.py:360
  25.3 68.6 %all-gather = bf16[1280,384]{1,0:T(8,128)(2,1)S(1)} all-gather(bf16[160,384]{1,0:T(8,128)(2,1)S(1)} %gather_rows.1), channel_id=2, replica_groups=mesh['rep'=2,'x'=8,'core'=2,'pair'=8,'odd'=2] {'pair'}, dimensions={0}, use_global_device_ids=true | all-gather | bytes 1105920 | tf_op jit(solution)/shard_map/all_gather | solution.py:364
  94.0 6.3 %collective-permute-start.2 = (bf16[4,160,384]{2,1,0:T(8,128)(2,1)S(1)}, bf16[4,160,384]{2,1,0:T(8,128)(2,1)}, u32[]{:S(2)}, u32[]{:S(2)}) collective-permute-start(bf16[4,160,384]{2,1,0:T(8,128)(2,1)S(1)} %bitcast.19), channel_id=1, source_target_pairs={{0,1},{1,2},{2,3},{3,4},{4,5},{5,6},{6,7},{7,8},{8,9},{9,10},{10,1... | collective-permute-start | bytes 1474568 | tf_op jit(solution)/shard_map/ppermute | solution.py:365
  100.3 5.1 %collective-permute-start.3 = (bf16[4,160,384]{2,1,0:T(8,128)(2,1)S(1)}, bf16[4,160,384]{2,1,0:T(8,128)(2,1)}, u32[]{:S(2)}, u32[]{:S(2)}) collective-permute-start(bf16[4,160,384]{2,1,0:T(8,128)(2,1)S(1)} %bitcast.18), channel_id=1, source_target_pairs={{1,0},{2,1},{3,2},{4,3},{5,4},{6,5},{7,6},{8,7},{9,8},{10,9},{11,1... | collective-permute-start | bytes 1474568 | tf_op jit(solution)/shard_map/ppermute | solution.py:366
  105.4 4.3 %own_part.1.total_ref = f32[160,512]{1,0:T(8,128)} custom-call(bf16[8,160,384]{2,1,0:T(8,128)(2,1)} %bitcast.13, bf16[8,2,384,128]{3,2,1,0:T(8,128)(2,1)} %bitcast.14, bf16[8,2,384,128]{3,2,1,0:T(8,128)(2,1)} %bitcast.4.gate2_ref, bf16[8,2,384,128]{3,2,1,0:T(8,128)(2,1)} %bitcast.16, bf16[8,2,384,128]{3,2,1,0:T(8,128)(2,1)} %bitcast.6.up2_ref), custom_call_target="tpu_custom_call" | custom-call | flops 503316480 | bytes 4200000 | tf_op jit(solution)/shard_map/own_part/pallas_call | solution.py:166
  110.3 1.4 collective-permute-done.3.right_ref
  111.7 1.2 copy-done.1
  112.8 5.6 %ffn.1 = (bf16[160,256]{1,0:T(8,128)(2,1)}, bf16[4,160,384]{2,1,0:T(8,128)(2,1)}, bf16[4,160,384]{2,1,0:T(8,128)(2,1)}) custom-call(f32[160,512]{1,0:T(8,128)} %own_part.1.total_ref, bf16[4,160,384]{2,1,0:T(8,128)(2,1)} %collective-permute-done.2.left_ref, bf16[4,160,384]{2,1,0:T(8,128)(2,1)} %collective-permute-done.3.right_ref, ...), custom_call_target="tpu_custom_call" | custom-call | flops 754974720 | bytes 7000000 | tf_op jit(solution)/shard_map/ffn/pallas_call | solution.py:247
  118.4 4.2 %collective-permute-start.5 = (bf16[4,160,384]{2,1,0:T(8,128)(2,1)}, bf16[4,160,384]{2,1,0:T(8,128)(2,1)S(1)}, u32[]{:S(2)}, u32[]{:S(2)}) collective-permute-start(bf16[4,160,384]{2,1,0:T(8,128)(2,1)} %get-tuple-element.17), channel_id=1, source_target_pairs={{0,1},{1,2},{2,3},{3,4},{4,5},{5,6},{6,7},{7,8},{8,9},{9,10},{10,1... | collective-permute-start | bytes 1474568 | tf_op jit(solution)/shard_map/ppermute | solution.py:370
  122.6 3.5 %collective-permute-start.6 = (bf16[4,160,384]{2,1,0:T(8,128)(2,1)}, bf16[4,160,384]{2,1,0:T(8,128)(2,1)S(1)}, u32[]{:S(2)}, u32[]{:S(2)}) collective-permute-start(bf16[4,160,384]{2,1,0:T(8,128)(2,1)} %get-tuple-element.18), channel_id=1, source_target_pairs={{1,0},{2,1},{3,2},{4,3},{5,4},{6,5},{7,6},{8,7},{9,8},{10,9},{11,1... | collective-permute-start | bytes 1474568 | tf_op jit(solution)/shard_map/ppermute | solution.py:371
  126.2 1.4 copy-done.2
  127.6 0.9 copy-done.3
  128.9 2.3 %collective-permute-done.5.left_ref = bf16[4,160,384]{2,1,0:T(8,128)(2,1)S(1)} collective-permute-done((bf16[4,160,384]{2,1,0:T(8,128)(2,1)}, bf16[4,160,384]{2,1,0:T(8,128)(2,1)S(1)}, u32[]{:S(2)}, u32[]{:S(2)}) %collective-permute-start.5) | collective-permute-done | bytes 491552 | tf_op jit(solution)/shard_map/ppermute | solution.py:370
  131.2 2.4 %collective-permute-done.6.right_ref = bf16[4,160,384]{2,1,0:T(8,128)(2,1)S(1)} collective-permute-done((bf16[4,160,384]{2,1,0:T(8,128)(2,1)}, bf16[4,160,384]{2,1,0:T(8,128)(2,1)S(1)}, u32[]{:S(2)}, u32[]{:S(2)}) %collective-permute-start.6) | collective-permute-done | bytes 491552 | tf_op jit(solution)/shard_map/ppermute | solution.py:371
  133.6 1.1 join.1
  134.7 3.9 %all-to-all-start.1 = ((bf16[8,80,768]{2,1,0:T(8,128)(2,1)}), bf16[8,80,768]{2,1,0:T(8,128)(2,1)S(1)}, u32[]{:S(2)}, u32[]{:S(2)}) async-start(bf16[8,80,768]{2,1,0:T(8,128)(2,1)} %join.1), calls=%async_computation.1 | async-start | bytes 1966080 | tf_op jit(solution)/shard_map/all_to_all | solution.py:373
  139.1 19.6 %all-to-all-done.1 = bf16[8,80,768]{2,1,0:T(8,128)(2,1)S(1)} async-done(((bf16[8,80,768]{2,1,0:T(8,128)(2,1)}), bf16[8,80,768]{2,1,0:T(8,128)(2,1)S(1)}, u32[]{:S(2)}, u32[]{:S(2)}) %all-to-all-start.1) | async-done | bytes 983072 | tf_op jit(solution)/shard_map/all_to_all | solution.py:373
  159.0 22.8 %all_to_all.16 = bf16[8,32,384]{2,1,0:T(8,128)(2,1)S(1)} all-to-all(bf16[8,32,384]{2,1,0:T(8,128)(2,1)S(1)} %combine.1), channel_id=1, replica_groups=mesh['rep'=2,'x'=8,'core'=2,'pair'=8,'odd'=2] {'pair'}, dimensions={0} | all-to-all | bytes 393216 | tf_op jit(solution)/shard_map/all_to_all | solution.py:377
  181.8 0.6 reduce_sum.12
  (27 shorter events, 2.2 us)
Async XLA Ops:
  0.0 0.7 copy-start.4
  0.7 0.7 copy-start.5
  1.7 103.7 %collective-permute-start = (bf16[6144,128]{1,0:T(8,128)(2,1)}, bf16[6144,128]{1,0:T(8,128)(2,1)}, u32[]{:S(2)}, u32[]{:S(2)}) collective-permute-start(bf16[6144,128]{1,0:T(8,128)(2,1)} %param.9), channel_id=1, source_target_pairs={{0,16},{16,0},{1,17},{17,1},{2,18},{18,2},{3,19},{19,3},{4,20},{20... | collective-permute-start | bytes 4718600 | tf_op jit(solution)/shard_map/ppermute | solution.py:361
  3.6 101.7 %collective-permute-start.1 = (bf16[6144,128]{1,0:T(8,128)(2,1)}, bf16[6144,128]{1,0:T(8,128)(2,1)}, u32[]{:S(2)}, u32[]{:S(2)}) collective-permute-start(bf16[6144,128]{1,0:T(8,128)(2,1)} %param.10), channel_id=1, source_target_pairs={{0,16},{16,0},{1,17},{17,1},{2,18},{18,2},{3,19},{19,3},{4,20},{20... | collective-permute-start | bytes 4718600 | tf_op jit(solution)/shard_map/ppermute | solution.py:362
  6.1 105.6 %collective-permute-start.4 = (bf16[128,6144]{1,0:T(8,128)(2,1)}, bf16[128,6144]{1,0:T(8,128)(2,1)S(1)}, u32[]{:S(2)}, u32[]{:S(2)}) collective-permute-start(bf16[128,6144]{1,0:T(8,128)(2,1)} %down_ref.1), channel_id=1, source_target_pairs={{0,16},{16,0},{1,17},{17,1},{2,18},{18,2},{3,19},{19,3},{4,20},{20... | collective-permute-start | bytes 4718600 | tf_op jit(solution)/shard_map/ppermute | solution.py:363
  93.9 11.5 %copy-start.7 = (bf16[1280,384]{1,0:T(8,128)(2,1)}, bf16[1280,384]{1,0:T(8,128)(2,1)S(1)}, u32[]{:S(2)}) copy-start(bf16[1280,384]{1,0:T(8,128)(2,1)S(1)} %all-gather) | copy-start | bytes 2949124
  94.0 16.3 %collective-permute-start.2 = (bf16[4,160,384]{2,1,0:T(8,128)(2,1)S(1)}, bf16[4,160,384]{2,1,0:T(8,128)(2,1)}, u32[]{:S(2)}, u32[]{:S(2)}) collective-permute-start(bf16[4,160,384]{2,1,0:T(8,128)(2,1)S(1)} %bitcast.19), channel_id=1, source_target_pairs={{0,1},{1,2},{2,3},{3,4},{4,5},{5,6},{6,7},{7,8},{8,9},{9,10},{10,1... | collective-permute-start | bytes 1474568 | tf_op jit(solution)/shard_map/ppermute | solution.py:365
  100.3 11.4 %collective-permute-start.3 = (bf16[4,160,384]{2,1,0:T(8,128)(2,1)S(1)}, bf16[4,160,384]{2,1,0:T(8,128)(2,1)}, u32[]{:S(2)}, u32[]{:S(2)}) collective-permute-start(bf16[4,160,384]{2,1,0:T(8,128)(2,1)S(1)} %bitcast.18), channel_id=1, source_target_pairs={{1,0},{2,1},{3,2},{4,3},{5,4},{6,5},{7,6},{8,7},{9,8},{10,9},{11,1... | collective-permute-start | bytes 1474568 | tf_op jit(solution)/shard_map/ppermute | solution.py:366
  109.6 16.5 %copy-start = (bf16[128,6144]{1,0:T(8,128)(2,1)S(1)}, bf16[128,6144]{1,0:T(8,128)(2,1)}, u32[]{:S(2)}) copy-start(bf16[128,6144]{1,0:T(8,128)(2,1)} %down_ref.1) | copy-start | bytes 4718596
  111.7 1.2 copy-start.1
  118.4 12.8 %collective-permute-start.5 = (bf16[4,160,384]{2,1,0:T(8,128)(2,1)}, bf16[4,160,384]{2,1,0:T(8,128)(2,1)S(1)}, u32[]{:S(2)}, u32[]{:S(2)}) collective-permute-start(bf16[4,160,384]{2,1,0:T(8,128)(2,1)} %get-tuple-element.17), channel_id=1, source_target_pairs={{0,1},{1,2},{2,3},{3,4},{4,5},{5,6},{6,7},{7,8},{8,9},{9,10},{10,1... | collective-permute-start | bytes 1474568 | tf_op jit(solution)/shard_map/ppermute | solution.py:370
  122.6 11.0 %collective-permute-start.6 = (bf16[4,160,384]{2,1,0:T(8,128)(2,1)}, bf16[4,160,384]{2,1,0:T(8,128)(2,1)S(1)}, u32[]{:S(2)}, u32[]{:S(2)}) collective-permute-start(bf16[4,160,384]{2,1,0:T(8,128)(2,1)} %get-tuple-element.18), channel_id=1, source_target_pairs={{1,0},{2,1},{3,2},{4,3},{5,4},{6,5},{7,6},{8,7},{9,8},{10,9},{11,1... | collective-permute-start | bytes 1474568 | tf_op jit(solution)/shard_map/ppermute | solution.py:371
  126.1 1.4 copy-start.2
  127.6 0.9 copy-start.3
  134.7 3.9 %copy-start.6 = (s32[32,2]{0,1:T(2,128)S(1)}, s32[32,2]{0,1:T(2,128)}, u32[]{:S(2)}) copy-start(s32[32,2]{0,1:T(2,128)} %param.7) | copy-start | bytes 772
  134.7 4.0 %copy-start.8 = (f32[32,2]{0,1:T(2,128)S(1)}, f32[32,2]{0,1:T(2,128)}, u32[]{:S(2)}) copy-start(f32[32,2]{0,1:T(2,128)} %param.8) | copy-start | bytes 772
  134.7 23.9 %all-to-all-start.1 = ((bf16[8,80,768]{2,1,0:T(8,128)(2,1)}), bf16[8,80,768]{2,1,0:T(8,128)(2,1)S(1)}, u32[]{:S(2)}, u32[]{:S(2)}) async-start(bf16[8,80,768]{2,1,0:T(8,128)(2,1)} %join.1), calls=%async_computation.1 | async-start | bytes 1966080 | tf_op jit(solution)/shard_map/all_to_all | solution.py:373

commit v5 on v4

--- a/solution.py
+++ b/solution.py
@@ -67,7 +67,7 @@
         functools.partial(dispatch_kernel, chips),
         out_shape=jax.ShapeDtypeStruct((chips, CAP, features), jnp.bfloat16),
         cost_estimate=cost(2 * EXPERTS * CAP * count * features, 200000),
-        compiler_params=pltpu.CompilerParams(vmem_limit_bytes=4 << 20),
+        compiler_params=pltpu.CompilerParams(vmem_limit_bytes=60 << 20),
         name="dispatch",
     )(ids, tokens)
 
@@ -122,141 +122,76 @@
     )(jnp.tile(ids, (1, QUARTERS)), jnp.tile(logits, (1, QUARTERS)))
 
 
-def multiply(total, tokens, first, weights, start, number):
-    for b in range(0, number, 2):
-        rows = jnp.concatenate([tokens[first + b], tokens[first + b + 1]], axis=1)
-        weight = jnp.concatenate([weights[start + b], weights[start + b + 1]], axis=0)
+def side_by_side(refs, b, parity):
+    return jnp.concatenate([ref[b, parity] for ref in refs], axis=1)
+
+
+def multiply(total, tokens, refs, parity, start):
+    for b in range(0, tokens.shape[0], 2):
+        rows = jnp.concatenate([tokens[b], tokens[b + 1]], axis=1)
+        weight = jnp.concatenate(
+            [side_by_side(refs, start + b, parity), side_by_side(refs, start + b + 1, parity)],
+            axis=0,
+        )
         added = jnp.dot(rows, weight, preferred_element_type=jnp.float32)
         total = added if total is None else total + added
     return total
 
 
-def own_kernel(slots_ref, gate_ref, gate2_ref, up_ref, up2_ref, out_ref, ins, sems):
-    pairs = slots_ref.shape[0]
-    parity = lax.axis_index("odd")
-    width = gate_ref.shape[-1]
-    half = pairs // 2
+def own_kernel(slots_ref, gate_ref, gate2_ref, up_ref, up2_ref, out_ref):
     refs = (gate_ref, gate2_ref, up_ref, up2_ref)
-    groups = [
-        [
-            pltpu.make_async_copy(
-                ref.at[pl.ds(g * half, half), parity],
-                ins.at[pl.ds(g * half, half), :, pl.ds(i * width, width)],
-                sems.at[g, i],
-            )
-            for i, ref in enumerate(refs)
-        ]
-        for g in range(2)
-    ]
-    for group in groups:
-        for copy in group:
-            copy.start()
-    total = None
-    for g, group in enumerate(groups):
-        for copy in group:
-            copy.wait()
-        total = multiply(total, slots_ref, g * half, ins, g * half, half)
-    out_ref[...] = total
+    out_ref[...] = multiply(None, slots_ref, refs, lax.axis_index("odd"), 0)
 
 
 def own_part(slots, *weights):
     pairs, rows, depth = slots.shape
     width = weights[0].shape[-1]
-    hbm = pl.BlockSpec(memory_space=pltpu.HBM)
     return pl.pallas_call(
         own_kernel,
-        in_specs=[pl.BlockSpec(memory_space=pltpu.VMEM)] + [hbm] * 4,
-        out_specs=pl.BlockSpec(memory_space=pltpu.VMEM),
         out_shape=jax.ShapeDtypeStruct((rows, 4 * width), jnp.float32),
-        scratch_shapes=[
-            pltpu.VMEM((pairs, depth, 4 * width), jnp.bfloat16),
-            pltpu.SemaphoreType.DMA((2, 4)),
-        ],
         cost_estimate=cost(2 * pairs * rows * depth * 4 * width, 4200000),
-        compiler_params=pltpu.CompilerParams(vmem_limit_bytes=60 << 20),
+        compiler_params=pltpu.CompilerParams(vmem_limit_bytes=16 << 20),
         name="own_part",
     )(slots, *weights)
 
 
-def down_copies(refs, scratch, sems, parity):
-    pairs, _, depth = scratch.shape
-    width = refs[0].shape[0]
-    return [
-        [
-            pltpu.make_async_copy(
-                ref.at[:, pl.ds(pl.multiple_of((2 * b + parity) * depth, 128), depth)],
-                scratch.at[b, pl.ds(i * width, width)],
-                sems.at[b, i],
-            )
-            for i, ref in enumerate(refs)
-        ]
-        for b in range(pairs)
-    ]
-
-
-def down_pair(hidden, scratch, copies, b):
-    for copy in copies[b] + copies[b + 1]:
-        copy.wait()
-    weight = jnp.concatenate([scratch[b], scratch[b + 1]], axis=1)
+def down_pair(hidden, refs, b, parity, depth):
+    def block(b):
+        lanes = pl.ds(pl.multiple_of((2 * b + parity) * depth, 128), depth)
+        return jnp.concatenate([ref[:, lanes] for ref in refs], axis=0)
+
+    weight = jnp.concatenate([block(b), block(b + 1)], axis=1)
     return jnp.dot(hidden, weight, preferred_element_type=jnp.float32)
 
 
 def ffn_kernel(
-    total_ref, left_ref, right_ref, gate_ref, gate2_ref, up_ref, up2_ref, down_ref, down2_ref, hidden_ref, to_right_ref, to_left_ref, ins, downs, in_sems, down_sems
+    total_ref, left_ref, right_ref, gate_ref, gate2_ref, up_ref, up2_ref, down_ref, down2_ref, hidden_ref, to_right_ref, to_left_ref
 ):
     half, _, depth = left_ref.shape
     parity = 1 - lax.axis_index("odd")
     width = gate_ref.shape[-1]
     refs = (gate_ref, gate2_ref, up_ref, up2_ref)
-    groups = [
-        [
-            pltpu.make_async_copy(
-                ref.at[pl.ds(g * half, half), parity],
-                ins.at[pl.ds(g * half, half), :, pl.ds(i * width, width)],
-                in_sems.at[g, i],
-            )
-            for i, ref in enumerate(refs)
-        ]
-        for g in range(2)
-    ]
-    second = down_copies((down_ref, down2_ref), downs, down_sems, parity)
-    for group in groups + second:
-        for copy in group:
-            copy.start()
-    total = total_ref[...]
-    for g, group in enumerate(groups):
-        for copy in group:
-            copy.wait()
-        total = multiply(total, (left_ref, right_ref)[g], 0, ins, g * half, half)
+    total = multiply(total_ref[...], left_ref, refs, parity, 0)
+    total = multiply(total, right_ref, refs, parity, half)
     gate = total[:, : 2 * width]
     hidden = (gate * jax.nn.sigmoid(gate) * total[:, 2 * width :]).astype(jnp.bfloat16)
     hidden_ref[...] = hidden
     for b in range(0, 2 * half, 2):
-        partial = down_pair(hidden, downs, second, b).astype(jnp.bfloat16)
+        partial = down_pair(hidden, (down_ref, down2_ref), b, parity, depth).astype(jnp.bfloat16)
         out_ref, at = (to_right_ref, b) if b < half else (to_left_ref, b - half)
         out_ref[at] = partial[:, :depth]
         out_ref[at + 1] = partial[:, depth:]
 
 
 def ffn(total, left, right, *weights):
-    half, rows, depth = left.shape
+    _, rows, _ = left.shape
     width, model = weights[-1].shape
-    hbm = pl.BlockSpec(memory_space=pltpu.HBM)
-    vmem = pl.BlockSpec(memory_space=pltpu.VMEM)
     sent = jax.ShapeDtypeStruct(left.shape, jnp.bfloat16)
     return pl.pallas_call(
         ffn_kernel,
-        in_specs=[vmem] * 3 + [hbm] * 6,
-        out_specs=(vmem, vmem, vmem),
         out_shape=(jax.ShapeDtypeStruct((rows, 2 * width), jnp.bfloat16), sent, sent),
-        scratch_shapes=[
-            pltpu.VMEM((2 * half, depth, 4 * width), jnp.bfloat16),
-            pltpu.VMEM((2 * half, 2 * width, depth), jnp.bfloat16),
-            pltpu.SemaphoreType.DMA((2, 4)),
-            pltpu.SemaphoreType.DMA((2 * half, 2)),
-        ],
         cost_estimate=cost(2 * rows * model * width * 3, 7000000),
-        compiler_params=pltpu.CompilerParams(vmem_limit_bytes=60 << 20),
+        compiler_params=pltpu.CompilerParams(vmem_limit_bytes=20 << 20),
         name="ffn",
     )(total, left, right, *weights)
 
@@ -264,14 +199,8 @@
 def own_down_kernel(hidden_ref, down_ref, down2_ref, out_ref):
     pairs, _, depth = out_ref.shape
     parity = lax.axis_index("odd")
-
-    def block(b):
-        lanes = pl.ds(pl.multiple_of((2 * b + parity) * depth, 128), depth)
-        return jnp.concatenate([down_ref[:, lanes], down2_ref[:, lanes]], axis=0)
-
     for b in range(0, pairs, 2):
-        weight = jnp.concatenate([block(b), block(b + 1)], axis=1)
-        partial = jnp.dot(hidden_ref[...], weight, preferred_element_type=jnp.float32)
+        partial = down_pair(hidden_ref[...], (down_ref, down2_ref), b, parity, depth)
         out_ref[b] = partial[:, :depth]
         out_ref[b + 1] = partial[:, depth:]
 

time: 183 us -> 177 us (0.967)
  Pallas kernels: 12.3 us -> 5.59 us
  waiting for transfers between devices: 26.3 us -> 32 us
  local copies, waits for them, and re-layouts: 5.15 us -> 0.29 us
    pallas_call x2, Pallas kernels: 9.83 us -> 1.74 us  [the longest x1 1.06 us: ffn(): pl.pallas_call(ffn_kernel, out_shape=(jax.ShapeDtypeStruct((rows, 2 * wid...]
    unnamed x18 -> x10, local copies, waits for them, and re-layouts: 4.88 us -> 0.02 us
    ppermute x1, waiting for transfers between devices: 0.64 us -> 4.09 us  [on_device(): left = lax.ppermute(own[:pairs // 2], along, up_z)]
    ppermute x1, waiting for transfers between devices: 2.3 us -> 4.38 us  [on_device(): from_left = lax.ppermute(to_right, along, up_z)]
  transfers between devices with their start and end apart: 8 -> 8, of which waited for: 5 -> 5; matrix products, arithmetic and copies ran while one was open for 0% -> 0% of each run, Pallas kernels for 3% -> 1%
where the time goes in v5:
time: 177 us
  blocking collectives  109 us (62%)
  waiting for transfers between devices  32 us (18%)
  starting transfers between devices  29 us (16%)
  Pallas kernels  5.59 us (3%)
    all_gather x1, blocking collectives, on_device(): own = lax.all_gather(gather_rows(incoming), 'pair')  68.7 us
    all_to_all x1, blocking collectives, on_device(): blocks = lax.all_to_all(combined, 'pair', 0, 0, tiled=True)  22.9 us
    all_to_all x1, waiting for transfers between devices, on_device(): returned = lax.all_to_all(partial_value, 'x', 0, 0, tiled=True)  19.1 us
    all_to_all x1, blocking collectives, on_device(): incoming = lax.all_to_all(outgoing, 'x', 0, 0, tiled=True)  17.4 us
    ppermute x1, starting transfers between devices, on_device(): left = lax.ppermute(own[:pairs // 2], along, up_z)  6.17 us
    ppermute x1, starting transfers between devices, on_device(): right = lax.ppermute(own[pairs // 2:], along, down_z)  5.05 us
    ppermute x1, waiting for transfers between devices, on_device(): from_left = lax.ppermute(to_right, along, up_z)  4.38 us
    ppermute x1, starting transfers between devices, on_device(): from_left = lax.ppermute(to_right, along, up_z)  4.2 us
  transfers between devices with their start and end apart: 8, of which 5 were waited for; matrix products, arithmetic and copies ran while one was open for 0% of the time, Pallas kernels for 1%

profile of v5, /device:TPU:80, one launch (start us, length us, event | category | flops | bytes accessed | tf_op | source)
XLA Modules:
  0.0 176.7 jit_solution(6924475672214678693)
XLA Ops:
  0.0 1.7 dispatch.1
  1.7 1.9 %collective-permute-start = (bf16[6144,128]{1,0:T(8,128)(2,1)}, bf16[6144,128]{1,0:T(8,128)(2,1)S(1)}, u32[]{:S(2)}, u32[]{:S(2)}) collective-permute-start(bf16[6144,128]{1,0:T(8,128)(2,1)} %param.9), channel_id=1, source_target_pairs={{0,16},{16,0},{1,17},{17,1},{2,18},{18,2},{3,19},{19,3},{4,20},{20... | collective-permute-start | bytes 4718600 | tf_op jit(solution)/shard_map/ppermute | solution.py:290
  3.6 2.4 %collective-permute-start.1 = (bf16[6144,128]{1,0:T(8,128)(2,1)}, bf16[6144,128]{1,0:T(8,128)(2,1)S(1)}, u32[]{:S(2)}, u32[]{:S(2)}) collective-permute-start(bf16[6144,128]{1,0:T(8,128)(2,1)} %param.10), channel_id=1, source_target_pairs={{0,16},{16,0},{1,17},{17,1},{2,18},{18,2},{3,19},{19,3},{4,20},{20... | collective-permute-start | bytes 4718600 | tf_op jit(solution)/shard_map/ppermute | solution.py:291
  6.1 2.0 %collective-permute-start.4 = (bf16[128,6144]{1,0:T(8,128)(2,1)}, bf16[128,6144]{1,0:T(8,128)(2,1)S(1)}, u32[]{:S(2)}, u32[]{:S(2)}) collective-permute-start(bf16[128,6144]{1,0:T(8,128)(2,1)} %down_ref.1), channel_id=1, source_target_pairs={{0,16},{16,0},{1,17},{17,1},{2,18},{18,2},{3,19},{19,3},{4,20},{20... | collective-permute-start | bytes 4718600 | tf_op jit(solution)/shard_map/ppermute | solution.py:292
  8.0 17.4 %all_to_all.15.in_ref = bf16[8,20,384]{2,1,0:T(8,128)(2,1)S(1)} all-to-all(bf16[8,20,384]{2,1,0:T(8,128)(2,1)} %dispatch.1), channel_id=1, replica_groups=mesh['rep'=2,'x'=8,'core'=2,'pair'=8,'odd'=2] {'x'}, dimensions={0} | all-to-all | bytes 245760 | tf_op jit(solution)/shard_map/all_to_all | solution.py:289
  25.5 68.7 %all-gather = bf16[1280,384]{1,0:T(8,128)(2,1)S(1)} all-gather(bf16[160,384]{1,0:T(8,128)(2,1)S(1)} %gather_rows.1), channel_id=2, replica_groups=mesh['rep'=2,'x'=8,'core'=2,'pair'=8,'odd'=2] {'pair'}, dimensions={0}, use_global_device_ids=true | all-gather | bytes 1105920 | tf_op jit(solution)/shard_map/all_gather | solution.py:293
  94.3 6.2 %collective-permute-start.2 = (bf16[4,160,384]{2,1,0:T(8,128)(2,1)S(1)}, bf16[4,160,384]{2,1,0:T(8,128)(2,1)S(1)}, u32[]{:S(2)}, u32[]{:S(2)}) collective-permute-start(bf16[4,160,384]{2,1,0:T(8,128)(2,1)S(1)} %bitcast.21), channel_id=1, source_target_pairs={{0,1},{1,2},{2,3},{3,4},{4,5},{5,6},{6,7},{7,8},{8,9},{9,10},{10,1... | collective-permute-start | bytes 1474568 | tf_op jit(solution)/shard_map/ppermute | solution.py:294
  100.5 5.1 %collective-permute-start.3 = (bf16[4,160,384]{2,1,0:T(8,128)(2,1)S(1)}, bf16[4,160,384]{2,1,0:T(8,128)(2,1)S(1)}, u32[]{:S(2)}, u32[]{:S(2)}) collective-permute-start(bf16[4,160,384]{2,1,0:T(8,128)(2,1)S(1)} %bitcast.20), channel_id=1, source_target_pairs={{1,0},{2,1},{3,2},{4,3},{5,4},{6,5},{7,6},{8,7},{9,8},{10,9},{11,1... | collective-permute-start | bytes 1474568 | tf_op jit(solution)/shard_map/ppermute | solution.py:295
  105.6 0.7 own_part.1.total_ref
  106.3 4.1 %collective-permute-done.2.left_ref = bf16[4,160,384]{2,1,0:T(8,128)(2,1)S(1)} collective-permute-done((bf16[4,160,384]{2,1,0:T(8,128)(2,1)S(1)}, bf16[4,160,384]{2,1,0:T(8,128)(2,1)S(1)}, u32[]{:S(2)}, u32[]{:S(2)}) %collective-permute-start.2) | collective-permute-done | bytes 491552 | tf_op jit(solution)/shard_map/ppermute | solution.py:294
  110.4 1.5 collective-permute-done.3.right_ref
  111.9 1.1 ffn.1
  112.9 4.2 %collective-permute-start.5 = (bf16[4,160,384]{2,1,0:T(8,128)(2,1)S(1)}, bf16[4,160,384]{2,1,0:T(8,128)(2,1)S(1)}, u32[]{:S(2)}, u32[]{:S(2)}) collective-permute-start(bf16[4,160,384]{2,1,0:T(8,128)(2,1)S(1)} %get-tuple-element.17), channel_id=1, source_target_pairs={{0,1},{1,2},{2,3},{3,4},{4,5},{5,6},{6,7},{7,8},{8,9},{9,10},{10,1... | collective-permute-start | bytes 1474568 | tf_op jit(solution)/shard_map/ppermute | solution.py:299
  117.1 3.4 %collective-permute-start.6 = (bf16[4,160,384]{2,1,0:T(8,128)(2,1)S(1)}, bf16[4,160,384]{2,1,0:T(8,128)(2,1)S(1)}, u32[]{:S(2)}, u32[]{:S(2)}) collective-permute-start(bf16[4,160,384]{2,1,0:T(8,128)(2,1)S(1)} %get-tuple-element.18), channel_id=1, source_target_pairs={{1,0},{2,1},{3,2},{4,3},{5,4},{6,5},{7,6},{8,7},{9,8},{10,9},{11,1... | collective-permute-start | bytes 1474568 | tf_op jit(solution)/shard_map/ppermute | solution.py:300
  120.5 0.4 own_down.1.own_ref
  121.0 4.4 %collective-permute-done.5.left_ref = bf16[4,160,384]{2,1,0:T(8,128)(2,1)S(1)} collective-permute-done((bf16[4,160,384]{2,1,0:T(8,128)(2,1)S(1)}, bf16[4,160,384]{2,1,0:T(8,128)(2,1)S(1)}, u32[]{:S(2)}, u32[]{:S(2)}) %collective-permute-start.5) | collective-permute-done | bytes 491552 | tf_op jit(solution)/shard_map/ppermute | solution.py:299
  125.4 2.8 %collective-permute-done.6.right_ref = bf16[4,160,384]{2,1,0:T(8,128)(2,1)S(1)} collective-permute-done((bf16[4,160,384]{2,1,0:T(8,128)(2,1)S(1)}, bf16[4,160,384]{2,1,0:T(8,128)(2,1)S(1)}, u32[]{:S(2)}, u32[]{:S(2)}) %collective-permute-start.6) | collective-permute-done | bytes 491552 | tf_op jit(solution)/shard_map/ppermute | solution.py:300
  128.2 1.1 join.1
  129.3 3.9 %all-to-all-start.1 = ((bf16[8,80,768]{2,1,0:T(8,128)(2,1)}), bf16[8,80,768]{2,1,0:T(8,128)(2,1)S(1)}, u32[]{:S(2)}, u32[]{:S(2)}) async-start(bf16[8,80,768]{2,1,0:T(8,128)(2,1)} %join.1), calls=%async_computation.1 | async-start | bytes 1966080 | tf_op jit(solution)/shard_map/all_to_all | solution.py:302
  133.4 0.2 mixing.1.mix_ref
  133.7 19.1 %all-to-all-done.1 = bf16[8,80,768]{2,1,0:T(8,128)(2,1)S(1)} async-done(((bf16[8,80,768]{2,1,0:T(8,128)(2,1)}), bf16[8,80,768]{2,1,0:T(8,128)(2,1)S(1)}, u32[]{:S(2)}, u32[]{:S(2)}) %all-to-all-start.1) | async-done | bytes 983072 | tf_op jit(solution)/shard_map/all_to_all | solution.py:302
  152.8 0.4 combine.1
  153.2 22.9 %all_to_all.16 = bf16[8,32,384]{2,1,0:T(8,128)(2,1)S(1)} all-to-all(bf16[8,32,384]{2,1,0:T(8,128)(2,1)S(1)} %combine.1), channel_id=1, replica_groups=mesh['rep'=2,'x'=8,'core'=2,'pair'=8,'odd'=2] {'pair'}, dimensions={0} | all-to-all | bytes 393216 | tf_op jit(solution)/shard_map/all_to_all | solution.py:306
  176.0 0.6 reduce_sum.12
  (19 shorter events, 0.3 us)
Async XLA Ops:
  1.7 103.9 %collective-permute-start = (bf16[6144,128]{1,0:T(8,128)(2,1)}, bf16[6144,128]{1,0:T(8,128)(2,1)S(1)}, u32[]{:S(2)}, u32[]{:S(2)}) collective-permute-start(bf16[6144,128]{1,0:T(8,128)(2,1)} %param.9), channel_id=1, source_target_pairs={{0,16},{16,0},{1,17},{17,1},{2,18},{18,2},{3,19},{19,3},{4,20},{20... | collective-permute-start | bytes 4718600 | tf_op jit(solution)/shard_map/ppermute | solution.py:290
  3.6 101.9 %collective-permute-start.1 = (bf16[6144,128]{1,0:T(8,128)(2,1)}, bf16[6144,128]{1,0:T(8,128)(2,1)S(1)}, u32[]{:S(2)}, u32[]{:S(2)}) collective-permute-start(bf16[6144,128]{1,0:T(8,128)(2,1)} %param.10), channel_id=1, source_target_pairs={{0,16},{16,0},{1,17},{17,1},{2,18},{18,2},{3,19},{19,3},{4,20},{20... | collective-permute-start | bytes 4718600 | tf_op jit(solution)/shard_map/ppermute | solution.py:291
  6.1 105.8 %collective-permute-start.4 = (bf16[128,6144]{1,0:T(8,128)(2,1)}, bf16[128,6144]{1,0:T(8,128)(2,1)S(1)}, u32[]{:S(2)}, u32[]{:S(2)}) collective-permute-start(bf16[128,6144]{1,0:T(8,128)(2,1)} %down_ref.1), channel_id=1, source_target_pairs={{0,16},{16,0},{1,17},{17,1},{2,18},{18,2},{3,19},{19,3},{4,20},{20... | collective-permute-start | bytes 4718600 | tf_op jit(solution)/shard_map/ppermute | solution.py:292
  25.4 80.1 %copy-start.2 = (bf16[6144,128]{1,0:T(8,128)(2,1)S(1)}, bf16[6144,128]{1,0:T(8,128)(2,1)}, u32[]{:S(2)}) copy-start(bf16[6144,128]{1,0:T(8,128)(2,1)} %param.10) | copy-start | bytes 4718596
  25.5 80.1 %copy-start.1 = (bf16[6144,128]{1,0:T(8,128)(2,1)S(1)}, bf16[6144,128]{1,0:T(8,128)(2,1)}, u32[]{:S(2)}) copy-start(bf16[6144,128]{1,0:T(8,128)(2,1)} %param.9) | copy-start | bytes 4718596
  94.3 16.1 %collective-permute-start.2 = (bf16[4,160,384]{2,1,0:T(8,128)(2,1)S(1)}, bf16[4,160,384]{2,1,0:T(8,128)(2,1)S(1)}, u32[]{:S(2)}, u32[]{:S(2)}) collective-permute-start(bf16[4,160,384]{2,1,0:T(8,128)(2,1)S(1)} %bitcast.21), channel_id=1, source_target_pairs={{0,1},{1,2},{2,3},{3,4},{4,5},{5,6},{6,7},{7,8},{8,9},{9,10},{10,1... | collective-permute-start | bytes 1474568 | tf_op jit(solution)/shard_map/ppermute | solution.py:294
  100.5 11.4 %collective-permute-start.3 = (bf16[4,160,384]{2,1,0:T(8,128)(2,1)S(1)}, bf16[4,160,384]{2,1,0:T(8,128)(2,1)S(1)}, u32[]{:S(2)}, u32[]{:S(2)}) collective-permute-start(bf16[4,160,384]{2,1,0:T(8,128)(2,1)S(1)} %bitcast.20), channel_id=1, source_target_pairs={{1,0},{2,1},{3,2},{4,3},{5,4},{6,5},{7,6},{8,7},{9,8},{10,9},{11,1... | collective-permute-start | bytes 1474568 | tf_op jit(solution)/shard_map/ppermute | solution.py:295
  105.6 6.3 %copy-start = (bf16[128,6144]{1,0:T(8,128)(2,1)S(1)}, bf16[128,6144]{1,0:T(8,128)(2,1)}, u32[]{:S(2)}) copy-start(bf16[128,6144]{1,0:T(8,128)(2,1)} %down_ref.1) | copy-start | bytes 4718596
  112.9 12.4 %collective-permute-start.5 = (bf16[4,160,384]{2,1,0:T(8,128)(2,1)S(1)}, bf16[4,160,384]{2,1,0:T(8,128)(2,1)S(1)}, u32[]{:S(2)}, u32[]{:S(2)}) collective-permute-start(bf16[4,160,384]{2,1,0:T(8,128)(2,1)S(1)} %get-tuple-element.17), channel_id=1, source_target_pairs={{0,1},{1,2},{2,3},{3,4},{4,5},{5,6},{6,7},{7,8},{8,9},{9,10},{10,1... | collective-permute-start | bytes 1474568 | tf_op jit(solution)/shard_map/ppermute | solution.py:299
  117.1 11.1 %collective-permute-start.6 = (bf16[4,160,384]{2,1,0:T(8,128)(2,1)S(1)}, bf16[4,160,384]{2,1,0:T(8,128)(2,1)S(1)}, u32[]{:S(2)}, u32[]{:S(2)}) collective-permute-start(bf16[4,160,384]{2,1,0:T(8,128)(2,1)S(1)} %get-tuple-element.18), channel_id=1, source_target_pairs={{1,0},{2,1},{3,2},{4,3},{5,4},{6,5},{7,6},{8,7},{9,8},{10,9},{11,1... | collective-permute-start | bytes 1474568 | tf_op jit(solution)/shard_map/ppermute | solution.py:300
  129.3 3.9 %copy-start.3 = (s32[32,2]{0,1:T(2,128)S(1)}, s32[32,2]{0,1:T(2,128)}, u32[]{:S(2)}) copy-start(s32[32,2]{0,1:T(2,128)} %param.7) | copy-start | bytes 772
  129.3 4.0 %copy-start.4 = (f32[32,2]{0,1:T(2,128)S(1)}, f32[32,2]{0,1:T(2,128)}, u32[]{:S(2)}) copy-start(f32[32,2]{0,1:T(2,128)} %param.8) | copy-start | bytes 772
  129.3 23.5 %all-to-all-start.1 = ((bf16[8,80,768]{2,1,0:T(8,128)(2,1)}), bf16[8,80,768]{2,1,0:T(8,128)(2,1)S(1)}, u32[]{:S(2)}, u32[]{:S(2)}) async-start(bf16[8,80,768]{2,1,0:T(8,128)(2,1)} %join.1), calls=%async_computation.1 | async-start | bytes 1966080 | tf_op jit(solution)/shard_map/all_to_all | solution.py:302

commit v6 on v5

v6 whole, which is shorter than its diff:
```python
import functools

import jax
import jax.numpy as jnp
from jax import lax
from jax.experimental import pallas as pl
from jax.experimental.pallas import tpu as pltpu
from jax.sharding import Mesh, PartitionSpec as P


EXPERTS = 4
CAP = 20
MAIN = 16
TAIL = CAP - MAIN
QUARTERS = 4
CLASSES = 4
CORES = 2


def cost(flops, nbytes):
    return pl.CostEstimate(flops=flops, bytes_accessed=nbytes, transcendentals=0)


def count_at_least(index, width, parts):
    total = jnp.zeros_like(index)
    for k in range(1, parts):
        total = total + (index >= k * width).astype(jnp.int32)
    return total


def placed(ids, expert, slot, before):
    chosen = ((ids[0:1, :] == expert) | (ids[1:2, :] == expert)).astype(jnp.float32)
    position = jnp.dot(chosen, before, preferred_element_type=jnp.float32)
    return chosen * (position == slot.astype(jnp.float32)).astype(jnp.float32)


def grouped(row, groups):
    later = row >= groups * MAIN
    rest = row - groups * MAIN
    main = count_at_least(row, MAIN, groups)
    tail = count_at_least(rest, TAIL, groups)
    group = jnp.where(later, tail, main)
    slot = jnp.where(later, MAIN + rest - TAIL * tail, row - MAIN * main)
    return group, slot


def dispatch_kernel(chips, ids_ref, tokens_ref, out_ref):
    blocks, count, _ = tokens_ref.shape
    per_expert = chips // EXPERTS
    row = lax.broadcasted_iota(jnp.int32, (EXPERTS * CAP, count), 0)
    expert, slot = grouped(row, EXPERTS)
    first = lax.broadcasted_iota(jnp.int32, (count, count), 0)
    second = lax.broadcasted_iota(jnp.int32, (count, count), 1)
    before = (first < second).astype(jnp.float32)
    placement = placed(ids_ref[...], expert, slot, before).astype(jnp.bfloat16)
    for q in range(blocks):
        slots = jnp.dot(placement, tokens_ref[q], preferred_element_type=jnp.float32).astype(
            jnp.bfloat16
        )
        for chip in range(chips):
            e = chip // per_expert
            out_ref[chip, q * MAIN : (q + 1) * MAIN] = slots[e * MAIN : (e + 1) * MAIN]
            to, at = QUARTERS * MAIN + q * TAIL, EXPERTS * MAIN + e * TAIL
            out_ref[chip, to : to + TAIL] = slots[at : at + TAIL]


def dispatch(ids, tokens, chips):
    blocks, count, depth = tokens.shape
    return pl.pallas_call(
        functools.partial(dispatch_kernel, chips),
        out_shape=jax.ShapeDtypeStruct((chips, blocks * CAP, depth), jnp.bfloat16),
        cost_estimate=cost(2 * EXPERTS * CAP * count * blocks * depth, 700000),
        compiler_params=pltpu.CompilerParams(vmem_limit_bytes=60 << 20),
        name="dispatch",
    )(ids, tokens)


def unpack_kernel(in_ref, out_ref, low_ref, high_ref):
    chips = in_ref.shape[0]
    for q in range(QUARTERS):
        at = QUARTERS * MAIN + q * TAIL
        rows = jnp.concatenate(
            [in_ref[chip, q * MAIN : (q + 1) * MAIN] for chip in range(chips)]
            + [in_ref[chip, at : at + TAIL] for chip in range(chips)],
            axis=0,
        )
        out_ref[q] = rows
        half_ref = low_ref if q < QUARTERS // 2 else high_ref
        half_ref[q % (QUARTERS // 2)] = rows


def unpack(slots):
    chips, _, depth = slots.shape
    half = jax.ShapeDtypeStruct((QUARTERS // 2, chips * CAP, depth), jnp.bfloat16)
    return pl.pallas_call(
        unpack_kernel,
        out_shape=(jax.ShapeDtypeStruct((QUARTERS, chips * CAP, depth), jnp.bfloat16), half, half),
        cost_estimate=cost(1000, 1500000),
        compiler_params=pltpu.CompilerParams(vmem_limit_bytes=8 << 20),
        name="unpack",
    )(slots)


def mixing_kernel(chips, count, ids_ref, logits_ref, out_ref):
    lanes = ids_ref.shape[1]
    rows = chips * QUARTERS * CAP
    row = lax.broadcasted_iota(jnp.int32, (rows, lanes), 0)
    chip = count_at_least(row, QUARTERS * CAP, chips)
    quarter, slot = grouped(row - QUARTERS * CAP * chip, QUARTERS)
    expert = count_at_least(chip, chips // EXPERTS, EXPERTS)
    lane = lax.broadcasted_iota(jnp.int32, (rows, lanes), 1)
    own = (count_at_least(lane, count, QUARTERS) == quarter).astype(jnp.float32)
    first = lax.broadcasted_iota(jnp.int32, (lanes, lanes), 0)
    second = lax.broadcasted_iota(jnp.int32, (lanes, lanes), 1)
    same = count_at_least(first, count, QUARTERS) == count_at_least(second, count, QUARTERS)
    before = ((first < second) & same).astype(jnp.float32)
    ids = ids_ref[...]
    diff = logits_ref[0:1, :] - logits_ref[1:2, :]
    share = jnp.where(ids[0:1, :] == expert, jax.nn.sigmoid(diff), jax.nn.sigmoid(-diff))
    out_ref[...] = (placed(ids, expert, slot, before) * share * own).astype(jnp.bfloat16)


def mixing(ids, logits, chips):
    count = ids.shape[1]
    rows = chips * QUARTERS * CAP
    return pl.pallas_call(
        functools.partial(mixing_kernel, chips, count),
        out_shape=jax.ShapeDtypeStruct((rows, QUARTERS * count), jnp.bfloat16),
        cost_estimate=cost(2 * rows * 128 * 128, 200000),
        compiler_params=pltpu.CompilerParams(vmem_limit_bytes=8 << 20),
        name="mixing",
    )(jnp.tile(ids, (1, QUARTERS)), jnp.tile(logits, (1, QUARTERS)))


def class_at(distance):
    return lax.rem(lax.axis_index("class") + CLASSES + distance, CLASSES)


def side_by_side(refs, q, kind):
    return jnp.concatenate([ref[q, kind] for ref in refs], axis=1)


def multiply(total, tokens, refs, kind, start):
    for b in range(0, tokens.shape[0], 2):
        rows = jnp.concatenate([tokens[b], tokens[b + 1]], axis=1)
        weight = jnp.concatenate(
            [side_by_side(refs, start + b, kind), side_by_side(refs, start + b + 1, kind)], axis=0
        )
        added = jnp.dot(rows, weight, preferred_element_type=jnp.float32)
        total = added if total is None else total + added
    return total


def own_kernel(slots_ref, gate_ref, gate2_ref, up_ref, up2_ref, out_ref):
    refs = (gate_ref, gate2_ref, up_ref, up2_ref)
    out_ref[...] = multiply(None, slots_ref, refs, class_at(0), 0)


def own_part(slots, *weights):
    blocks, rows, depth = slots.shape
    width = weights[0].shape[-1]
    return pl.pallas_call(
        own_kernel,
        out_shape=jax.ShapeDtypeStruct((rows, 4 * width), jnp.float32),
        cost_estimate=cost(2 * blocks * rows * depth * 4 * width, 2200000),
        compiler_params=pltpu.CompilerParams(vmem_limit_bytes=16 << 20),
        name="own_part",
    )(slots, *weights)


def down_pair(hidden, refs, q, kind, depth):
    def block(q):
        lanes = pl.ds(pl.multiple_of((CLASSES * q + kind) * depth, 128), depth)
        return jnp.concatenate([ref[:, lanes] for ref in refs], axis=0)

    weight = jnp.concatenate([block(q), block(q + 1)], axis=1)
    return jnp.dot(hidden, weight, preferred_element_type=jnp.float32)


def ffn_kernel(
    total_ref, left_ref, right_ref, left2_ref, right2_ref, gate_ref, gate2_ref, up_ref, up2_ref, down_ref, down2_ref, hidden_ref, to_right_ref, to_left_ref, to_right2_ref, to_left2_ref
):
    depth = left_ref.shape[2]
    width = gate_ref.shape[-1]
    half = QUARTERS // 2
    refs = (gate_ref, gate2_ref, up_ref, up2_ref)
    total = multiply(total_ref[...], left_ref, refs, class_at(-1), 0)
    total = multiply(total, right_ref, refs, class_at(1), 0)
    total = multiply(total, left2_ref, refs, class_at(2), 0)
    total = multiply(total, right2_ref, refs, class_at(2), half)
    gate = total[:, : 2 * width]
    hidden = (gate * jax.nn.sigmoid(gate) * total[:, 2 * width :]).astype(jnp.bfloat16)
    hidden_ref[...] = hidden
    downs = (down_ref, down2_ref)
    for out_ref, distance, start in (
        (to_right_ref, 1, 0),
        (to_left_ref, -1, 0),
        (to_right2_ref, 2, 0),
        (to_left2_ref, 2, half),
    ):
        for b in range(0, out_ref.shape[0], 2):
            partial = down_pair(hidden, downs, start + b, class_at(distance), depth)
            partial = partial.astype(jnp.bfloat16)
            out_ref[b] = partial[:, :depth]
            out_ref[b + 1] = partial[:, depth:]


def ffn(total, left, right, left2, right2, *weights):
    rows = left.shape[1]
    width, model = weights[-1].shape
    sent = jax.ShapeDtypeStruct(left.shape, jnp.bfloat16)
    half = jax.ShapeDtypeStruct(left2.shape, jnp.bfloat16)
    return pl.pallas_call(
        ffn_kernel,
        out_shape=(
            jax.ShapeDtypeStruct((rows, 2 * width), jnp.bfloat16),
            sent,
            sent,
            half,
            half,
        ),
        cost_estimate=cost(2 * rows * model * width * 4, 9000000),
        compiler_params=pltpu.CompilerParams(vmem_limit_bytes=20 << 20),
        name="ffn",
    )(total, left, right, left2, right2, *weights)


def own_down_kernel(hidden_ref, down_ref, down2_ref, out_ref):
    blocks, _, depth = out_ref.shape
    for b in range(0, blocks, 2):
        partial = down_pair(hidden_ref[...], (down_ref, down2_ref), b, class_at(0), depth)
        out_ref[b] = partial[:, :depth]
        out_ref[b + 1] = partial[:, depth:]


def own_down(hidden, down, down2):
    rows = hidden.shape[0]
    width, model = down.shape
    depth = model // (CLASSES * QUARTERS)
    return pl.pallas_call(
        own_down_kernel,
        out_shape=jax.ShapeDtypeStruct((QUARTERS, rows, depth), jnp.float32),
        cost_estimate=cost(rows * model * width, 4000000),
        compiler_params=pltpu.CompilerParams(vmem_limit_bytes=16 << 20),
        name="own_down",
    )(hidden, down, down2)


def join_kernel(own_ref, left_ref, right_ref, left2_ref, right2_ref, out_ref):
    blocks = own_ref.shape[0]
    chips = out_ref.shape[0]
    half = blocks // 2
    for q in range(blocks):
        both = own_ref[q] + left_ref[q].astype(jnp.float32) + right_ref[q].astype(jnp.float32)
        third = left2_ref[q] if q < half else right2_ref[q - half]
        both = (both + third.astype(jnp.float32)).astype(jnp.bfloat16)
        at = QUARTERS * MAIN + q * TAIL
        for chip in range(chips):
            tail = chips * MAIN + chip * TAIL
            out_ref[chip, q * MAIN : (q + 1) * MAIN] = both[chip * MAIN : (chip + 1) * MAIN]
            out_ref[chip, at : at + TAIL] = both[tail : tail + TAIL]


def join(own, left, right, left2, right2, chips):
    blocks, rows, depth = own.shape
    return pl.pallas_call(
        join_kernel,
        out_shape=jax.ShapeDtypeStruct((chips, blocks * CAP, depth), jnp.bfloat16),
        cost_estimate=cost(blocks * rows * depth, 12 * blocks * rows * depth),
        compiler_params=pltpu.CompilerParams(vmem_limit_bytes=16 << 20),
        name="join",
    )(own, left, right, left2, right2)


def combine_kernel(mix_ref, back_ref, out_ref):
    blocks, count, depth = out_ref.shape
    per_quarter = blocks // QUARTERS
    summed = lax.dot_general(
        mix_ref[...], back_ref[...], (((0,), (0,)), ((), ())), preferred_element_type=jnp.float32
    ).astype(jnp.bfloat16)
    for q in range(QUARTERS):
        for s in range(per_quarter):
            out_ref[q * per_quarter + s] = summed[
                q * count : (q + 1) * count, s * depth : (s + 1) * depth
            ]


def combine(mix, back, count, blocks):
    rows, quarter = back.shape
    depth = QUARTERS * quarter // blocks
    return pl.pallas_call(
        combine_kernel,
        out_shape=jax.ShapeDtypeStruct((blocks, count, depth), jnp.bfloat16),
        cost_estimate=cost(2 * rows * quarter * 128, 2400000),
        compiler_params=pltpu.CompilerParams(vmem_limit_bytes=12 << 20),
        name="combine",
    )(mix, back)


def on_device(tokens, expert_ids, route_logits, gate_weight, up_weight, down_weight):
    chips = lax.axis_size("x")
    parts = QUARTERS * CLASSES
    count, depth = tokens.shape
    swap = [(0, 1), (1, 0)]
    along = ("quarter", "class")
    ids = expert_ids.T

    def shift(value, distance):
        return lax.ppermute(value, along, [(i, (i + distance) % parts) for i in range(parts)])

    outgoing = dispatch(ids, lax.all_gather(tokens, "quarter"), chips)
    gate, up, down, outgoing = lax.optimization_barrier(
        (gate_weight, up_weight, down_weight, outgoing)
    )
    incoming = lax.all_to_all(outgoing, "x", 0, 0, tiled=True)
    gate2 = lax.ppermute(gate, "core", swap)
    up2 = lax.ppermute(up, "core", swap)
    down2 = lax.ppermute(down, "core", swap)
    own, low, high = unpack(incoming)
    left, right = shift(own, 1), shift(own, -1)
    left2, right2 = shift(low, 2), shift(high, -2)
    blocks = [w.reshape(QUARTERS, CLASSES, depth, w.shape[1]) for w in (gate, gate2, up, up2)]
    total = own_part(own, *blocks)
    hidden, to_right, to_left, to_right2, to_left2 = ffn(
        total, left, right, left2, right2, *blocks, down, down2
    )
    left, right = shift(to_right, 1), shift(to_left, -1)
    left2, right2 = shift(to_right2, 2), shift(to_left2, -2)
    partial_value = join(own_down(hidden, down, down2), left, right, left2, right2, chips)
    returned = lax.all_to_all(partial_value, "x", 0, 0, tiled=True)
    mix = mixing(ids, route_logits.T, chips)
    combined = combine(mix, returned.reshape(chips * QUARTERS * CAP, depth), count, QUARTERS)
    blocks = lax.all_to_all(combined, "quarter", 0, 0, tiled=True)
    return jnp.sum(blocks.astype(jnp.float32), axis=0).astype(jnp.bfloat16)


def solution(mesh):
    sizes = [mesh.shape[axis] for axis in ("rep", "exp", "tp")]
    devices = mesh.devices.reshape(sizes[0], sizes[1] // CORES, CORES, QUARTERS, CLASSES)
    split = Mesh(devices, ("rep", "x", "core", "quarter", "class"))
    tokens = ("rep", "x", "core")
    features = ("quarter", "class")
    hidden = ("x", "core", "quarter", "class")
    return jax.shard_map(
        on_device,
        mesh=split,
        in_specs=(
            P(tokens, features),
            P(tokens, None),
            P(tokens, None),
            P(None, hidden),
            P(None, hidden),
            P(hidden, None),
        ),
        out_specs=P(tokens, features),
        check_vma=False,
    )
```

time: 177 us -> 190 us (1.073)
  starting transfers between devices: 29 us -> 46.1 us
  blocking collectives: 109 us -> 95.3 us
  waiting for transfers between devices: 32 us -> 39.9 us
    all_gather x1, blocking collectives: 68.7 us -> 50.8 us  [on_device(): outgoing = dispatch(ids, lax.all_gather(tokens, 'quarter'), chips)]
    ppermute x4 -> x8, starting transfers between devices: 18.8 us -> 36.1 us  [shift(): lax.ppermute(value, along, [(i, (i + distance) % parts) for i in range(pa...]
    ppermute x4 -> x8, waiting for transfers between devices: 12.8 us -> 25.3 us  [shift(): lax.ppermute(value, along, [(i, (i + distance) % parts) for i in range(pa...]
    all_to_all x1, blocking collectives: 17.4 us -> 24.8 us  [on_device(): incoming = lax.all_to_all(outgoing, 'x', 0, 0, tiled=True)]
    all_to_all x1, waiting for transfers between devices: 19.1 us -> 14.6 us  [on_device(): returned = lax.all_to_all(partial_value, 'x', 0, 0, tiled=True)]
    all_to_all x1, blocking collectives: 22.9 us -> 19.7 us  [on_device(): blocks = lax.all_to_all(combined, 'quarter', 0, 0, tiled=True)]
  transfers between devices with their start and end apart: 8 -> 12, of which waited for: 5 -> 3; matrix products, arithmetic and copies ran while one was open for 0% -> 0% of each run, Pallas kernels for 1% -> 1%
where the time goes in v6:
time: 190 us
  blocking collectives  95.3 us (50%)
  starting transfers between devices  46.1 us (24%)
  waiting for transfers between devices  39.9 us (21%)
  Pallas kernels  5.86 us (3%)
    all_gather x1, blocking collectives, on_device(): outgoing = dispatch(ids, lax.all_gather(tokens, 'quarter'), chips)  50.8 us
    ppermute x8, starting transfers between devices, shift(): lax.ppermute(value, along, [(i, (i + distance) % parts) for i in range(pa...  36.1 us
    ppermute x8, waiting for transfers between devices, shift(): lax.ppermute(value, along, [(i, (i + distance) % parts) for i in range(pa...  25.3 us
    all_to_all x1, blocking collectives, on_device(): incoming = lax.all_to_all(outgoing, 'x', 0, 0, tiled=True)  24.8 us
    all_to_all x1, blocking collectives, on_device(): blocks = lax.all_to_all(combined, 'quarter', 0, 0, tiled=True)  19.7 us
    all_to_all x1, waiting for transfers between devices, on_device(): returned = lax.all_to_all(partial_value, 'x', 0, 0, tiled=True)  14.6 us
  transfers between devices with their start and end apart: 12, of which 3 were waited for; matrix products, arithmetic and copies ran while one was open for 0% of the time, Pallas kernels for 1%

profile of v6, /device:TPU:80, one launch (start us, length us, event | category | flops | bytes accessed | tf_op | source)
XLA Modules:
  0.0 189.6 jit_solution(17805883563419262765)
XLA Ops:
  0.0 50.8 %all-gather = bf16[128,384]{1,0:T(8,128)(2,1)} all-gather(bf16[32,384]{1,0:T(8,128)(2,1)} %param.6), channel_id=2, replica_groups=mesh['rep'=2,'x'=8,'core'=2,'quarter'=4,'class'=4] {'quarter'}, dimensions={0}, use_global_device_ids=true | all-gather | bytes 122880 | tf_op jit(solution)/shard_map/all_gather | solution.py:311
  50.8 2.0 %dispatch.1 = bf16[8,80,384]{2,1,0:T(8,128)(2,1)} custom-call(s32[2,32]{1,0:T(2,128)} %bitcast.18, bf16[4,32,384]{2,1,0:T(8,128)(2,1)} %bitcast.17), custom_call_target="tpu_custom_call" | custom-call | flops 7864320 | bytes 700000 | tf_op jit(solution)/shard_map/dispatch/pallas_call | solution.py:69
  52.8 1.9 %collective-permute-start = (bf16[6144,128]{1,0:T(8,128)(2,1)}, bf16[6144,128]{1,0:T(8,128)(2,1)S(1)}, u32[]{:S(2)}, u32[]{:S(2)}) collective-permute-start(bf16[6144,128]{1,0:T(8,128)(2,1)} %param.9), channel_id=1, source_target_pairs={{0,16},{16,0},{1,17},{17,1},{2,18},{18,2},{3,19},{19,3},{4,20},{20... | collective-permute-start | bytes 4718600 | tf_op jit(solution)/shard_map/ppermute | solution.py:316
  54.8 2.4 %collective-permute-start.1 = (bf16[6144,128]{1,0:T(8,128)(2,1)}, bf16[6144,128]{1,0:T(8,128)(2,1)S(1)}, u32[]{:S(2)}, u32[]{:S(2)}) collective-permute-start(bf16[6144,128]{1,0:T(8,128)(2,1)} %param.10), channel_id=1, source_target_pairs={{0,16},{16,0},{1,17},{17,1},{2,18},{18,2},{3,19},{19,3},{4,20},{20... | collective-permute-start | bytes 4718600 | tf_op jit(solution)/shard_map/ppermute | solution.py:317
  57.2 2.0 %collective-permute-start.6 = (bf16[128,6144]{1,0:T(8,128)(2,1)}, bf16[128,6144]{1,0:T(8,128)(2,1)S(1)}, u32[]{:S(2)}, u32[]{:S(2)}) collective-permute-start(bf16[128,6144]{1,0:T(8,128)(2,1)} %down_ref.1), channel_id=1, source_target_pairs={{0,16},{16,0},{1,17},{17,1},{2,18},{18,2},{3,19},{19,3},{4,20},{20... | collective-permute-start | bytes 4718600 | tf_op jit(solution)/shard_map/ppermute | solution.py:318
  59.2 24.8 %all_to_all.15.in_ref = bf16[8,80,384]{2,1,0:T(8,128)(2,1)S(1)} all-to-all(bf16[8,80,384]{2,1,0:T(8,128)(2,1)} %dispatch.1), channel_id=1, replica_groups=mesh['rep'=2,'x'=8,'core'=2,'quarter'=4,'class'=4] {'x'}, dimensions={0} | all-to-all | bytes 983040 | tf_op jit(solution)/shard_map/all_to_all | solution.py:315
  84.0 5.1 %collective-permute-start.2 = (bf16[4,160,384]{2,1,0:T(8,128)(2,1)S(1)}, bf16[4,160,384]{2,1,0:T(8,128)(2,1)S(1)}, u32[]{:S(2)}, u32[]{:S(2)}) collective-permute-start(bf16[4,160,384]{2,1,0:T(8,128)(2,1)S(1)} %get-tuple-element.18.slots_ref), channel_id=1, source_target_pairs={{0,1},{1,2},{2,3},{3,4},{4,5},{5,6},{6,7},{7,8},{8,9},{9,10},{10,1... | collective-permute-start | bytes 1474568 | tf_op jit(solution)/shard_map/ppermute | solution.py:309
  89.2 8.5 %collective-permute-start.3 = (bf16[4,160,384]{2,1,0:T(8,128)(2,1)S(1)}, bf16[4,160,384]{2,1,0:T(8,128)(2,1)S(1)}, u32[]{:S(2)}, u32[]{:S(2)}) collective-permute-start(bf16[4,160,384]{2,1,0:T(8,128)(2,1)S(1)} %get-tuple-element.18.slots_ref), channel_id=1, source_target_pairs={{0,15},{1,0},{2,1},{3,2},{4,3},{5,4},{6,5},{7,6},{8,7},{9,8},{10,9... | collective-permute-start | bytes 1474568 | tf_op jit(solution)/shard_map/ppermute | solution.py:309
  97.8 2.0 %collective-permute-start.4 = (bf16[2,160,384]{2,1,0:T(8,128)(2,1)S(1)}, bf16[2,160,384]{2,1,0:T(8,128)(2,1)S(1)}, u32[]{:S(2)}, u32[]{:S(2)}) collective-permute-start(bf16[2,160,384]{2,1,0:T(8,128)(2,1)S(1)} %get-tuple-element.21), channel_id=1, source_target_pairs={{0,2},{1,3},{2,4},{3,5},{4,6},{5,7},{6,8},{7,9},{8,10},{9,11},{10,... | collective-permute-start | bytes 737288 | tf_op jit(solution)/shard_map/ppermute | solution.py:309
  99.7 6.1 %collective-permute-start.5 = (bf16[2,160,384]{2,1,0:T(8,128)(2,1)S(1)}, bf16[2,160,384]{2,1,0:T(8,128)(2,1)S(1)}, u32[]{:S(2)}, u32[]{:S(2)}) collective-permute-start(bf16[2,160,384]{2,1,0:T(8,128)(2,1)S(1)} %get-tuple-element.22), channel_id=1, source_target_pairs={{0,14},{1,15},{2,0},{3,1},{4,2},{5,3},{6,4},{7,5},{8,6},{9,7},{10,... | collective-permute-start | bytes 737288 | tf_op jit(solution)/shard_map/ppermute | solution.py:309
  105.8 1.4 copy-done.1
  107.2 0.4 own_part.1.total_ref
  107.6 11.3 %collective-permute-done.4.left2_ref = bf16[2,160,384]{2,1,0:T(8,128)(2,1)S(1)} collective-permute-done((bf16[2,160,384]{2,1,0:T(8,128)(2,1)S(1)}, bf16[2,160,384]{2,1,0:T(8,128)(2,1)S(1)}, u32[]{:S(2)}, u32[]{:S(2)}) %collective-permute-start.4) | collective-permute-done | bytes 245792 | tf_op jit(solution)/shard_map/ppermute | solution.py:309
  119.0 1.5 ffn.1
  120.4 2.0 %collective-permute-start.7 = (bf16[4,160,384]{2,1,0:T(8,128)(2,1)S(1)}, bf16[4,160,384]{2,1,0:T(8,128)(2,1)S(1)}, u32[]{:S(2)}, u32[]{:S(2)}) collective-permute-start(bf16[4,160,384]{2,1,0:T(8,128)(2,1)S(1)} %get-tuple-element.25), channel_id=1, source_target_pairs={{0,1},{1,2},{2,3},{3,4},{4,5},{5,6},{6,7},{7,8},{8,9},{9,10},{10,1... | collective-permute-start | bytes 1474568 | tf_op jit(solution)/shard_map/ppermute | solution.py:309
  122.4 5.2 %collective-permute-start.8 = (bf16[4,160,384]{2,1,0:T(8,128)(2,1)S(1)}, bf16[4,160,384]{2,1,0:T(8,128)(2,1)S(1)}, u32[]{:S(2)}, u32[]{:S(2)}) collective-permute-start(bf16[4,160,384]{2,1,0:T(8,128)(2,1)S(1)} %get-tuple-element.26), channel_id=1, source_target_pairs={{0,15},{1,0},{2,1},{3,2},{4,3},{5,4},{6,5},{7,6},{8,7},{9,8},{10,9... | collective-permute-start | bytes 1474568 | tf_op jit(solution)/shard_map/ppermute | solution.py:309
  127.6 5.3 %collective-permute-start.10 = (bf16[2,160,384]{2,1,0:T(8,128)(2,1)S(1)}, bf16[2,160,384]{2,1,0:T(8,128)(2,1)S(1)}, u32[]{:S(2)}, u32[]{:S(2)}) collective-permute-start(bf16[2,160,384]{2,1,0:T(8,128)(2,1)S(1)} %get-tuple-element.28), channel_id=1, source_target_pairs={{0,14},{1,15},{2,0},{3,1},{4,2},{5,3},{6,4},{7,5},{8,6},{9,7},{10,... | collective-permute-start | bytes 737288 | tf_op jit(solution)/shard_map/ppermute | solution.py:309
  132.9 2.0 %collective-permute-start.9 = (bf16[2,160,384]{2,1,0:T(8,128)(2,1)S(1)}, bf16[2,160,384]{2,1,0:T(8,128)(2,1)S(1)}, u32[]{:S(2)}, u32[]{:S(2)}) collective-permute-start(bf16[2,160,384]{2,1,0:T(8,128)(2,1)S(1)} %get-tuple-element.27), channel_id=1, source_target_pairs={{0,2},{1,3},{2,4},{3,5},{4,6},{5,7},{6,8},{7,9},{8,10},{9,11},{10,... | collective-permute-start | bytes 737288 | tf_op jit(solution)/shard_map/ppermute | solution.py:309
  135.2 14.0 %collective-permute-done.10.right2_ref = bf16[2,160,384]{2,1,0:T(8,128)(2,1)S(1)} collective-permute-done((bf16[2,160,384]{2,1,0:T(8,128)(2,1)S(1)}, bf16[2,160,384]{2,1,0:T(8,128)(2,1)S(1)}, u32[]{:S(2)}, u32[]{:S(2)}) %collective-permute-start.10) | collective-permute-done | bytes 245792 | tf_op jit(solution)/shard_map/ppermute | solution.py:309
  149.2 1.0 join.1
  150.2 3.7 %all-to-all-start.1 = ((bf16[8,80,384]{2,1,0:T(8,128)(2,1)}), bf16[8,80,384]{2,1,0:T(8,128)(2,1)S(1)}, u32[]{:S(2)}, u32[]{:S(2)}) async-start(bf16[8,80,384]{2,1,0:T(8,128)(2,1)} %join.1), calls=%async_computation.1 | async-start | bytes 983040 | tf_op jit(solution)/shard_map/all_to_all | solution.py:330
  154.3 14.6 %all-to-all-done.1 = bf16[8,80,384]{2,1,0:T(8,128)(2,1)S(1)} async-done(((bf16[8,80,384]{2,1,0:T(8,128)(2,1)}), bf16[8,80,384]{2,1,0:T(8,128)(2,1)S(1)}, u32[]{:S(2)}, u32[]{:S(2)}) %all-to-all-start.1) | async-done | bytes 491552 | tf_op jit(solution)/shard_map/all_to_all | solution.py:330
  169.2 19.7 %all_to_all.16 = bf16[4,32,384]{2,1,0:T(8,128)(2,1)S(1)} all-to-all(bf16[4,32,384]{2,1,0:T(8,128)(2,1)S(1)} %combine.1), channel_id=1, replica_groups=mesh['rep'=2,'x'=8,'core'=2,'quarter'=4,'class'=4] {'quarter'}, dimensions={0} | all-to-all | bytes 196608 | tf_op jit(solution)/shard_map/all_to_all | solution.py:333
  189.0 0.6 reduce_sum.12
  (28 shorter events, 1.2 us)
Async XLA Ops:
  0.0 105.8 %copy-start = (bf16[6144,128]{1,0:T(8,128)(2,1)S(1)}, bf16[6144,128]{1,0:T(8,128)(2,1)}, u32[]{:S(2)}) copy-start(bf16[6144,128]{1,0:T(8,128)(2,1)} %param.9) | copy-start | bytes 4718596
  52.8 44.9 %collective-permute-start = (bf16[6144,128]{1,0:T(8,128)(2,1)}, bf16[6144,128]{1,0:T(8,128)(2,1)S(1)}, u32[]{:S(2)}, u32[]{:S(2)}) collective-permute-start(bf16[6144,128]{1,0:T(8,128)(2,1)} %param.9), channel_id=1, source_target_pairs={{0,16},{16,0},{1,17},{17,1},{2,18},{18,2},{3,19},{19,3},{4,20},{20... | collective-permute-start | bytes 4718600 | tf_op jit(solution)/shard_map/ppermute | solution.py:316
  54.8 44.9 %collective-permute-start.1 = (bf16[6144,128]{1,0:T(8,128)(2,1)}, bf16[6144,128]{1,0:T(8,128)(2,1)S(1)}, u32[]{:S(2)}, u32[]{:S(2)}) collective-permute-start(bf16[6144,128]{1,0:T(8,128)(2,1)} %param.10), channel_id=1, source_target_pairs={{0,16},{16,0},{1,17},{17,1},{2,18},{18,2},{3,19},{19,3},{4,20},{20... | collective-permute-start | bytes 4718600 | tf_op jit(solution)/shard_map/ppermute | solution.py:317
  57.2 61.7 %collective-permute-start.6 = (bf16[128,6144]{1,0:T(8,128)(2,1)}, bf16[128,6144]{1,0:T(8,128)(2,1)S(1)}, u32[]{:S(2)}, u32[]{:S(2)}) collective-permute-start(bf16[128,6144]{1,0:T(8,128)(2,1)} %down_ref.1), channel_id=1, source_target_pairs={{0,16},{16,0},{1,17},{17,1},{2,18},{18,2},{3,19},{19,3},{4,20},{20... | collective-permute-start | bytes 4718600 | tf_op jit(solution)/shard_map/ppermute | solution.py:318
  84.0 34.9 %collective-permute-start.2 = (bf16[4,160,384]{2,1,0:T(8,128)(2,1)S(1)}, bf16[4,160,384]{2,1,0:T(8,128)(2,1)S(1)}, u32[]{:S(2)}, u32[]{:S(2)}) collective-permute-start(bf16[4,160,384]{2,1,0:T(8,128)(2,1)S(1)} %get-tuple-element.18.slots_ref), channel_id=1, source_target_pairs={{0,1},{1,2},{2,3},{3,4},{4,5},{5,6},{6,7},{7,8},{8,9},{9,10},{10,1... | collective-permute-start | bytes 1474568 | tf_op jit(solution)/shard_map/ppermute | solution.py:309
  89.2 29.8 %collective-permute-start.3 = (bf16[4,160,384]{2,1,0:T(8,128)(2,1)S(1)}, bf16[4,160,384]{2,1,0:T(8,128)(2,1)S(1)}, u32[]{:S(2)}, u32[]{:S(2)}) collective-permute-start(bf16[4,160,384]{2,1,0:T(8,128)(2,1)S(1)} %get-tuple-element.18.slots_ref), channel_id=1, source_target_pairs={{0,15},{1,0},{2,1},{3,2},{4,3},{5,4},{6,5},{7,6},{8,7},{9,8},{10,9... | collective-permute-start | bytes 1474568 | tf_op jit(solution)/shard_map/ppermute | solution.py:309
  97.8 21.1 %collective-permute-start.4 = (bf16[2,160,384]{2,1,0:T(8,128)(2,1)S(1)}, bf16[2,160,384]{2,1,0:T(8,128)(2,1)S(1)}, u32[]{:S(2)}, u32[]{:S(2)}) collective-permute-start(bf16[2,160,384]{2,1,0:T(8,128)(2,1)S(1)} %get-tuple-element.21), channel_id=1, source_target_pairs={{0,2},{1,3},{2,4},{3,5},{4,6},{5,7},{6,8},{7,9},{8,10},{9,11},{10,... | collective-permute-start | bytes 737288 | tf_op jit(solution)/shard_map/ppermute | solution.py:309
  99.7 19.2 %collective-permute-start.5 = (bf16[2,160,384]{2,1,0:T(8,128)(2,1)S(1)}, bf16[2,160,384]{2,1,0:T(8,128)(2,1)S(1)}, u32[]{:S(2)}, u32[]{:S(2)}) collective-permute-start(bf16[2,160,384]{2,1,0:T(8,128)(2,1)S(1)} %get-tuple-element.22), channel_id=1, source_target_pairs={{0,14},{1,15},{2,0},{3,1},{4,2},{5,3},{6,4},{7,5},{8,6},{9,7},{10,... | collective-permute-start | bytes 737288 | tf_op jit(solution)/shard_map/ppermute | solution.py:309
  105.8 1.4 copy-start.1
  107.2 11.7 %copy-start.2 = (bf16[6144,128]{1,0:T(8,128)(2,1)S(1)}, bf16[6144,128]{1,0:T(8,128)(2,1)}, u32[]{:S(2)}) copy-start(bf16[6144,128]{1,0:T(8,128)(2,1)} %param.10) | copy-start | bytes 4718596
  107.2 11.8 %copy-start.3 = (bf16[128,6144]{1,0:T(8,128)(2,1)S(1)}, bf16[128,6144]{1,0:T(8,128)(2,1)}, u32[]{:S(2)}) copy-start(bf16[128,6144]{1,0:T(8,128)(2,1)} %down_ref.1) | copy-start | bytes 4718596
  120.4 28.7 %collective-permute-start.7 = (bf16[4,160,384]{2,1,0:T(8,128)(2,1)S(1)}, bf16[4,160,384]{2,1,0:T(8,128)(2,1)S(1)}, u32[]{:S(2)}, u32[]{:S(2)}) collective-permute-start(bf16[4,160,384]{2,1,0:T(8,128)(2,1)S(1)} %get-tuple-element.25), channel_id=1, source_target_pairs={{0,1},{1,2},{2,3},{3,4},{4,5},{5,6},{6,7},{7,8},{8,9},{9,10},{10,1... | collective-permute-start | bytes 1474568 | tf_op jit(solution)/shard_map/ppermute | solution.py:309
  122.4 26.8 %collective-permute-start.8 = (bf16[4,160,384]{2,1,0:T(8,128)(2,1)S(1)}, bf16[4,160,384]{2,1,0:T(8,128)(2,1)S(1)}, u32[]{:S(2)}, u32[]{:S(2)}) collective-permute-start(bf16[4,160,384]{2,1,0:T(8,128)(2,1)S(1)} %get-tuple-element.26), channel_id=1, source_target_pairs={{0,15},{1,0},{2,1},{3,2},{4,3},{5,4},{6,5},{7,6},{8,7},{9,8},{10,9... | collective-permute-start | bytes 1474568 | tf_op jit(solution)/shard_map/ppermute | solution.py:309
  127.6 21.6 %collective-permute-start.10 = (bf16[2,160,384]{2,1,0:T(8,128)(2,1)S(1)}, bf16[2,160,384]{2,1,0:T(8,128)(2,1)S(1)}, u32[]{:S(2)}, u32[]{:S(2)}) collective-permute-start(bf16[2,160,384]{2,1,0:T(8,128)(2,1)S(1)} %get-tuple-element.28), channel_id=1, source_target_pairs={{0,14},{1,15},{2,0},{3,1},{4,2},{5,3},{6,4},{7,5},{8,6},{9,7},{10,... | collective-permute-start | bytes 737288 | tf_op jit(solution)/shard_map/ppermute | solution.py:309
  132.9 16.3 %collective-permute-start.9 = (bf16[2,160,384]{2,1,0:T(8,128)(2,1)S(1)}, bf16[2,160,384]{2,1,0:T(8,128)(2,1)S(1)}, u32[]{:S(2)}, u32[]{:S(2)}) collective-permute-start(bf16[2,160,384]{2,1,0:T(8,128)(2,1)S(1)} %get-tuple-element.27), channel_id=1, source_target_pairs={{0,2},{1,3},{2,4},{3,5},{4,6},{5,7},{6,8},{7,9},{8,10},{9,11},{10,... | collective-permute-start | bytes 737288 | tf_op jit(solution)/shard_map/ppermute | solution.py:309
  135.2 18.7 %copy-start.4 = (s32[32,2]{0,1:T(2,128)S(1)}, s32[32,2]{0,1:T(2,128)}, u32[]{:S(2)}) copy-start(s32[32,2]{0,1:T(2,128)} %param.7) | copy-start | bytes 772
  135.2 18.8 %copy-start.5 = (f32[32,2]{0,1:T(2,128)S(1)}, f32[32,2]{0,1:T(2,128)}, u32[]{:S(2)}) copy-start(f32[32,2]{0,1:T(2,128)} %param.8) | copy-start | bytes 772
  150.2 18.7 %all-to-all-start.1 = ((bf16[8,80,384]{2,1,0:T(8,128)(2,1)}), bf16[8,80,384]{2,1,0:T(8,128)(2,1)S(1)}, u32[]{:S(2)}, u32[]{:S(2)}) async-start(bf16[8,80,384]{2,1,0:T(8,128)(2,1)} %join.1), calls=%async_computation.1 | async-start | bytes 983040 | tf_op jit(solution)/shard_map/all_to_all | solution.py:330

commit v7 on v5

--- a/solution.py
+++ b/solution.py
@@ -165,35 +165,38 @@
 
 
 def ffn_kernel(
-    total_ref, left_ref, right_ref, gate_ref, gate2_ref, up_ref, up2_ref, down_ref, down2_ref, hidden_ref, to_right_ref, to_left_ref
+    total_ref, early_ref, late_ref, gate_ref, gate2_ref, up_ref, up2_ref, down_ref, down2_ref, hidden_ref, send_early_ref, send_late_ref
 ):
-    half, _, depth = left_ref.shape
+    half, _, depth = early_ref.shape
     parity = 1 - lax.axis_index("odd")
+    early = half * (1 - lax.axis_index("core"))
+    late = half - early
     width = gate_ref.shape[-1]
     refs = (gate_ref, gate2_ref, up_ref, up2_ref)
-    total = multiply(total_ref[...], left_ref, refs, parity, 0)
-    total = multiply(total, right_ref, refs, parity, half)
+    total = multiply(total_ref[...], early_ref, refs, parity, early)
+    total = multiply(total, late_ref, refs, parity, late)
     gate = total[:, : 2 * width]
     hidden = (gate * jax.nn.sigmoid(gate) * total[:, 2 * width :]).astype(jnp.bfloat16)
     hidden_ref[...] = hidden
-    for b in range(0, 2 * half, 2):
-        partial = down_pair(hidden, (down_ref, down2_ref), b, parity, depth).astype(jnp.bfloat16)
-        out_ref, at = (to_right_ref, b) if b < half else (to_left_ref, b - half)
-        out_ref[at] = partial[:, :depth]
-        out_ref[at + 1] = partial[:, depth:]
-
-
-def ffn(total, left, right, *weights):
-    _, rows, _ = left.shape
+    for out_ref, start in ((send_early_ref, early), (send_late_ref, late)):
+        for b in range(0, half, 2):
+            partial = down_pair(hidden, (down_ref, down2_ref), start + b, parity, depth)
+            partial = partial.astype(jnp.bfloat16)
+            out_ref[b] = partial[:, :depth]
+            out_ref[b + 1] = partial[:, depth:]
+
+
+def ffn(total, early, late, *weights):
+    _, rows, _ = early.shape
     width, model = weights[-1].shape
-    sent = jax.ShapeDtypeStruct(left.shape, jnp.bfloat16)
+    sent = jax.ShapeDtypeStruct(early.shape, jnp.bfloat16)
     return pl.pallas_call(
         ffn_kernel,
         out_shape=(jax.ShapeDtypeStruct((rows, 2 * width), jnp.bfloat16), sent, sent),
         cost_estimate=cost(2 * rows * model * width * 3, 7000000),
         compiler_params=pltpu.CompilerParams(vmem_limit_bytes=20 << 20),
         name="ffn",
-    )(total, left, right, *weights)
+    )(total, early, late, *weights)
 
 
 def own_down_kernel(hidden_ref, down_ref, down2_ref, out_ref):
@@ -218,13 +221,16 @@
     )(hidden, down, down2)
 
 
-def join_kernel(own_ref, left_ref, right_ref, out_ref):
+def join_kernel(own_ref, early_ref, late_ref, out_ref):
     pairs, _, depth = own_ref.shape
     chips = out_ref.shape[0]
     half = pairs // 2
+    upward = lax.axis_index("core") == 1
     per_quarter = pairs // QUARTERS
     for b in range(pairs):
-        other = left_ref[b] if b < half else right_ref[b - half]
+        lower = b < half
+        i = b if lower else b - half
+        other = jnp.where(upward == lower, early_ref[i], late_ref[i])
         both = (own_ref[b] + other.astype(jnp.float32)).astype(jnp.bfloat16)
         q, s = b // per_quarter, b % per_quarter
         at = QUARTERS * MAIN + q * TAIL
@@ -235,7 +241,7 @@
             out_ref[chip, at : at + TAIL, lanes] = both[tail : tail + TAIL]
 
 
-def join(own, left, right, chips):
+def join(own, early, late, chips):
     pairs, rows, depth = own.shape
     out = (chips, QUARTERS * CAP, pairs * depth // QUARTERS)
     return pl.pallas_call(
@@ -244,7 +250,7 @@
         cost_estimate=cost(pairs * rows * depth, 8 * pairs * rows * depth),
         compiler_params=pltpu.CompilerParams(vmem_limit_bytes=16 << 20),
         name="join",
-    )(own, left, right)
+    )(own, early, late)
 
 
 def combine_kernel(mix_ref, back_ref, out_ref):
@@ -278,10 +284,21 @@
     parts = 2 * pairs
     count, depth = tokens.shape
     swap = [(0, 1), (1, 0)]
-    along = ("pair", "odd")
     ids = expert_ids.T
-    up_z = [(i, (i + 1) % parts) for i in range(parts)]
-    down_z = [((i + 1) % parts, i) for i in range(parts)]
+    along = ("core", "pair", "odd")
+    half = pairs // 2
+
+    def exchange(early, late):
+        def shift(value, core_up):
+            steps = [(c, 1 if c == core_up else -1) for c in range(CORES)]
+            return lax.ppermute(
+                value,
+                along,
+                [(c * parts + z, c * parts + (z + to) % parts) for c, to in steps for z in range(parts)],
+            )
+
+        return shift(early, 1), shift(late, 0)
+
     outgoing = dispatch(ids, tokens, chips)
     gate, up, down, outgoing = lax.optimization_barrier(
         (gate_weight, up_weight, down_weight, outgoing)
@@ -291,14 +308,15 @@
     up2 = lax.ppermute(up, "core", swap)
     down2 = lax.ppermute(down, "core", swap)
     own = lax.all_gather(gather_rows(incoming), "pair")
-    left = lax.ppermute(own[: pairs // 2], along, up_z)
-    right = lax.ppermute(own[pairs // 2 :], along, down_z)
+    first = half * (1 - lax.axis_index("core"))
+    early, late = exchange(
+        lax.dynamic_slice_in_dim(own, first, half), lax.dynamic_slice_in_dim(own, half - first, half)
+    )
     blocks = [w.reshape(pairs, 2, depth, w.shape[1]) for w in (gate, gate2, up, up2)]
     total = own_part(own, *blocks)
-    hidden, to_right, to_left = ffn(total, left, right, *blocks, down, down2)
-    from_left = lax.ppermute(to_right, along, up_z)
-    from_right = lax.ppermute(to_left, along, down_z)
-    partial_value = join(own_down(hidden, down, down2, pairs), from_left, from_right, chips)
+    hidden, early, late = ffn(total, early, late, *blocks, down, down2)
+    early, late = exchange(early, late)
+    partial_value = join(own_down(hidden, down, down2, pairs), early, late, chips)
     returned = lax.all_to_all(partial_value, "x", 0, 0, tiled=True)
     mix = mixing(ids, route_logits.T, chips)
     back = returned.reshape(chips * QUARTERS * CAP, pairs * depth // QUARTERS)

time: 177 us -> 189 us (1.068)
  waiting for transfers between devices: 32 us -> 51.5 us
  blocking collectives: 109 us -> 92.3 us
  starting transfers between devices: 29 us -> 34.7 us
  Pallas kernels: 5.59 us -> 8.56 us
    all_to_all x1 -> x0, blocking collectives: 17.4 us -> none  [on_device(): incoming = lax.all_to_all(outgoing, 'x', 0, 0, tiled=True)]
    all_to_all x0 -> x1, waiting for transfers between devices: none -> 10.1 us  [on_device(): incoming = lax.all_to_all(outgoing, 'x', 0, 0, tiled=True)]
    all_to_all x0 -> x1, starting transfers between devices: none -> 7.33 us  [on_device(): incoming = lax.all_to_all(outgoing, 'x', 0, 0, tiled=True)]
    ppermute x4, waiting for transfers between devices: 12.8 us -> 18.2 us  [shift(): lax.ppermute(value, along, [(c * parts + z, c * parts + (z + to) % parts)...]
    all_to_all x1, waiting for transfers between devices: 19.1 us -> 23.2 us  [on_device(): returned = lax.all_to_all(partial_value, 'x', 0, 0, tiled=True)]
  transfers between devices with their start and end apart: 8 -> 9, of which waited for: 5 -> 6; matrix products, arithmetic and copies ran while one was open for 0% -> 0% of each run, Pallas kernels for 1% -> 2%
where the time goes in v7:
time: 189 us; the launch traced here: 188 us
  blocking collectives  92.3 us (49%)
  waiting for transfers between devices  51.5 us (27%)
  starting transfers between devices  34.7 us (18%)
  Pallas kernels  8.56 us (5%)
    all_gather x1, blocking collectives, on_device(): own = lax.all_gather(gather_rows(incoming), 'pair')  68.7 us
    all_to_all x1, blocking collectives, on_device(): blocks = lax.all_to_all(combined, 'pair', 0, 0, tiled=True)  23.6 us
    all_to_all x1, waiting for transfers between devices, on_device(): returned = lax.all_to_all(partial_value, 'x', 0, 0, tiled=True)  23.2 us
    ppermute x4, waiting for transfers between devices, shift(): lax.ppermute(value, along, [(c * parts + z, c * parts + (z + to) % parts)...  18.2 us
    ppermute x4, starting transfers between devices, shift(): lax.ppermute(value, along, [(c * parts + z, c * parts + (z + to) % parts)...  17.1 us
    all_to_all x1, waiting for transfers between devices, on_device(): incoming = lax.all_to_all(outgoing, 'x', 0, 0, tiled=True)  10.1 us
    all_to_all x1, starting transfers between devices, on_device(): incoming = lax.all_to_all(outgoing, 'x', 0, 0, tiled=True)  7.33 us
    all_to_all x1, starting transfers between devices, on_device(): returned = lax.all_to_all(partial_value, 'x', 0, 0, tiled=True)  3.89 us
  transfers between devices with their start and end apart: 9, of which 6 were waited for; matrix products, arithmetic and copies ran while one was open for 0% of the time, Pallas kernels for 2%

profile of v7, /device:TPU:80, one launch (start us, length us, event | category | flops | bytes accessed | tf_op | source)
XLA Modules:
  0.0 188.2 jit_solution(12467739510661178917)
XLA Ops:
  0.0 1.7 dispatch.1
  1.7 1.9 %collective-permute-start = (bf16[6144,128]{1,0:T(8,128)(2,1)}, bf16[6144,128]{1,0:T(8,128)(2,1)S(1)}, u32[]{:S(2)}, u32[]{:S(2)}) collective-permute-start(bf16[6144,128]{1,0:T(8,128)(2,1)} %param.9), channel_id=1, source_target_pairs={{0,16},{16,0},{1,17},{17,1},{2,18},{18,2},{3,19},{19,3},{4,20},{20... | collective-permute-start | bytes 4718600 | tf_op jit(solution)/shard_map/ppermute | solution.py:307
  3.6 2.4 %collective-permute-start.1 = (bf16[6144,128]{1,0:T(8,128)(2,1)}, bf16[6144,128]{1,0:T(8,128)(2,1)}, u32[]{:S(2)}, u32[]{:S(2)}) collective-permute-start(bf16[6144,128]{1,0:T(8,128)(2,1)} %param.10), channel_id=1, source_target_pairs={{0,16},{16,0},{1,17},{17,1},{2,18},{18,2},{3,19},{19,3},{4,20},{20... | collective-permute-start | bytes 4718600 | tf_op jit(solution)/shard_map/ppermute | solution.py:308
  6.1 2.0 %collective-permute-start.4 = (bf16[128,6144]{1,0:T(8,128)(2,1)}, bf16[128,6144]{1,0:T(8,128)(2,1)S(1)}, u32[]{:S(2)}, u32[]{:S(2)}) collective-permute-start(bf16[128,6144]{1,0:T(8,128)(2,1)} %down_ref.1), channel_id=1, source_target_pairs={{0,16},{16,0},{1,17},{17,1},{2,18},{18,2},{3,19},{19,3},{4,20},{20... | collective-permute-start | bytes 4718600 | tf_op jit(solution)/shard_map/ppermute | solution.py:309
  8.0 7.3 %all-to-all-start = ((bf16[8,20,384]{2,1,0:T(8,128)(2,1)}), bf16[8,20,384]{2,1,0:T(8,128)(2,1)S(1)}, u32[]{:S(2)}, u32[]{:S(2)}) async-start(bf16[8,20,384]{2,1,0:T(8,128)(2,1)} %dispatch.1), calls=%async_computation | async-start | bytes 294912 | tf_op jit(solution)/shard_map/all_to_all | solution.py:306
  15.4 10.1 %all-to-all-done.in_ref = bf16[8,20,384]{2,1,0:T(8,128)(2,1)S(1)} async-done(((bf16[8,20,384]{2,1,0:T(8,128)(2,1)}), bf16[8,20,384]{2,1,0:T(8,128)(2,1)S(1)}, u32[]{:S(2)}, u32[]{:S(2)}) %all-to-all-start) | async-done | bytes 122912 | tf_op jit(solution)/shard_map/all_to_all | solution.py:306
  25.5 68.7 %all-gather = bf16[1280,384]{1,0:T(8,128)(2,1)S(1)} all-gather(bf16[160,384]{1,0:T(8,128)(2,1)S(1)} %gather_rows.1), channel_id=2, replica_groups=mesh['rep'=2,'x'=8,'core'=2,'pair'=8,'odd'=2] {'pair'}, dimensions={0}, use_global_device_ids=true | all-gather | bytes 1105920 | tf_op jit(solution)/shard_map/all_gather | solution.py:310
  94.3 9.3 %collective-permute-start.2 = (bf16[4,160,384]{2,1,0:T(8,128)(2,1)S(1)}, bf16[4,160,384]{2,1,0:T(8,128)(2,1)S(1)}, u32[]{:S(2)}, u32[]{:S(2)}) collective-permute-start(bf16[4,160,384]{2,1,0:T(8,128)(2,1)S(1)} %get-tuple-element.20), channel_id=1, source_target_pairs={{0,15},{1,0},{2,1},{3,2},{4,3},{5,4},{6,5},{7,6},{8,7},{9,8},{10,9... | collective-permute-start | bytes 1474568 | tf_op jit(solution)/shard_map/ppermute | solution.py:294
  103.6 2.0 %collective-permute-start.3 = (bf16[4,160,384]{2,1,0:T(8,128)(2,1)S(1)}, bf16[4,160,384]{2,1,0:T(8,128)(2,1)S(1)}, u32[]{:S(2)}, u32[]{:S(2)}) collective-permute-start(bf16[4,160,384]{2,1,0:T(8,128)(2,1)S(1)} %get-tuple-element.19), channel_id=1, source_target_pairs={{0,1},{1,2},{2,3},{3,4},{4,5},{5,6},{6,7},{7,8},{8,9},{9,10},{10,1... | collective-permute-start | bytes 1474568 | tf_op jit(solution)/shard_map/ppermute | solution.py:294
  105.6 2.2 %own_part.1.total_ref = f32[160,512]{1,0:T(8,128)S(1)} custom-call(bf16[8,160,384]{2,1,0:T(8,128)(2,1)S(1)} %bitcast.9, bf16[8,2,384,128]{3,2,1,0:T(8,128)(2,1)S(1)} %bitcast.10, bf16[8,2,384,128]{3,2,1,0:T(8,128)(2,1)S(1)} %bitcast.14, bf16[8,2,384,128]{3,2,1,0:T(8,128)(2,1)S(1)} %bitcast.12, bf16[8,2,384,128]{3,2,1,0:T(8,128)(2,1)} %bitcast.6.up2_ref), custom_call_target="tpu_custom_call" | custom-call | flops 503316480 | bytes 4200000 | tf_op jit(solution)/shard_map/own_part/pallas_call | solution.py:149
  107.8 2.1 %collective-permute-done.2.early_ref = bf16[4,160,384]{2,1,0:T(8,128)(2,1)S(1)} collective-permute-done((bf16[4,160,384]{2,1,0:T(8,128)(2,1)S(1)}, bf16[4,160,384]{2,1,0:T(8,128)(2,1)S(1)}, u32[]{:S(2)}, u32[]{:S(2)}) %collective-permute-start.2) | collective-permute-done | bytes 491552 | tf_op jit(solution)/shard_map/ppermute | solution.py:294
  109.9 8.6 %collective-permute-done.3.late_ref = bf16[4,160,384]{2,1,0:T(8,128)(2,1)S(1)} collective-permute-done((bf16[4,160,384]{2,1,0:T(8,128)(2,1)S(1)}, bf16[4,160,384]{2,1,0:T(8,128)(2,1)S(1)}, u32[]{:S(2)}, u32[]{:S(2)}) %collective-permute-start.3) | collective-permute-done | bytes 491552 | tf_op jit(solution)/shard_map/ppermute | solution.py:294
  118.5 2.5 %ffn.1 = (bf16[160,256]{1,0:T(8,128)(2,1)S(1)}, bf16[4,160,384]{2,1,0:T(8,128)(2,1)S(1)}, bf16[4,160,384]{2,1,0:T(8,128)(2,1)S(1)}) custom-call(f32[160,512]{1,0:T(8,128)S(1)} %own_part.1.total_ref, bf16[4,160,384]{2,1,0:T(8,128)(2,1)S(1)} %collective-permute-done.2.early_ref, bf16[4,160,384]{2,1,0:T(8,128)(2,1)S(1)} %collective-permute-done.3.late_ref, ...), custom_call_target="tpu_custom_call" | custom-call | flops 754974720 | bytes 7000000 | tf_op jit(solution)/shard_map/ffn/pallas_call | solution.py:193
  121.0 2.0 %collective-permute-start.5 = (bf16[4,160,384]{2,1,0:T(8,128)(2,1)S(1)}, bf16[4,160,384]{2,1,0:T(8,128)(2,1)S(1)}, u32[]{:S(2)}, u32[]{:S(2)}) collective-permute-start(bf16[4,160,384]{2,1,0:T(8,128)(2,1)S(1)} %get-tuple-element.17), channel_id=1, source_target_pairs={{0,15},{1,0},{2,1},{3,2},{4,3},{5,4},{6,5},{7,6},{8,7},{9,8},{10,9... | collective-permute-start | bytes 1474568 | tf_op jit(solution)/shard_map/ppermute | solution.py:294
  122.9 4.0 %collective-permute-start.6 = (bf16[4,160,384]{2,1,0:T(8,128)(2,1)S(1)}, bf16[4,160,384]{2,1,0:T(8,128)(2,1)S(1)}, u32[]{:S(2)}, u32[]{:S(2)}) collective-permute-start(bf16[4,160,384]{2,1,0:T(8,128)(2,1)S(1)} %get-tuple-element.18), channel_id=1, source_target_pairs={{0,1},{1,2},{2,3},{3,4},{4,5},{5,6},{6,7},{7,8},{8,9},{9,10},{10,1... | collective-permute-start | bytes 1474568 | tf_op jit(solution)/shard_map/ppermute | solution.py:294
  126.9 0.4 own_down.1.own_ref
  127.3 4.4 %collective-permute-done.5.early_ref = bf16[4,160,384]{2,1,0:T(8,128)(2,1)S(1)} collective-permute-done((bf16[4,160,384]{2,1,0:T(8,128)(2,1)S(1)}, bf16[4,160,384]{2,1,0:T(8,128)(2,1)S(1)}, u32[]{:S(2)}, u32[]{:S(2)}) %collective-permute-start.5) | collective-permute-done | bytes 491552 | tf_op jit(solution)/shard_map/ppermute | solution.py:294
  131.7 3.2 %collective-permute-done.6.late_ref = bf16[4,160,384]{2,1,0:T(8,128)(2,1)S(1)} collective-permute-done((bf16[4,160,384]{2,1,0:T(8,128)(2,1)S(1)}, bf16[4,160,384]{2,1,0:T(8,128)(2,1)S(1)}, u32[]{:S(2)}, u32[]{:S(2)}) %collective-permute-start.6) | collective-permute-done | bytes 491552 | tf_op jit(solution)/shard_map/ppermute | solution.py:294
  134.9 1.2 join.1
  136.1 3.9 %all-to-all-start.1 = ((bf16[8,80,768]{2,1,0:T(8,128)(2,1)}), bf16[8,80,768]{2,1,0:T(8,128)(2,1)S(1)}, u32[]{:S(2)}, u32[]{:S(2)}) async-start(bf16[8,80,768]{2,1,0:T(8,128)(2,1)} %join.1), calls=%async_computation.1 | async-start | bytes 1966080 | tf_op jit(solution)/shard_map/all_to_all | solution.py:320
  140.4 23.2 %all-to-all-done.1 = bf16[8,80,768]{2,1,0:T(8,128)(2,1)S(1)} async-done(((bf16[8,80,768]{2,1,0:T(8,128)(2,1)}), bf16[8,80,768]{2,1,0:T(8,128)(2,1)S(1)}, u32[]{:S(2)}, u32[]{:S(2)}) %all-to-all-start.1) | async-done | bytes 983072 | tf_op jit(solution)/shard_map/all_to_all | solution.py:320
  163.6 0.4 combine.1
  164.0 23.6 %all_to_all.15 = bf16[8,32,384]{2,1,0:T(8,128)(2,1)S(1)} all-to-all(bf16[8,32,384]{2,1,0:T(8,128)(2,1)S(1)} %combine.1), channel_id=1, replica_groups=mesh['rep'=2,'x'=8,'core'=2,'pair'=8,'odd'=2] {'pair'}, dimensions={0} | all-to-all | bytes 393216 | tf_op jit(solution)/shard_map/all_to_all | solution.py:324
  187.5 0.6 reduce_sum.12
  (20 shorter events, 0.5 us)
Async XLA Ops:
  1.7 103.9 %collective-permute-start = (bf16[6144,128]{1,0:T(8,128)(2,1)}, bf16[6144,128]{1,0:T(8,128)(2,1)S(1)}, u32[]{:S(2)}, u32[]{:S(2)}) collective-permute-start(bf16[6144,128]{1,0:T(8,128)(2,1)} %param.9), channel_id=1, source_target_pairs={{0,16},{16,0},{1,17},{17,1},{2,18},{18,2},{3,19},{19,3},{4,20},{20... | collective-permute-start | bytes 4718600 | tf_op jit(solution)/shard_map/ppermute | solution.py:307
  3.6 101.9 %collective-permute-start.1 = (bf16[6144,128]{1,0:T(8,128)(2,1)}, bf16[6144,128]{1,0:T(8,128)(2,1)}, u32[]{:S(2)}, u32[]{:S(2)}) collective-permute-start(bf16[6144,128]{1,0:T(8,128)(2,1)} %param.10), channel_id=1, source_target_pairs={{0,16},{16,0},{1,17},{17,1},{2,18},{18,2},{3,19},{19,3},{4,20},{20... | collective-permute-start | bytes 4718600 | tf_op jit(solution)/shard_map/ppermute | solution.py:308
  6.1 112.4 %collective-permute-start.4 = (bf16[128,6144]{1,0:T(8,128)(2,1)}, bf16[128,6144]{1,0:T(8,128)(2,1)S(1)}, u32[]{:S(2)}, u32[]{:S(2)}) collective-permute-start(bf16[128,6144]{1,0:T(8,128)(2,1)} %down_ref.1), channel_id=1, source_target_pairs={{0,16},{16,0},{1,17},{17,1},{2,18},{18,2},{3,19},{19,3},{4,20},{20... | collective-permute-start | bytes 4718600 | tf_op jit(solution)/shard_map/ppermute | solution.py:309
  8.0 17.4 %all-to-all-start = ((bf16[8,20,384]{2,1,0:T(8,128)(2,1)}), bf16[8,20,384]{2,1,0:T(8,128)(2,1)S(1)}, u32[]{:S(2)}, u32[]{:S(2)}) async-start(bf16[8,20,384]{2,1,0:T(8,128)(2,1)} %dispatch.1), calls=%async_computation | async-start | bytes 294912 | tf_op jit(solution)/shard_map/all_to_all | solution.py:306
  25.5 80.1 %copy-start.2 = (bf16[6144,128]{1,0:T(8,128)(2,1)S(1)}, bf16[6144,128]{1,0:T(8,128)(2,1)}, u32[]{:S(2)}) copy-start(bf16[6144,128]{1,0:T(8,128)(2,1)} %param.10) | copy-start | bytes 4718596
  25.5 80.1 %copy-start.1 = (bf16[6144,128]{1,0:T(8,128)(2,1)S(1)}, bf16[6144,128]{1,0:T(8,128)(2,1)}, u32[]{:S(2)}) copy-start(bf16[6144,128]{1,0:T(8,128)(2,1)} %param.9) | copy-start | bytes 4718596
  94.3 15.6 %collective-permute-start.2 = (bf16[4,160,384]{2,1,0:T(8,128)(2,1)S(1)}, bf16[4,160,384]{2,1,0:T(8,128)(2,1)S(1)}, u32[]{:S(2)}, u32[]{:S(2)}) collective-permute-start(bf16[4,160,384]{2,1,0:T(8,128)(2,1)S(1)} %get-tuple-element.20), channel_id=1, source_target_pairs={{0,15},{1,0},{2,1},{3,2},{4,3},{5,4},{6,5},{7,6},{8,7},{9,8},{10,9... | collective-permute-start | bytes 1474568 | tf_op jit(solution)/shard_map/ppermute | solution.py:294
  103.6 14.9 %collective-permute-start.3 = (bf16[4,160,384]{2,1,0:T(8,128)(2,1)S(1)}, bf16[4,160,384]{2,1,0:T(8,128)(2,1)S(1)}, u32[]{:S(2)}, u32[]{:S(2)}) collective-permute-start(bf16[4,160,384]{2,1,0:T(8,128)(2,1)S(1)} %get-tuple-element.19), channel_id=1, source_target_pairs={{0,1},{1,2},{2,3},{3,4},{4,5},{5,6},{6,7},{7,8},{8,9},{9,10},{10,1... | collective-permute-start | bytes 1474568 | tf_op jit(solution)/shard_map/ppermute | solution.py:294
  105.6 12.9 %copy-start = (bf16[128,6144]{1,0:T(8,128)(2,1)S(1)}, bf16[128,6144]{1,0:T(8,128)(2,1)}, u32[]{:S(2)}) copy-start(bf16[128,6144]{1,0:T(8,128)(2,1)} %down_ref.1) | copy-start | bytes 4718596
  121.0 10.8 %collective-permute-start.5 = (bf16[4,160,384]{2,1,0:T(8,128)(2,1)S(1)}, bf16[4,160,384]{2,1,0:T(8,128)(2,1)S(1)}, u32[]{:S(2)}, u32[]{:S(2)}) collective-permute-start(bf16[4,160,384]{2,1,0:T(8,128)(2,1)S(1)} %get-tuple-element.17), channel_id=1, source_target_pairs={{0,15},{1,0},{2,1},{3,2},{4,3},{5,4},{6,5},{7,6},{8,7},{9,8},{10,9... | collective-permute-start | bytes 1474568 | tf_op jit(solution)/shard_map/ppermute | solution.py:294
  122.9 12.0 %collective-permute-start.6 = (bf16[4,160,384]{2,1,0:T(8,128)(2,1)S(1)}, bf16[4,160,384]{2,1,0:T(8,128)(2,1)S(1)}, u32[]{:S(2)}, u32[]{:S(2)}) collective-permute-start(bf16[4,160,384]{2,1,0:T(8,128)(2,1)S(1)} %get-tuple-element.18), channel_id=1, source_target_pairs={{0,1},{1,2},{2,3},{3,4},{4,5},{5,6},{6,7},{7,8},{8,9},{9,10},{10,1... | collective-permute-start | bytes 1474568 | tf_op jit(solution)/shard_map/ppermute | solution.py:294
  136.0 3.9 %copy-start.3 = (s32[32,2]{0,1:T(2,128)S(1)}, s32[32,2]{0,1:T(2,128)}, u32[]{:S(2)}) copy-start(s32[32,2]{0,1:T(2,128)} %param.7) | copy-start | bytes 772
  136.1 4.0 %copy-start.4 = (f32[32,2]{0,1:T(2,128)S(1)}, f32[32,2]{0,1:T(2,128)}, u32[]{:S(2)}) copy-start(f32[32,2]{0,1:T(2,128)} %param.8) | copy-start | bytes 772
  136.1 27.6 %all-to-all-start.1 = ((bf16[8,80,768]{2,1,0:T(8,128)(2,1)}), bf16[8,80,768]{2,1,0:T(8,128)(2,1)S(1)}, u32[]{:S(2)}, u32[]{:S(2)}) async-start(bf16[8,80,768]{2,1,0:T(8,128)(2,1)} %join.1), calls=%async_computation.1 | async-start | bytes 1966080 | tf_op jit(solution)/shard_map/all_to_all | solution.py:320

commit v8 on v5

--- a/solution.py
+++ b/solution.py
@@ -165,35 +165,35 @@
 
 
 def ffn_kernel(
-    total_ref, left_ref, right_ref, gate_ref, gate2_ref, up_ref, up2_ref, down_ref, down2_ref, hidden_ref, to_right_ref, to_left_ref
+    total_ref, inside_ref, outside_ref, gate_ref, gate2_ref, up_ref, up2_ref, down_ref, down2_ref, hidden_ref, to_inside_ref, to_outside_ref
 ):
-    half, _, depth = left_ref.shape
+    half, _, depth = inside_ref.shape
     parity = 1 - lax.axis_index("odd")
     width = gate_ref.shape[-1]
     refs = (gate_ref, gate2_ref, up_ref, up2_ref)
-    total = multiply(total_ref[...], left_ref, refs, parity, 0)
-    total = multiply(total, right_ref, refs, parity, half)
+    total = multiply(total_ref[...], inside_ref, refs, parity, 0)
+    total = multiply(total, outside_ref, refs, parity, half)
     gate = total[:, : 2 * width]
     hidden = (gate * jax.nn.sigmoid(gate) * total[:, 2 * width :]).astype(jnp.bfloat16)
     hidden_ref[...] = hidden
     for b in range(0, 2 * half, 2):
         partial = down_pair(hidden, (down_ref, down2_ref), b, parity, depth).astype(jnp.bfloat16)
-        out_ref, at = (to_right_ref, b) if b < half else (to_left_ref, b - half)
+        out_ref, at = (to_inside_ref, b) if b < half else (to_outside_ref, b - half)
         out_ref[at] = partial[:, :depth]
         out_ref[at + 1] = partial[:, depth:]
 
 
-def ffn(total, left, right, *weights):
-    _, rows, _ = left.shape
+def ffn(total, inside, outside, *weights):
+    _, rows, _ = inside.shape
     width, model = weights[-1].shape
-    sent = jax.ShapeDtypeStruct(left.shape, jnp.bfloat16)
+    sent = jax.ShapeDtypeStruct(inside.shape, jnp.bfloat16)
     return pl.pallas_call(
         ffn_kernel,
         out_shape=(jax.ShapeDtypeStruct((rows, 2 * width), jnp.bfloat16), sent, sent),
         cost_estimate=cost(2 * rows * model * width * 3, 7000000),
         compiler_params=pltpu.CompilerParams(vmem_limit_bytes=20 << 20),
         name="ffn",
-    )(total, left, right, *weights)
+    )(total, inside, outside, *weights)
 
 
 def own_down_kernel(hidden_ref, down_ref, down2_ref, out_ref):
@@ -218,13 +218,13 @@
     )(hidden, down, down2)
 
 
-def join_kernel(own_ref, left_ref, right_ref, out_ref):
+def join_kernel(own_ref, inside_ref, outside_ref, out_ref):
     pairs, _, depth = own_ref.shape
     chips = out_ref.shape[0]
     half = pairs // 2
     per_quarter = pairs // QUARTERS
     for b in range(pairs):
-        other = left_ref[b] if b < half else right_ref[b - half]
+        other = inside_ref[b] if b < half else outside_ref[b - half]
         both = (own_ref[b] + other.astype(jnp.float32)).astype(jnp.bfloat16)
         q, s = b // per_quarter, b % per_quarter
         at = QUARTERS * MAIN + q * TAIL
@@ -235,7 +235,7 @@
             out_ref[chip, at : at + TAIL, lanes] = both[tail : tail + TAIL]
 
 
-def join(own, left, right, chips):
+def join(own, inside, outside, chips):
     pairs, rows, depth = own.shape
     out = (chips, QUARTERS * CAP, pairs * depth // QUARTERS)
     return pl.pallas_call(
@@ -244,7 +244,7 @@
         cost_estimate=cost(pairs * rows * depth, 8 * pairs * rows * depth),
         compiler_params=pltpu.CompilerParams(vmem_limit_bytes=16 << 20),
         name="join",
-    )(own, left, right)
+    )(own, inside, outside)
 
 
 def combine_kernel(mix_ref, back_ref, out_ref):
@@ -280,8 +280,8 @@
     swap = [(0, 1), (1, 0)]
     along = ("pair", "odd")
     ids = expert_ids.T
-    up_z = [(i, (i + 1) % parts) for i in range(parts)]
-    down_z = [((i + 1) % parts, i) for i in range(parts)]
+    inner = [(z, z + 1 if z % 2 == 0 else z - 1) for z in range(parts)]
+    outer = [(z, (z - 1 if z % 2 == 0 else z + 1) % parts) for z in range(parts)]
     outgoing = dispatch(ids, tokens, chips)
     gate, up, down, outgoing = lax.optimization_barrier(
         (gate_weight, up_weight, down_weight, outgoing)
@@ -291,14 +291,14 @@
     up2 = lax.ppermute(up, "core", swap)
     down2 = lax.ppermute(down, "core", swap)
     own = lax.all_gather(gather_rows(incoming), "pair")
-    left = lax.ppermute(own[: pairs // 2], along, up_z)
-    right = lax.ppermute(own[pairs // 2 :], along, down_z)
+    inside = lax.ppermute(own[: pairs // 2], along, inner)
+    outside = lax.ppermute(own[pairs // 2 :], along, outer)
     blocks = [w.reshape(pairs, 2, depth, w.shape[1]) for w in (gate, gate2, up, up2)]
     total = own_part(own, *blocks)
-    hidden, to_right, to_left = ffn(total, left, right, *blocks, down, down2)
-    from_left = lax.ppermute(to_right, along, up_z)
-    from_right = lax.ppermute(to_left, along, down_z)
-    partial_value = join(own_down(hidden, down, down2, pairs), from_left, from_right, chips)
+    hidden, inside, outside = ffn(total, inside, outside, *blocks, down, down2)
+    inside = lax.ppermute(inside, along, inner)
+    outside = lax.ppermute(outside, along, outer)
+    partial_value = join(own_down(hidden, down, down2, pairs), inside, outside, chips)
     returned = lax.all_to_all(partial_value, "x", 0, 0, tiled=True)
     mix = mixing(ids, route_logits.T, chips)
     back = returned.reshape(chips * QUARTERS * CAP, pairs * depth // QUARTERS)

time: 177 us -> 179 us (1.011)
  no operation moved by 1% of the time
where the time goes in v8:
time: 179 us; the launch traced here: 178 us
  blocking collectives  109 us (61%)
  waiting for transfers between devices  33 us (18%)
  starting transfers between devices  29.4 us (16%)
  Pallas kernels  5.58 us (3%)
    all_gather x1, blocking collectives, on_device(): own = lax.all_gather(gather_rows(incoming), 'pair')  68.7 us
    all_to_all x1, blocking collectives, on_device(): blocks = lax.all_to_all(combined, 'pair', 0, 0, tiled=True)  22.8 us
    all_to_all x1, waiting for transfers between devices, on_device(): returned = lax.all_to_all(partial_value, 'x', 0, 0, tiled=True)  19.7 us
    all_to_all x1, blocking collectives, on_device(): incoming = lax.all_to_all(outgoing, 'x', 0, 0, tiled=True)  17.4 us
    ppermute x1, starting transfers between devices, on_device(): inside = lax.ppermute(own[:pairs // 2], along, inner)  6.16 us
    ppermute x1, waiting for transfers between devices, on_device(): outside = lax.ppermute(own[pairs // 2:], along, outer)  5.17 us
    ppermute x1, starting transfers between devices, on_device(): outside = lax.ppermute(own[pairs // 2:], along, outer)  5.06 us
    ppermute x1, waiting for transfers between devices, on_device(): outside = lax.ppermute(outside, along, outer)  4.88 us
  transfers between devices with their start and end apart: 8, of which 5 were waited for; matrix products, arithmetic and copies ran while one was open for 0% of the time, Pallas kernels for 1%

profile of v8, /device:TPU:80, one launch (start us, length us, event | category | flops | bytes accessed | tf_op | source)
XLA Modules:
  0.0 178.1 jit_solution(12535800281925406809)
XLA Ops:
  0.0 1.7 dispatch.1
  1.7 1.9 %collective-permute-start = (bf16[6144,128]{1,0:T(8,128)(2,1)}, bf16[6144,128]{1,0:T(8,128)(2,1)S(1)}, u32[]{:S(2)}, u32[]{:S(2)}) collective-permute-start(bf16[6144,128]{1,0:T(8,128)(2,1)} %param.9), channel_id=1, source_target_pairs={{0,16},{16,0},{1,17},{17,1},{2,18},{18,2},{3,19},{19,3},{4,20},{20... | collective-permute-start | bytes 4718600 | tf_op jit(solution)/shard_map/ppermute | solution.py:290
  3.6 2.4 %collective-permute-start.1 = (bf16[6144,128]{1,0:T(8,128)(2,1)}, bf16[6144,128]{1,0:T(8,128)(2,1)S(1)}, u32[]{:S(2)}, u32[]{:S(2)}) collective-permute-start(bf16[6144,128]{1,0:T(8,128)(2,1)} %param.10), channel_id=1, source_target_pairs={{0,16},{16,0},{1,17},{17,1},{2,18},{18,2},{3,19},{19,3},{4,20},{20... | collective-permute-start | bytes 4718600 | tf_op jit(solution)/shard_map/ppermute | solution.py:291
  6.1 2.0 %collective-permute-start.4 = (bf16[128,6144]{1,0:T(8,128)(2,1)}, bf16[128,6144]{1,0:T(8,128)(2,1)S(1)}, u32[]{:S(2)}, u32[]{:S(2)}) collective-permute-start(bf16[128,6144]{1,0:T(8,128)(2,1)} %down_ref.1), channel_id=1, source_target_pairs={{0,16},{16,0},{1,17},{17,1},{2,18},{18,2},{3,19},{19,3},{4,20},{20... | collective-permute-start | bytes 4718600 | tf_op jit(solution)/shard_map/ppermute | solution.py:292
  8.0 17.4 %all_to_all.15.in_ref = bf16[8,20,384]{2,1,0:T(8,128)(2,1)S(1)} all-to-all(bf16[8,20,384]{2,1,0:T(8,128)(2,1)} %dispatch.1), channel_id=1, replica_groups=mesh['rep'=2,'x'=8,'core'=2,'pair'=8,'odd'=2] {'x'}, dimensions={0} | all-to-all | bytes 245760 | tf_op jit(solution)/shard_map/all_to_all | solution.py:289
  25.5 68.7 %all-gather = bf16[1280,384]{1,0:T(8,128)(2,1)S(1)} all-gather(bf16[160,384]{1,0:T(8,128)(2,1)S(1)} %gather_rows.1), channel_id=2, replica_groups=mesh['rep'=2,'x'=8,'core'=2,'pair'=8,'odd'=2] {'pair'}, dimensions={0}, use_global_device_ids=true | all-gather | bytes 1105920 | tf_op jit(solution)/shard_map/all_gather | solution.py:293
  94.3 6.2 %collective-permute-start.2 = (bf16[4,160,384]{2,1,0:T(8,128)(2,1)S(1)}, bf16[4,160,384]{2,1,0:T(8,128)(2,1)S(1)}, u32[]{:S(2)}, u32[]{:S(2)}) collective-permute-start(bf16[4,160,384]{2,1,0:T(8,128)(2,1)S(1)} %bitcast.21), channel_id=1, source_target_pairs={{0,1},{1,0},{2,3},{3,2},{4,5},{5,4},{6,7},{7,6},{8,9},{9,8},{10,11... | collective-permute-start | bytes 1474568 | tf_op jit(solution)/shard_map/ppermute | solution.py:294
  100.5 5.1 %collective-permute-start.3 = (bf16[4,160,384]{2,1,0:T(8,128)(2,1)S(1)}, bf16[4,160,384]{2,1,0:T(8,128)(2,1)S(1)}, u32[]{:S(2)}, u32[]{:S(2)}) collective-permute-start(bf16[4,160,384]{2,1,0:T(8,128)(2,1)S(1)} %bitcast.20), channel_id=1, source_target_pairs={{0,15},{1,2},{2,1},{3,4},{4,3},{5,6},{6,5},{7,8},{8,7},{9,10},{10,... | collective-permute-start | bytes 1474568 | tf_op jit(solution)/shard_map/ppermute | solution.py:295
  105.6 0.7 own_part.1.total_ref
  106.3 1.0 collective-permute-done.2.inside_ref
  107.3 5.2 %collective-permute-done.3.outside_ref = bf16[4,160,384]{2,1,0:T(8,128)(2,1)S(1)} collective-permute-done((bf16[4,160,384]{2,1,0:T(8,128)(2,1)S(1)}, bf16[4,160,384]{2,1,0:T(8,128)(2,1)S(1)}, u32[]{:S(2)}, u32[]{:S(2)}) %collective-permute-start.3) | collective-permute-done | bytes 491552 | tf_op jit(solution)/shard_map/ppermute | solution.py:295
  112.5 1.1 ffn.1
  113.5 3.7 %collective-permute-start.5 = (bf16[4,160,384]{2,1,0:T(8,128)(2,1)S(1)}, bf16[4,160,384]{2,1,0:T(8,128)(2,1)S(1)}, u32[]{:S(2)}, u32[]{:S(2)}) collective-permute-start(bf16[4,160,384]{2,1,0:T(8,128)(2,1)S(1)} %get-tuple-element.17), channel_id=1, source_target_pairs={{0,1},{1,0},{2,3},{3,2},{4,5},{5,4},{6,7},{7,6},{8,9},{9,8},{10,11... | collective-permute-start | bytes 1474568 | tf_op jit(solution)/shard_map/ppermute | solution.py:299
  117.2 4.3 %collective-permute-start.6 = (bf16[4,160,384]{2,1,0:T(8,128)(2,1)S(1)}, bf16[4,160,384]{2,1,0:T(8,128)(2,1)S(1)}, u32[]{:S(2)}, u32[]{:S(2)}) collective-permute-start(bf16[4,160,384]{2,1,0:T(8,128)(2,1)S(1)} %get-tuple-element.18), channel_id=1, source_target_pairs={{0,15},{1,2},{2,1},{3,4},{4,3},{5,6},{6,5},{7,8},{8,7},{9,10},{10,... | collective-permute-start | bytes 1474568 | tf_op jit(solution)/shard_map/ppermute | solution.py:300
  121.5 0.4 own_down.1.own_ref
  122.0 2.3 %collective-permute-done.5.inside_ref = bf16[4,160,384]{2,1,0:T(8,128)(2,1)S(1)} collective-permute-done((bf16[4,160,384]{2,1,0:T(8,128)(2,1)S(1)}, bf16[4,160,384]{2,1,0:T(8,128)(2,1)S(1)}, u32[]{:S(2)}, u32[]{:S(2)}) %collective-permute-start.5) | collective-permute-done | bytes 491552 | tf_op jit(solution)/shard_map/ppermute | solution.py:299
  124.3 4.9 %collective-permute-done.6.outside_ref = bf16[4,160,384]{2,1,0:T(8,128)(2,1)S(1)} collective-permute-done((bf16[4,160,384]{2,1,0:T(8,128)(2,1)S(1)}, bf16[4,160,384]{2,1,0:T(8,128)(2,1)S(1)}, u32[]{:S(2)}, u32[]{:S(2)}) %collective-permute-start.6) | collective-permute-done | bytes 491552 | tf_op jit(solution)/shard_map/ppermute | solution.py:300
  129.2 1.1 join.1
  130.3 3.9 %all-to-all-start.1 = ((bf16[8,80,768]{2,1,0:T(8,128)(2,1)}), bf16[8,80,768]{2,1,0:T(8,128)(2,1)S(1)}, u32[]{:S(2)}, u32[]{:S(2)}) async-start(bf16[8,80,768]{2,1,0:T(8,128)(2,1)} %join.1), calls=%async_computation.1 | async-start | bytes 1966080 | tf_op jit(solution)/shard_map/all_to_all | solution.py:302
  134.4 0.2 mixing.1.mix_ref
  134.6 19.7 %all-to-all-done.1 = bf16[8,80,768]{2,1,0:T(8,128)(2,1)S(1)} async-done(((bf16[8,80,768]{2,1,0:T(8,128)(2,1)}), bf16[8,80,768]{2,1,0:T(8,128)(2,1)S(1)}, u32[]{:S(2)}, u32[]{:S(2)}) %all-to-all-start.1) | async-done | bytes 983072 | tf_op jit(solution)/shard_map/all_to_all | solution.py:302
  154.3 0.4 combine.1
  154.6 22.8 %all_to_all.16 = bf16[8,32,384]{2,1,0:T(8,128)(2,1)S(1)} all-to-all(bf16[8,32,384]{2,1,0:T(8,128)(2,1)S(1)} %combine.1), channel_id=1, replica_groups=mesh['rep'=2,'x'=8,'core'=2,'pair'=8,'odd'=2] {'pair'}, dimensions={0} | all-to-all | bytes 393216 | tf_op jit(solution)/shard_map/all_to_all | solution.py:306
  177.4 0.6 reduce_sum.12
  (19 shorter events, 0.3 us)
Async XLA Ops:
  1.7 103.9 %collective-permute-start = (bf16[6144,128]{1,0:T(8,128)(2,1)}, bf16[6144,128]{1,0:T(8,128)(2,1)S(1)}, u32[]{:S(2)}, u32[]{:S(2)}) collective-permute-start(bf16[6144,128]{1,0:T(8,128)(2,1)} %param.9), channel_id=1, source_target_pairs={{0,16},{16,0},{1,17},{17,1},{2,18},{18,2},{3,19},{19,3},{4,20},{20... | collective-permute-start | bytes 4718600 | tf_op jit(solution)/shard_map/ppermute | solution.py:290
  3.6 101.9 %collective-permute-start.1 = (bf16[6144,128]{1,0:T(8,128)(2,1)}, bf16[6144,128]{1,0:T(8,128)(2,1)S(1)}, u32[]{:S(2)}, u32[]{:S(2)}) collective-permute-start(bf16[6144,128]{1,0:T(8,128)(2,1)} %param.10), channel_id=1, source_target_pairs={{0,16},{16,0},{1,17},{17,1},{2,18},{18,2},{3,19},{19,3},{4,20},{20... | collective-permute-start | bytes 4718600 | tf_op jit(solution)/shard_map/ppermute | solution.py:291
  6.1 106.4 %collective-permute-start.4 = (bf16[128,6144]{1,0:T(8,128)(2,1)}, bf16[128,6144]{1,0:T(8,128)(2,1)S(1)}, u32[]{:S(2)}, u32[]{:S(2)}) collective-permute-start(bf16[128,6144]{1,0:T(8,128)(2,1)} %down_ref.1), channel_id=1, source_target_pairs={{0,16},{16,0},{1,17},{17,1},{2,18},{18,2},{3,19},{19,3},{4,20},{20... | collective-permute-start | bytes 4718600 | tf_op jit(solution)/shard_map/ppermute | solution.py:292
  25.4 80.1 %copy-start.2 = (bf16[6144,128]{1,0:T(8,128)(2,1)S(1)}, bf16[6144,128]{1,0:T(8,128)(2,1)}, u32[]{:S(2)}) copy-start(bf16[6144,128]{1,0:T(8,128)(2,1)} %param.10) | copy-start | bytes 4718596
  25.5 80.1 %copy-start.1 = (bf16[6144,128]{1,0:T(8,128)(2,1)S(1)}, bf16[6144,128]{1,0:T(8,128)(2,1)}, u32[]{:S(2)}) copy-start(bf16[6144,128]{1,0:T(8,128)(2,1)} %param.9) | copy-start | bytes 4718596
  94.3 13.0 %collective-permute-start.2 = (bf16[4,160,384]{2,1,0:T(8,128)(2,1)S(1)}, bf16[4,160,384]{2,1,0:T(8,128)(2,1)S(1)}, u32[]{:S(2)}, u32[]{:S(2)}) collective-permute-start(bf16[4,160,384]{2,1,0:T(8,128)(2,1)S(1)} %bitcast.21), channel_id=1, source_target_pairs={{0,1},{1,0},{2,3},{3,2},{4,5},{5,4},{6,7},{7,6},{8,9},{9,8},{10,11... | collective-permute-start | bytes 1474568 | tf_op jit(solution)/shard_map/ppermute | solution.py:294
  100.5 12.0 %collective-permute-start.3 = (bf16[4,160,384]{2,1,0:T(8,128)(2,1)S(1)}, bf16[4,160,384]{2,1,0:T(8,128)(2,1)S(1)}, u32[]{:S(2)}, u32[]{:S(2)}) collective-permute-start(bf16[4,160,384]{2,1,0:T(8,128)(2,1)S(1)} %bitcast.20), channel_id=1, source_target_pairs={{0,15},{1,2},{2,1},{3,4},{4,3},{5,6},{6,5},{7,8},{8,7},{9,10},{10,... | collective-permute-start | bytes 1474568 | tf_op jit(solution)/shard_map/ppermute | solution.py:295
  105.6 6.9 %copy-start = (bf16[128,6144]{1,0:T(8,128)(2,1)S(1)}, bf16[128,6144]{1,0:T(8,128)(2,1)}, u32[]{:S(2)}) copy-start(bf16[128,6144]{1,0:T(8,128)(2,1)} %down_ref.1) | copy-start | bytes 4718596
  113.5 10.8 %collective-permute-start.5 = (bf16[4,160,384]{2,1,0:T(8,128)(2,1)S(1)}, bf16[4,160,384]{2,1,0:T(8,128)(2,1)S(1)}, u32[]{:S(2)}, u32[]{:S(2)}) collective-permute-start(bf16[4,160,384]{2,1,0:T(8,128)(2,1)S(1)} %get-tuple-element.17), channel_id=1, source_target_pairs={{0,1},{1,0},{2,3},{3,2},{4,5},{5,4},{6,7},{7,6},{8,9},{9,8},{10,11... | collective-permute-start | bytes 1474568 | tf_op jit(solution)/shard_map/ppermute | solution.py:299
  117.2 12.0 %collective-permute-start.6 = (bf16[4,160,384]{2,1,0:T(8,128)(2,1)S(1)}, bf16[4,160,384]{2,1,0:T(8,128)(2,1)S(1)}, u32[]{:S(2)}, u32[]{:S(2)}) collective-permute-start(bf16[4,160,384]{2,1,0:T(8,128)(2,1)S(1)} %get-tuple-element.18), channel_id=1, source_target_pairs={{0,15},{1,2},{2,1},{3,4},{4,3},{5,6},{6,5},{7,8},{8,7},{9,10},{10,... | collective-permute-start | bytes 1474568 | tf_op jit(solution)/shard_map/ppermute | solution.py:300
  130.3 3.9 %copy-start.3 = (s32[32,2]{0,1:T(2,128)S(1)}, s32[32,2]{0,1:T(2,128)}, u32[]{:S(2)}) copy-start(s32[32,2]{0,1:T(2,128)} %param.7) | copy-start | bytes 772
  130.3 4.0 %copy-start.4 = (f32[32,2]{0,1:T(2,128)S(1)}, f32[32,2]{0,1:T(2,128)}, u32[]{:S(2)}) copy-start(f32[32,2]{0,1:T(2,128)} %param.8) | copy-start | bytes 772
  130.3 24.0 %all-to-all-start.1 = ((bf16[8,80,768]{2,1,0:T(8,128)(2,1)}), bf16[8,80,768]{2,1,0:T(8,128)(2,1)S(1)}, u32[]{:S(2)}, u32[]{:S(2)}) async-start(bf16[8,80,768]{2,1,0:T(8,128)(2,1)} %join.1), calls=%async_computation.1 | async-start | bytes 1966080 | tf_op jit(solution)/shard_map/all_to_all | solution.py:302

commit v9 on v6

--- a/solution.py
+++ b/solution.py
@@ -45,59 +45,50 @@
 
 
 def dispatch_kernel(chips, ids_ref, tokens_ref, out_ref):
-    blocks, count, _ = tokens_ref.shape
-    per_expert = chips // EXPERTS
+    count = tokens_ref.shape[0]
     row = lax.broadcasted_iota(jnp.int32, (EXPERTS * CAP, count), 0)
-    expert, slot = grouped(row, EXPERTS)
+    expert = count_at_least(row, CAP, EXPERTS)
+    slot = row - CAP * expert
     first = lax.broadcasted_iota(jnp.int32, (count, count), 0)
     second = lax.broadcasted_iota(jnp.int32, (count, count), 1)
     before = (first < second).astype(jnp.float32)
     placement = placed(ids_ref[...], expert, slot, before).astype(jnp.bfloat16)
-    for q in range(blocks):
-        slots = jnp.dot(placement, tokens_ref[q], preferred_element_type=jnp.float32).astype(
-            jnp.bfloat16
-        )
-        for chip in range(chips):
-            e = chip // per_expert
-            out_ref[chip, q * MAIN : (q + 1) * MAIN] = slots[e * MAIN : (e + 1) * MAIN]
-            to, at = QUARTERS * MAIN + q * TAIL, EXPERTS * MAIN + e * TAIL
-            out_ref[chip, to : to + TAIL] = slots[at : at + TAIL]
+    slots = jnp.dot(placement, tokens_ref[...], preferred_element_type=jnp.float32).astype(
+        jnp.bfloat16
+    )
+    per_expert = chips // EXPERTS
+    for chip in range(chips):
+        e = chip // per_expert
+        out_ref[chip] = slots[e * CAP : (e + 1) * CAP]
 
 
 def dispatch(ids, tokens, chips):
-    blocks, count, depth = tokens.shape
+    count, features = tokens.shape
     return pl.pallas_call(
         functools.partial(dispatch_kernel, chips),
-        out_shape=jax.ShapeDtypeStruct((chips, blocks * CAP, depth), jnp.bfloat16),
-        cost_estimate=cost(2 * EXPERTS * CAP * count * blocks * depth, 700000),
+        out_shape=jax.ShapeDtypeStruct((chips, CAP, features), jnp.bfloat16),
+        cost_estimate=cost(2 * EXPERTS * CAP * count * features, 200000),
         compiler_params=pltpu.CompilerParams(vmem_limit_bytes=60 << 20),
         name="dispatch",
     )(ids, tokens)
 
 
-def unpack_kernel(in_ref, out_ref, low_ref, high_ref):
+def gather_rows_kernel(in_ref, out_ref):
     chips = in_ref.shape[0]
-    for q in range(QUARTERS):
-        at = QUARTERS * MAIN + q * TAIL
-        rows = jnp.concatenate(
-            [in_ref[chip, q * MAIN : (q + 1) * MAIN] for chip in range(chips)]
-            + [in_ref[chip, at : at + TAIL] for chip in range(chips)],
-            axis=0,
-        )
-        out_ref[q] = rows
-        half_ref = low_ref if q < QUARTERS // 2 else high_ref
-        half_ref[q % (QUARTERS // 2)] = rows
-
-
-def unpack(slots):
+    for chip in range(chips):
+        out_ref[chip * MAIN : (chip + 1) * MAIN] = in_ref[chip, :MAIN]
+        at = chips * MAIN + chip * TAIL
+        out_ref[at : at + TAIL] = in_ref[chip, MAIN:]
+
+
+def gather_rows(slots):
     chips, _, depth = slots.shape
-    half = jax.ShapeDtypeStruct((QUARTERS // 2, chips * CAP, depth), jnp.bfloat16)
-    return pl.pallas_call(
-        unpack_kernel,
-        out_shape=(jax.ShapeDtypeStruct((QUARTERS, chips * CAP, depth), jnp.bfloat16), half, half),
-        cost_estimate=cost(1000, 1500000),
-        compiler_params=pltpu.CompilerParams(vmem_limit_bytes=8 << 20),
-        name="unpack",
+    return pl.pallas_call(
+        gather_rows_kernel,
+        out_shape=jax.ShapeDtypeStruct((chips * CAP, depth), jnp.bfloat16),
+        cost_estimate=cost(1000, 250000),
+        compiler_params=pltpu.CompilerParams(vmem_limit_bytes=4 << 20),
+        name="gather_rows",
     )(slots)
 
 
@@ -133,18 +124,20 @@
 
 
 def class_at(distance):
-    return lax.rem(lax.axis_index("class") + CLASSES + distance, CLASSES)
-
-
-def side_by_side(refs, q, kind):
-    return jnp.concatenate([ref[q, kind] for ref in refs], axis=1)
-
-
-def multiply(total, tokens, refs, kind, start):
+    own = 2 * lax.axis_index("half") + lax.axis_index("odd")
+    return lax.rem(own + CLASSES + distance, CLASSES)
+
+
+def side_by_side(refs, b, parity):
+    return jnp.concatenate([ref[b, parity] for ref in refs], axis=1)
+
+
+def multiply(total, tokens, refs, parity, start):
     for b in range(0, tokens.shape[0], 2):
         rows = jnp.concatenate([tokens[b], tokens[b + 1]], axis=1)
         weight = jnp.concatenate(
-            [side_by_side(refs, start + b, kind), side_by_side(refs, start + b + 1, kind)], axis=0
+            [side_by_side(refs, start + b, parity), side_by_side(refs, start + b + 1, parity)],
+            axis=0,
         )
         added = jnp.dot(rows, weight, preferred_element_type=jnp.float32)
         total = added if total is None else total + added
@@ -153,16 +146,16 @@
 
 def own_kernel(slots_ref, gate_ref, gate2_ref, up_ref, up2_ref, out_ref):
     refs = (gate_ref, gate2_ref, up_ref, up2_ref)
-    out_ref[...] = multiply(None, slots_ref, refs, class_at(0), 0)
+    out_ref[...] = multiply(None, slots_ref, refs, lax.axis_index("odd"), 0)
 
 
 def own_part(slots, *weights):
-    blocks, rows, depth = slots.shape
+    pairs, rows, depth = slots.shape
     width = weights[0].shape[-1]
     return pl.pallas_call(
         own_kernel,
         out_shape=jax.ShapeDtypeStruct((rows, 4 * width), jnp.float32),
-        cost_estimate=cost(2 * blocks * rows * depth * 4 * width, 2200000),
+        cost_estimate=cost(2 * pairs * rows * depth * 4 * width, 4200000),
         compiler_params=pltpu.CompilerParams(vmem_limit_bytes=16 << 20),
         name="own_part",
     )(slots, *weights)
@@ -178,16 +171,15 @@
 
 
 def ffn_kernel(
-    total_ref, left_ref, right_ref, left2_ref, right2_ref, gate_ref, gate2_ref, up_ref, up2_ref, down_ref, down2_ref, hidden_ref, to_right_ref, to_left_ref, to_right2_ref, to_left2_ref
+    total_ref, left_ref, right_ref, gate_ref, gate2_ref, up_ref, up2_ref, down_ref, down2_ref, hidden_ref, to_right_ref, to_left_ref, to_right2_ref, to_left2_ref
 ):
-    depth = left_ref.shape[2]
+    pairs, _, depth = left_ref.shape
+    parity = 1 - lax.axis_index("odd")
     width = gate_ref.shape[-1]
     half = QUARTERS // 2
     refs = (gate_ref, gate2_ref, up_ref, up2_ref)
-    total = multiply(total_ref[...], left_ref, refs, class_at(-1), 0)
-    total = multiply(total, right_ref, refs, class_at(1), 0)
-    total = multiply(total, left2_ref, refs, class_at(2), 0)
-    total = multiply(total, right2_ref, refs, class_at(2), half)
+    total = multiply(total_ref[...], left_ref, refs, parity, 0)
+    total = multiply(total, right_ref, refs, parity, pairs)
     gate = total[:, : 2 * width]
     hidden = (gate * jax.nn.sigmoid(gate) * total[:, 2 * width :]).astype(jnp.bfloat16)
     hidden_ref[...] = hidden
@@ -205,11 +197,11 @@
             out_ref[b + 1] = partial[:, depth:]
 
 
-def ffn(total, left, right, left2, right2, *weights):
-    rows = left.shape[1]
+def ffn(total, left, right, *weights):
+    rows, depth = left.shape[1:]
     width, model = weights[-1].shape
-    sent = jax.ShapeDtypeStruct(left.shape, jnp.bfloat16)
-    half = jax.ShapeDtypeStruct(left2.shape, jnp.bfloat16)
+    sent = jax.ShapeDtypeStruct((QUARTERS, rows, depth), jnp.bfloat16)
+    half = jax.ShapeDtypeStruct((QUARTERS // 2, rows, depth), jnp.bfloat16)
     return pl.pallas_call(
         ffn_kernel,
         out_shape=(
@@ -222,7 +214,7 @@
         cost_estimate=cost(2 * rows * model * width * 4, 9000000),
         compiler_params=pltpu.CompilerParams(vmem_limit_bytes=20 << 20),
         name="ffn",
-    )(total, left, right, left2, right2, *weights)
+    )(total, left, right, *weights)
 
 
 def own_down_kernel(hidden_ref, down_ref, down2_ref, out_ref):
@@ -299,31 +291,29 @@
 
 def on_device(tokens, expert_ids, route_logits, gate_weight, up_weight, down_weight):
     chips = lax.axis_size("x")
-    parts = QUARTERS * CLASSES
+    pairs = lax.axis_size("quarter") * lax.axis_size("half")
+    parts = 2 * pairs
     count, depth = tokens.shape
     swap = [(0, 1), (1, 0)]
-    along = ("quarter", "class")
+    along = ("quarter", "half", "odd")
     ids = expert_ids.T
 
     def shift(value, distance):
         return lax.ppermute(value, along, [(i, (i + distance) % parts) for i in range(parts)])
 
-    outgoing = dispatch(ids, lax.all_gather(tokens, "quarter"), chips)
-    gate, up, down, outgoing = lax.optimization_barrier(
-        (gate_weight, up_weight, down_weight, outgoing)
-    )
+    outgoing = dispatch(ids, tokens, chips)
+    gate, up, outgoing = lax.optimization_barrier((gate_weight, up_weight, outgoing))
     incoming = lax.all_to_all(outgoing, "x", 0, 0, tiled=True)
     gate2 = lax.ppermute(gate, "core", swap)
     up2 = lax.ppermute(up, "core", swap)
+    own = lax.all_gather(gather_rows(incoming), ("quarter", "half"))
+    down, own = lax.optimization_barrier((down_weight, own))
+    left = shift(own[: pairs // 2], 1)
+    right = shift(own[pairs // 2 :], -1)
     down2 = lax.ppermute(down, "core", swap)
-    own, low, high = unpack(incoming)
-    left, right = shift(own, 1), shift(own, -1)
-    left2, right2 = shift(low, 2), shift(high, -2)
-    blocks = [w.reshape(QUARTERS, CLASSES, depth, w.shape[1]) for w in (gate, gate2, up, up2)]
+    blocks = [w.reshape(pairs, 2, depth, w.shape[1]) for w in (gate, gate2, up, up2)]
     total = own_part(own, *blocks)
-    hidden, to_right, to_left, to_right2, to_left2 = ffn(
-        total, left, right, left2, right2, *blocks, down, down2
-    )
+    hidden, to_right, to_left, to_right2, to_left2 = ffn(total, left, right, *blocks, down, down2)
     left, right = shift(to_right, 1), shift(to_left, -1)
     left2, right2 = shift(to_right2, 2), shift(to_left2, -2)
     partial_value = join(own_down(hidden, down, down2), left, right, left2, right2, chips)
@@ -336,11 +326,11 @@
 
 def solution(mesh):
     sizes = [mesh.shape[axis] for axis in ("rep", "exp", "tp")]
-    devices = mesh.devices.reshape(sizes[0], sizes[1] // CORES, CORES, QUARTERS, CLASSES)
-    split = Mesh(devices, ("rep", "x", "core", "quarter", "class"))
+    devices = mesh.devices.reshape(sizes[0], sizes[1] // CORES, CORES, QUARTERS, 2, 2)
+    split = Mesh(devices, ("rep", "x", "core", "quarter", "half", "odd"))
     tokens = ("rep", "x", "core")
-    features = ("quarter", "class")
-    hidden = ("x", "core", "quarter", "class")
+    features = ("quarter", "half", "odd")
+    hidden = ("x", "core", "quarter", "half", "odd")
     return jax.shard_map(
         on_device,
         mesh=split,

time: 190 us -> 186 us (0.979)
  blocking collectives: 95.3 us -> 90.7 us
  Pallas kernels: 5.86 us -> 8.47 us
  starting transfers between devices: 46.1 us -> 43.6 us
    all_to_all x1 -> x0, blocking collectives: 24.8 us -> none  [on_device(): incoming = lax.all_to_all(outgoing, 'x', 0, 0, tiled=True)]
    all_gather x1, blocking collectives: 50.8 us -> 69.5 us  [on_device(): own = lax.all_gather(gather_rows(incoming), ('quarter', 'half'))]
    ppermute x8 -> x6, starting transfers between devices: 36.1 us -> 25.1 us  [shift(): lax.ppermute(value, along, [(i, (i + distance) % parts) for i in range(pa...]
    all_to_all x0 -> x1, starting transfers between devices: none -> 7.32 us  [on_device(): incoming = lax.all_to_all(outgoing, 'x', 0, 0, tiled=True)]
    all_to_all x0 -> x1, waiting for transfers between devices: none -> 5.09 us  [on_device(): incoming = lax.all_to_all(outgoing, 'x', 0, 0, tiled=True)]
    ppermute x8 -> x6, waiting for transfers between devices: 25.3 us -> 20.6 us  [shift(): lax.ppermute(value, along, [(i, (i + distance) % parts) for i in range(pa...]
  transfers between devices with their start and end apart: 12 -> 11, of which waited for: 3 -> 6; matrix products, arithmetic and copies ran while one was open for 0% -> 0% of each run, Pallas kernels for 1% -> 1%
where the time goes in v9:
time: 186 us; the launch traced here: 185 us
  blocking collectives  90.7 us (49%)
  starting transfers between devices  43.6 us (23%)
  waiting for transfers between devices  39.8 us (21%)
  Pallas kernels  8.47 us (5%)
    all_gather x1, blocking collectives, on_device(): own = lax.all_gather(gather_rows(incoming), ('quarter', 'half'))  69.5 us
    ppermute x6, starting transfers between devices, shift(): lax.ppermute(value, along, [(i, (i + distance) % parts) for i in range(pa...  25.1 us
    all_to_all x1, blocking collectives, on_device(): blocks = lax.all_to_all(combined, 'quarter', 0, 0, tiled=True)  21.3 us
    ppermute x6, waiting for transfers between devices, shift(): lax.ppermute(value, along, [(i, (i + distance) % parts) for i in range(pa...  20.6 us
    all_to_all x1, waiting for transfers between devices, on_device(): returned = lax.all_to_all(partial_value, 'x', 0, 0, tiled=True)  14.1 us
    all_to_all x1, starting transfers between devices, on_device(): incoming = lax.all_to_all(outgoing, 'x', 0, 0, tiled=True)  7.32 us
    all_to_all x1, waiting for transfers between devices, on_device(): incoming = lax.all_to_all(outgoing, 'x', 0, 0, tiled=True)  5.09 us
    all_to_all x1, starting transfers between devices, on_device(): returned = lax.all_to_all(partial_value, 'x', 0, 0, tiled=True)  4.8 us
  transfers between devices with their start and end apart: 11, of which 6 were waited for; matrix products, arithmetic and copies ran while one was open for 0% of the time, Pallas kernels for 1%

profile of v9, /device:TPU:80, one launch (start us, length us, event | category | flops | bytes accessed | tf_op | source)
XLA Modules:
  0.0 185.0 jit_solution(8948713344102041291)
XLA Ops:
  0.0 1.8 dispatch.1
  1.8 7.3 %all-to-all-start = ((bf16[8,20,384]{2,1,0:T(8,128)(2,1)}), bf16[8,20,384]{2,1,0:T(8,128)(2,1)S(1)}, u32[]{:S(2)}, u32[]{:S(2)}) async-start(bf16[8,20,384]{2,1,0:T(8,128)(2,1)} %dispatch.1), calls=%async_computation | async-start | bytes 294912 | tf_op jit(solution)/shard_map/all_to_all | solution.py:306
  9.1 1.9 %collective-permute-start = (bf16[6144,128]{1,0:T(8,128)(2,1)}, bf16[6144,128]{1,0:T(8,128)(2,1)S(1)}, u32[]{:S(2)}, u32[]{:S(2)}) collective-permute-start(bf16[6144,128]{1,0:T(8,128)(2,1)} %param.9), channel_id=1, source_target_pairs={{0,16},{16,0},{1,17},{17,1},{2,18},{18,2},{3,19},{19,3},{4,20},{20... | collective-permute-start | bytes 4718600 | tf_op jit(solution)/shard_map/ppermute | solution.py:307
  11.1 2.4 %collective-permute-start.1 = (bf16[6144,128]{1,0:T(8,128)(2,1)}, bf16[6144,128]{1,0:T(8,128)(2,1)}, u32[]{:S(2)}, u32[]{:S(2)}) collective-permute-start(bf16[6144,128]{1,0:T(8,128)(2,1)} %param.10), channel_id=1, source_target_pairs={{0,16},{16,0},{1,17},{17,1},{2,18},{18,2},{3,19},{19,3},{4,20},{20... | collective-permute-start | bytes 4718600 | tf_op jit(solution)/shard_map/ppermute | solution.py:308
  13.5 5.1 %all-to-all-done.in_ref = bf16[8,20,384]{2,1,0:T(8,128)(2,1)S(1)} async-done(((bf16[8,20,384]{2,1,0:T(8,128)(2,1)}), bf16[8,20,384]{2,1,0:T(8,128)(2,1)S(1)}, u32[]{:S(2)}, u32[]{:S(2)}) %all-to-all-start) | async-done | bytes 122912 | tf_op jit(solution)/shard_map/all_to_all | solution.py:306
  18.6 69.5 %all-gather = bf16[1280,384]{1,0:T(8,128)(2,1)S(1)} all-gather(bf16[160,384]{1,0:T(8,128)(2,1)S(1)} %gather_rows.1), channel_id=2, replica_groups=mesh['rep'=2,'x'=8,'core'=2,'quarter'=4,'half'=2,'odd'=2] {'quarter','ha..., dimensions={0}, use_global_device_ids=true | all-gather | bytes 1105920 | tf_op jit(solution)/shard_map/all_gather | solution.py:309
  88.1 1.9 %collective-permute-start.4 = (bf16[128,6144]{1,0:T(8,128)(2,1)S(1)}, bf16[128,6144]{1,0:T(8,128)(2,1)S(1)}, u32[]{:S(2)}, u32[]{:S(2)}) collective-permute-start(bf16[128,6144]{1,0:T(8,128)(2,1)S(1)} %copy-done), channel_id=1, source_target_pairs={{0,16},{16,0},{1,17},{17,1},{2,18},{18,2},{3,19},{19,3},{4,20},{20... | collective-permute-start | bytes 4718600 | tf_op jit(solution)/shard_map/ppermute | solution.py:313
  90.2 5.1 %collective-permute-start.2 = (bf16[4,160,384]{2,1,0:T(8,128)(2,1)S(1)}, bf16[4,160,384]{2,1,0:T(8,128)(2,1)S(1)}, u32[]{:S(2)}, u32[]{:S(2)}) collective-permute-start(bf16[4,160,384]{2,1,0:T(8,128)(2,1)S(1)} %get-tuple-element.26), channel_id=1, source_target_pairs={{0,1},{1,2},{2,3},{3,4},{4,5},{5,6},{6,7},{7,8},{8,9},{9,10},{10,1... | collective-permute-start | bytes 1474568 | tf_op jit(solution)/shard_map/ppermute | solution.py:302
  95.3 4.4 %collective-permute-start.3 = (bf16[4,160,384]{2,1,0:T(8,128)(2,1)S(1)}, bf16[4,160,384]{2,1,0:T(8,128)(2,1)S(1)}, u32[]{:S(2)}, u32[]{:S(2)}) collective-permute-start(bf16[4,160,384]{2,1,0:T(8,128)(2,1)S(1)} %get-tuple-element.25), channel_id=1, source_target_pairs={{0,15},{1,0},{2,1},{3,2},{4,3},{5,4},{6,5},{7,6},{8,7},{9,8},{10,9... | collective-permute-start | bytes 1474568 | tf_op jit(solution)/shard_map/ppermute | solution.py:302
  99.7 1.4 copy-done.2
  101.2 2.2 %own_part.1.total_ref = f32[160,512]{1,0:T(8,128)S(1)} custom-call(bf16[8,160,384]{2,1,0:T(8,128)(2,1)S(1)} %bitcast.9, bf16[8,2,384,128]{3,2,1,0:T(8,128)(2,1)S(1)} %bitcast.10, bf16[8,2,384,128]{3,2,1,0:T(8,128)(2,1)S(1)} %bitcast.14, bf16[8,2,384,128]{3,2,1,0:T(8,128)(2,1)S(1)} %bitcast.12, bf16[8,2,384,128]{3,2,1,0:T(8,128)(2,1)} %bitcast.6.up2_ref), custom_call_target="tpu_custom_call" | custom-call | flops 503316480 | bytes 4200000 | tf_op jit(solution)/shard_map/own_part/pallas_call | solution.py:155
  103.4 6.3 %collective-permute-done.2.left_ref = bf16[4,160,384]{2,1,0:T(8,128)(2,1)S(1)} collective-permute-done((bf16[4,160,384]{2,1,0:T(8,128)(2,1)S(1)}, bf16[4,160,384]{2,1,0:T(8,128)(2,1)S(1)}, u32[]{:S(2)}, u32[]{:S(2)}) %collective-permute-start.2) | collective-permute-done | bytes 491552 | tf_op jit(solution)/shard_map/ppermute | solution.py:302
  109.6 1.2 collective-permute-done.3.right_ref
  110.8 2.6 %ffn.1 = (bf16[160,256]{1,0:T(8,128)(2,1)S(1)}, bf16[4,160,384]{2,1,0:T(8,128)(2,1)S(1)}, bf16[4,160,384]{2,1,0:T(8,128)(2,1)S(1)}, bf16[2,160,384]{2,1,0:T(8,128)(2,1)S(1)}, bf16[2,160,384]{2,1,0:T(8,128)(2,1)S(1)}) custom-call(f32[160,512]{1,0:T(8,128)S(1)} %own_part.1.total_ref, bf16[4,160,384]{2,1,0:T(8,128)(2,1)S(1)} %collective-permute-done.2.left_ref, ...), custom_call_target="tpu_custom_call" | custom-call | flops 1006632960 | bytes 9000000 | tf_op jit(solution)/shard_map/ffn/pallas_call | solution.py:205
  113.4 3.2 %collective-permute-start.5 = (bf16[4,160,384]{2,1,0:T(8,128)(2,1)S(1)}, bf16[4,160,384]{2,1,0:T(8,128)(2,1)S(1)}, u32[]{:S(2)}, u32[]{:S(2)}) collective-permute-start(bf16[4,160,384]{2,1,0:T(8,128)(2,1)S(1)} %get-tuple-element.21), channel_id=1, source_target_pairs={{0,1},{1,2},{2,3},{3,4},{4,5},{5,6},{6,7},{7,8},{8,9},{9,10},{10,1... | collective-permute-start | bytes 1474568 | tf_op jit(solution)/shard_map/ppermute | solution.py:302
  116.7 4.4 %collective-permute-start.6 = (bf16[4,160,384]{2,1,0:T(8,128)(2,1)S(1)}, bf16[4,160,384]{2,1,0:T(8,128)(2,1)S(1)}, u32[]{:S(2)}, u32[]{:S(2)}) collective-permute-start(bf16[4,160,384]{2,1,0:T(8,128)(2,1)S(1)} %get-tuple-element.22), channel_id=1, source_target_pairs={{0,15},{1,0},{2,1},{3,2},{4,3},{5,4},{6,5},{7,6},{8,7},{9,8},{10,9... | collective-permute-start | bytes 1474568 | tf_op jit(solution)/shard_map/ppermute | solution.py:302
  121.0 2.7 %collective-permute-start.7 = (bf16[2,160,384]{2,1,0:T(8,128)(2,1)S(1)}, bf16[2,160,384]{2,1,0:T(8,128)(2,1)S(1)}, u32[]{:S(2)}, u32[]{:S(2)}) collective-permute-start(bf16[2,160,384]{2,1,0:T(8,128)(2,1)S(1)} %get-tuple-element.23), channel_id=1, source_target_pairs={{0,2},{1,3},{2,4},{3,5},{4,6},{5,7},{6,8},{7,9},{8,10},{9,11},{10,... | collective-permute-start | bytes 737288 | tf_op jit(solution)/shard_map/ppermute | solution.py:302
  123.8 5.3 %collective-permute-start.8 = (bf16[2,160,384]{2,1,0:T(8,128)(2,1)S(1)}, bf16[2,160,384]{2,1,0:T(8,128)(2,1)S(1)}, u32[]{:S(2)}, u32[]{:S(2)}) collective-permute-start(bf16[2,160,384]{2,1,0:T(8,128)(2,1)S(1)} %get-tuple-element.24), channel_id=1, source_target_pairs={{0,14},{1,15},{2,0},{3,1},{4,2},{5,3},{6,4},{7,5},{8,6},{9,7},{10,... | collective-permute-start | bytes 737288 | tf_op jit(solution)/shard_map/ppermute | solution.py:302
  129.4 12.4 %collective-permute-done.7.left2_ref = bf16[2,160,384]{2,1,0:T(8,128)(2,1)S(1)} collective-permute-done((bf16[2,160,384]{2,1,0:T(8,128)(2,1)S(1)}, bf16[2,160,384]{2,1,0:T(8,128)(2,1)S(1)}, u32[]{:S(2)}, u32[]{:S(2)}) %collective-permute-start.7) | collective-permute-done | bytes 245792 | tf_op jit(solution)/shard_map/ppermute | solution.py:302
  141.8 0.7 collective-permute-done.8.right2_ref
  142.5 1.0 join.1
  143.6 4.8 %all-to-all-start.1 = ((bf16[8,80,384]{2,1,0:T(8,128)(2,1)}), bf16[8,80,384]{2,1,0:T(8,128)(2,1)S(1)}, u32[]{:S(2)}, u32[]{:S(2)}) async-start(bf16[8,80,384]{2,1,0:T(8,128)(2,1)} %join.1), calls=%async_computation.1 | async-start | bytes 983040 | tf_op jit(solution)/shard_map/all_to_all | solution.py:320
  148.8 14.1 %all-to-all-done.1 = bf16[8,80,384]{2,1,0:T(8,128)(2,1)S(1)} async-done(((bf16[8,80,384]{2,1,0:T(8,128)(2,1)}), bf16[8,80,384]{2,1,0:T(8,128)(2,1)S(1)}, u32[]{:S(2)}, u32[]{:S(2)}) %all-to-all-start.1) | async-done | bytes 491552 | tf_op jit(solution)/shard_map/all_to_all | solution.py:320
  163.1 21.3 %all_to_all.15 = bf16[4,32,384]{2,1,0:T(8,128)(2,1)S(1)} all-to-all(bf16[4,32,384]{2,1,0:T(8,128)(2,1)S(1)} %combine.1), channel_id=1, replica_groups=mesh['rep'=2,'x'=8,'core'=2,'quarter'=4,'half'=2,'odd'=2] {'quarter'}, dimensions={0} | all-to-all | bytes 196608 | tf_op jit(solution)/shard_map/all_to_all | solution.py:323
  (26 shorter events, 1.8 us)
Async XLA Ops:
  0.0 88.1 %copy-start = (bf16[128,6144]{1,0:T(8,128)(2,1)S(1)}, bf16[128,6144]{1,0:T(8,128)(2,1)}, u32[]{:S(2)}) copy-start(bf16[128,6144]{1,0:T(8,128)(2,1)} %down_ref.1) | copy-start | bytes 4718596
  1.8 16.8 %all-to-all-start = ((bf16[8,20,384]{2,1,0:T(8,128)(2,1)}), bf16[8,20,384]{2,1,0:T(8,128)(2,1)S(1)}, u32[]{:S(2)}, u32[]{:S(2)}) async-start(bf16[8,20,384]{2,1,0:T(8,128)(2,1)} %dispatch.1), calls=%async_computation | async-start | bytes 294912 | tf_op jit(solution)/shard_map/all_to_all | solution.py:306
  9.1 90.6 %collective-permute-start = (bf16[6144,128]{1,0:T(8,128)(2,1)}, bf16[6144,128]{1,0:T(8,128)(2,1)S(1)}, u32[]{:S(2)}, u32[]{:S(2)}) collective-permute-start(bf16[6144,128]{1,0:T(8,128)(2,1)} %param.9), channel_id=1, source_target_pairs={{0,16},{16,0},{1,17},{17,1},{2,18},{18,2},{3,19},{19,3},{4,20},{20... | collective-permute-start | bytes 4718600 | tf_op jit(solution)/shard_map/ppermute | solution.py:307
  11.1 88.7 %collective-permute-start.1 = (bf16[6144,128]{1,0:T(8,128)(2,1)}, bf16[6144,128]{1,0:T(8,128)(2,1)}, u32[]{:S(2)}, u32[]{:S(2)}) collective-permute-start(bf16[6144,128]{1,0:T(8,128)(2,1)} %param.10), channel_id=1, source_target_pairs={{0,16},{16,0},{1,17},{17,1},{2,18},{18,2},{3,19},{19,3},{4,20},{20... | collective-permute-start | bytes 4718600 | tf_op jit(solution)/shard_map/ppermute | solution.py:308
  18.6 81.1 %copy-start.1 = (bf16[6144,128]{1,0:T(8,128)(2,1)S(1)}, bf16[6144,128]{1,0:T(8,128)(2,1)}, u32[]{:S(2)}) copy-start(bf16[6144,128]{1,0:T(8,128)(2,1)} %param.9) | copy-start | bytes 4718596
  88.1 22.7 %collective-permute-start.4 = (bf16[128,6144]{1,0:T(8,128)(2,1)S(1)}, bf16[128,6144]{1,0:T(8,128)(2,1)S(1)}, u32[]{:S(2)}, u32[]{:S(2)}) collective-permute-start(bf16[128,6144]{1,0:T(8,128)(2,1)S(1)} %copy-done), channel_id=1, source_target_pairs={{0,16},{16,0},{1,17},{17,1},{2,18},{18,2},{3,19},{19,3},{4,20},{20... | collective-permute-start | bytes 4718600 | tf_op jit(solution)/shard_map/ppermute | solution.py:313
  90.2 19.5 %collective-permute-start.2 = (bf16[4,160,384]{2,1,0:T(8,128)(2,1)S(1)}, bf16[4,160,384]{2,1,0:T(8,128)(2,1)S(1)}, u32[]{:S(2)}, u32[]{:S(2)}) collective-permute-start(bf16[4,160,384]{2,1,0:T(8,128)(2,1)S(1)} %get-tuple-element.26), channel_id=1, source_target_pairs={{0,1},{1,2},{2,3},{3,4},{4,5},{5,6},{6,7},{7,8},{8,9},{9,10},{10,1... | collective-permute-start | bytes 1474568 | tf_op jit(solution)/shard_map/ppermute | solution.py:302
  95.3 15.6 %collective-permute-start.3 = (bf16[4,160,384]{2,1,0:T(8,128)(2,1)S(1)}, bf16[4,160,384]{2,1,0:T(8,128)(2,1)S(1)}, u32[]{:S(2)}, u32[]{:S(2)}) collective-permute-start(bf16[4,160,384]{2,1,0:T(8,128)(2,1)S(1)} %get-tuple-element.25), channel_id=1, source_target_pairs={{0,15},{1,0},{2,1},{3,2},{4,3},{5,4},{6,5},{7,6},{8,7},{9,8},{10,9... | collective-permute-start | bytes 1474568 | tf_op jit(solution)/shard_map/ppermute | solution.py:302
  99.7 1.4 copy-start.2
  101.1 9.7 %copy-start.3 = (bf16[6144,128]{1,0:T(8,128)(2,1)S(1)}, bf16[6144,128]{1,0:T(8,128)(2,1)}, u32[]{:S(2)}) copy-start(bf16[6144,128]{1,0:T(8,128)(2,1)} %param.10) | copy-start | bytes 4718596
  113.4 29.1 %collective-permute-start.5 = (bf16[4,160,384]{2,1,0:T(8,128)(2,1)S(1)}, bf16[4,160,384]{2,1,0:T(8,128)(2,1)S(1)}, u32[]{:S(2)}, u32[]{:S(2)}) collective-permute-start(bf16[4,160,384]{2,1,0:T(8,128)(2,1)S(1)} %get-tuple-element.21), channel_id=1, source_target_pairs={{0,1},{1,2},{2,3},{3,4},{4,5},{5,6},{6,7},{7,8},{8,9},{9,10},{10,1... | collective-permute-start | bytes 1474568 | tf_op jit(solution)/shard_map/ppermute | solution.py:302
  116.7 25.9 %collective-permute-start.6 = (bf16[4,160,384]{2,1,0:T(8,128)(2,1)S(1)}, bf16[4,160,384]{2,1,0:T(8,128)(2,1)S(1)}, u32[]{:S(2)}, u32[]{:S(2)}) collective-permute-start(bf16[4,160,384]{2,1,0:T(8,128)(2,1)S(1)} %get-tuple-element.22), channel_id=1, source_target_pairs={{0,15},{1,0},{2,1},{3,2},{4,3},{5,4},{6,5},{7,6},{8,7},{9,8},{10,9... | collective-permute-start | bytes 1474568 | tf_op jit(solution)/shard_map/ppermute | solution.py:302
  121.0 20.8 %collective-permute-start.7 = (bf16[2,160,384]{2,1,0:T(8,128)(2,1)S(1)}, bf16[2,160,384]{2,1,0:T(8,128)(2,1)S(1)}, u32[]{:S(2)}, u32[]{:S(2)}) collective-permute-start(bf16[2,160,384]{2,1,0:T(8,128)(2,1)S(1)} %get-tuple-element.23), channel_id=1, source_target_pairs={{0,2},{1,3},{2,4},{3,5},{4,6},{5,7},{6,8},{7,9},{8,10},{9,11},{10,... | collective-permute-start | bytes 737288 | tf_op jit(solution)/shard_map/ppermute | solution.py:302
  123.8 18.8 %collective-permute-start.8 = (bf16[2,160,384]{2,1,0:T(8,128)(2,1)S(1)}, bf16[2,160,384]{2,1,0:T(8,128)(2,1)S(1)}, u32[]{:S(2)}, u32[]{:S(2)}) collective-permute-start(bf16[2,160,384]{2,1,0:T(8,128)(2,1)S(1)} %get-tuple-element.24), channel_id=1, source_target_pairs={{0,14},{1,15},{2,0},{3,1},{4,2},{5,3},{6,4},{7,5},{8,6},{9,7},{10,... | collective-permute-start | bytes 737288 | tf_op jit(solution)/shard_map/ppermute | solution.py:302
  129.4 19.0 %copy-start.4 = (s32[32,2]{0,1:T(2,128)S(1)}, s32[32,2]{0,1:T(2,128)}, u32[]{:S(2)}) copy-start(s32[32,2]{0,1:T(2,128)} %param.7) | copy-start | bytes 772
  129.4 19.0 %copy-start.5 = (f32[32,2]{0,1:T(2,128)S(1)}, f32[32,2]{0,1:T(2,128)}, u32[]{:S(2)}) copy-start(f32[32,2]{0,1:T(2,128)} %param.8) | copy-start | bytes 772
  143.6 19.3 %all-to-all-start.1 = ((bf16[8,80,384]{2,1,0:T(8,128)(2,1)}), bf16[8,80,384]{2,1,0:T(8,128)(2,1)S(1)}, u32[]{:S(2)}, u32[]{:S(2)}) async-start(bf16[8,80,384]{2,1,0:T(8,128)(2,1)} %join.1), calls=%async_computation.1 | async-start | bytes 983040 | tf_op jit(solution)/shard_map/all_to_all | solution.py:320

commit v10 on v5

--- a/solution.py
+++ b/solution.py
@@ -123,7 +123,9 @@
 
 
 def side_by_side(refs, b, parity):
-    return jnp.concatenate([ref[b, parity] for ref in refs], axis=1)
+    return jnp.concatenate(
+        [ref[b, parity if ref.shape[1] > 1 else 0] for ref in refs], axis=1
+    )
 
 
 def multiply(total, tokens, refs, parity, start):
@@ -138,9 +140,12 @@
     return total
 
 
-def own_kernel(slots_ref, gate_ref, gate2_ref, up_ref, up2_ref, out_ref):
+def own_kernel(slots_ref, gate_ref, gate2_ref, up_ref, up2_ref, out_ref, rest_ref):
     refs = (gate_ref, gate2_ref, up_ref, up2_ref)
-    out_ref[...] = multiply(None, slots_ref, refs, lax.axis_index("odd"), 0)
+    parity = lax.axis_index("odd")
+    out_ref[...] = multiply(None, slots_ref, refs, parity, 0)
+    for b in range(slots_ref.shape[0]):
+        rest_ref[b, 0] = up2_ref[b, 1 - parity]
 
 
 def own_part(slots, *weights):
@@ -148,7 +153,10 @@
     width = weights[0].shape[-1]
     return pl.pallas_call(
         own_kernel,
-        out_shape=jax.ShapeDtypeStruct((rows, 4 * width), jnp.float32),
+        out_shape=(
+            jax.ShapeDtypeStruct((rows, 4 * width), jnp.float32),
+            jax.ShapeDtypeStruct((pairs, 1, depth, width), jnp.bfloat16),
+        ),
         cost_estimate=cost(2 * pairs * rows * depth * 4 * width, 4200000),
         compiler_params=pltpu.CompilerParams(vmem_limit_bytes=16 << 20),
         name="own_part",
@@ -294,8 +302,8 @@
     left = lax.ppermute(own[: pairs // 2], along, up_z)
     right = lax.ppermute(own[pairs // 2 :], along, down_z)
     blocks = [w.reshape(pairs, 2, depth, w.shape[1]) for w in (gate, gate2, up, up2)]
-    total = own_part(own, *blocks)
-    hidden, to_right, to_left = ffn(total, left, right, *blocks, down, down2)
+    total, rest = own_part(own, *blocks)
+    hidden, to_right, to_left = ffn(total, left, right, *blocks[:3], rest, down, down2)
     from_left = lax.ppermute(to_right, along, up_z)
     from_right = lax.ppermute(to_left, along, down_z)
     partial_value = join(own_down(hidden, down, down2, pairs), from_left, from_right, chips)

time: 177 us -> 177 us (level)
  no operation moved by 1% of the time
where the time goes in v10:
time: 177 us
  blocking collectives  109 us (62%)
  waiting for transfers between devices  31.9 us (18%)
  starting transfers between devices  29 us (16%)
  Pallas kernels  5.66 us (3%)
    all_gather x1, blocking collectives, on_device(): own = lax.all_gather(gather_rows(incoming), 'pair')  68.7 us
    all_to_all x1, blocking collectives, on_device(): blocks = lax.all_to_all(combined, 'pair', 0, 0, tiled=True)  22.9 us
    all_to_all x1, waiting for transfers between devices, on_device(): returned = lax.all_to_all(partial_value, 'x', 0, 0, tiled=True)  19.1 us
    all_to_all x1, blocking collectives, on_device(): incoming = lax.all_to_all(outgoing, 'x', 0, 0, tiled=True)  17.4 us
    ppermute x1, starting transfers between devices, on_device(): left = lax.ppermute(own[:pairs // 2], along, up_z)  6.17 us
    ppermute x1, starting transfers between devices, on_device(): right = lax.ppermute(own[pairs // 2:], along, down_z)  5.05 us
    ppermute x1, waiting for transfers between devices, on_device(): from_left = lax.ppermute(to_right, along, up_z)  4.38 us
    ppermute x1, starting transfers between devices, on_device(): from_left = lax.ppermute(to_right, along, up_z)  4.2 us
  transfers between devices with their start and end apart: 8, of which 5 were waited for; matrix products, arithmetic and copies ran while one was open for 0% of the time, Pallas kernels for 1%

profile of v10, /device:TPU:80, one launch (start us, length us, event | category | flops | bytes accessed | tf_op | source)
XLA Modules:
  0.0 176.7 jit_solution(12844065045184031142)
XLA Ops:
  0.0 1.7 dispatch.1
  1.7 1.9 %collective-permute-start = (bf16[6144,128]{1,0:T(8,128)(2,1)}, bf16[6144,128]{1,0:T(8,128)(2,1)S(1)}, u32[]{:S(2)}, u32[]{:S(2)}) collective-permute-start(bf16[6144,128]{1,0:T(8,128)(2,1)} %param.9), channel_id=1, source_target_pairs={{0,16},{16,0},{1,17},{17,1},{2,18},{18,2},{3,19},{19,3},{4,20},{20... | collective-permute-start | bytes 4718600 | tf_op jit(solution)/shard_map/ppermute | solution.py:298
  3.6 2.4 %collective-permute-start.1 = (bf16[6144,128]{1,0:T(8,128)(2,1)}, bf16[6144,128]{1,0:T(8,128)(2,1)S(1)}, u32[]{:S(2)}, u32[]{:S(2)}) collective-permute-start(bf16[6144,128]{1,0:T(8,128)(2,1)} %param.10), channel_id=1, source_target_pairs={{0,16},{16,0},{1,17},{17,1},{2,18},{18,2},{3,19},{19,3},{4,20},{20... | collective-permute-start | bytes 4718600 | tf_op jit(solution)/shard_map/ppermute | solution.py:299
  6.1 2.0 %collective-permute-start.4 = (bf16[128,6144]{1,0:T(8,128)(2,1)}, bf16[128,6144]{1,0:T(8,128)(2,1)S(1)}, u32[]{:S(2)}, u32[]{:S(2)}) collective-permute-start(bf16[128,6144]{1,0:T(8,128)(2,1)} %down_ref.1), channel_id=1, source_target_pairs={{0,16},{16,0},{1,17},{17,1},{2,18},{18,2},{3,19},{19,3},{4,20},{20... | collective-permute-start | bytes 4718600 | tf_op jit(solution)/shard_map/ppermute | solution.py:300
  8.0 17.4 %all_to_all.15.in_ref = bf16[8,20,384]{2,1,0:T(8,128)(2,1)S(1)} all-to-all(bf16[8,20,384]{2,1,0:T(8,128)(2,1)} %dispatch.1), channel_id=1, replica_groups=mesh['rep'=2,'x'=8,'core'=2,'pair'=8,'odd'=2] {'x'}, dimensions={0} | all-to-all | bytes 245760 | tf_op jit(solution)/shard_map/all_to_all | solution.py:297
  25.5 68.7 %all-gather = bf16[1280,384]{1,0:T(8,128)(2,1)S(1)} all-gather(bf16[160,384]{1,0:T(8,128)(2,1)S(1)} %gather_rows.1), channel_id=2, replica_groups=mesh['rep'=2,'x'=8,'core'=2,'pair'=8,'odd'=2] {'pair'}, dimensions={0}, use_global_device_ids=true | all-gather | bytes 1105920 | tf_op jit(solution)/shard_map/all_gather | solution.py:301
  94.3 6.2 %collective-permute-start.2 = (bf16[4,160,384]{2,1,0:T(8,128)(2,1)S(1)}, bf16[4,160,384]{2,1,0:T(8,128)(2,1)S(1)}, u32[]{:S(2)}, u32[]{:S(2)}) collective-permute-start(bf16[4,160,384]{2,1,0:T(8,128)(2,1)S(1)} %bitcast.20), channel_id=1, source_target_pairs={{0,1},{1,2},{2,3},{3,4},{4,5},{5,6},{6,7},{7,8},{8,9},{9,10},{10,1... | collective-permute-start | bytes 1474568 | tf_op jit(solution)/shard_map/ppermute | solution.py:302
  100.5 5.1 %collective-permute-start.3 = (bf16[4,160,384]{2,1,0:T(8,128)(2,1)S(1)}, bf16[4,160,384]{2,1,0:T(8,128)(2,1)S(1)}, u32[]{:S(2)}, u32[]{:S(2)}) collective-permute-start(bf16[4,160,384]{2,1,0:T(8,128)(2,1)S(1)} %bitcast.19), channel_id=1, source_target_pairs={{1,0},{2,1},{3,2},{4,3},{5,4},{6,5},{7,6},{8,7},{9,8},{10,9},{11,1... | collective-permute-start | bytes 1474568 | tf_op jit(solution)/shard_map/ppermute | solution.py:303
  105.6 0.7 own_part.1
  106.3 4.0 %collective-permute-done.2.left_ref = bf16[4,160,384]{2,1,0:T(8,128)(2,1)S(1)} collective-permute-done((bf16[4,160,384]{2,1,0:T(8,128)(2,1)S(1)}, bf16[4,160,384]{2,1,0:T(8,128)(2,1)S(1)}, u32[]{:S(2)}, u32[]{:S(2)}) %collective-permute-start.2) | collective-permute-done | bytes 491552 | tf_op jit(solution)/shard_map/ppermute | solution.py:302
  110.4 1.5 collective-permute-done.3.right_ref
  111.9 1.1 ffn.1
  113.0 4.2 %collective-permute-start.5 = (bf16[4,160,384]{2,1,0:T(8,128)(2,1)S(1)}, bf16[4,160,384]{2,1,0:T(8,128)(2,1)S(1)}, u32[]{:S(2)}, u32[]{:S(2)}) collective-permute-start(bf16[4,160,384]{2,1,0:T(8,128)(2,1)S(1)} %get-tuple-element.21), channel_id=1, source_target_pairs={{0,1},{1,2},{2,3},{3,4},{4,5},{5,6},{6,7},{7,8},{8,9},{9,10},{10,1... | collective-permute-start | bytes 1474568 | tf_op jit(solution)/shard_map/ppermute | solution.py:307
  117.2 3.4 %collective-permute-start.6 = (bf16[4,160,384]{2,1,0:T(8,128)(2,1)S(1)}, bf16[4,160,384]{2,1,0:T(8,128)(2,1)S(1)}, u32[]{:S(2)}, u32[]{:S(2)}) collective-permute-start(bf16[4,160,384]{2,1,0:T(8,128)(2,1)S(1)} %get-tuple-element.22), channel_id=1, source_target_pairs={{1,0},{2,1},{3,2},{4,3},{5,4},{6,5},{7,6},{8,7},{9,8},{10,9},{11,1... | collective-permute-start | bytes 1474568 | tf_op jit(solution)/shard_map/ppermute | solution.py:308
  120.5 0.4 own_down.1.own_ref
  121.0 4.4 %collective-permute-done.5.left_ref = bf16[4,160,384]{2,1,0:T(8,128)(2,1)S(1)} collective-permute-done((bf16[4,160,384]{2,1,0:T(8,128)(2,1)S(1)}, bf16[4,160,384]{2,1,0:T(8,128)(2,1)S(1)}, u32[]{:S(2)}, u32[]{:S(2)}) %collective-permute-start.5) | collective-permute-done | bytes 491552 | tf_op jit(solution)/shard_map/ppermute | solution.py:307
  125.4 2.9 %collective-permute-done.6.right_ref = bf16[4,160,384]{2,1,0:T(8,128)(2,1)S(1)} collective-permute-done((bf16[4,160,384]{2,1,0:T(8,128)(2,1)S(1)}, bf16[4,160,384]{2,1,0:T(8,128)(2,1)S(1)}, u32[]{:S(2)}, u32[]{:S(2)}) %collective-permute-start.6) | collective-permute-done | bytes 491552 | tf_op jit(solution)/shard_map/ppermute | solution.py:308
  128.2 1.1 join.1
  129.4 3.9 %all-to-all-start.1 = ((bf16[8,80,768]{2,1,0:T(8,128)(2,1)}), bf16[8,80,768]{2,1,0:T(8,128)(2,1)S(1)}, u32[]{:S(2)}, u32[]{:S(2)}) async-start(bf16[8,80,768]{2,1,0:T(8,128)(2,1)} %join.1), calls=%async_computation.1 | async-start | bytes 1966080 | tf_op jit(solution)/shard_map/all_to_all | solution.py:310
  133.5 0.2 mixing.1.mix_ref
  133.7 19.1 %all-to-all-done.1 = bf16[8,80,768]{2,1,0:T(8,128)(2,1)S(1)} async-done(((bf16[8,80,768]{2,1,0:T(8,128)(2,1)}), bf16[8,80,768]{2,1,0:T(8,128)(2,1)S(1)}, u32[]{:S(2)}, u32[]{:S(2)}) %all-to-all-start.1) | async-done | bytes 983072 | tf_op jit(solution)/shard_map/all_to_all | solution.py:310
  152.8 0.4 combine.1
  153.2 22.9 %all_to_all.16 = bf16[8,32,384]{2,1,0:T(8,128)(2,1)S(1)} all-to-all(bf16[8,32,384]{2,1,0:T(8,128)(2,1)S(1)} %combine.1), channel_id=1, replica_groups=mesh['rep'=2,'x'=8,'core'=2,'pair'=8,'odd'=2] {'pair'}, dimensions={0} | all-to-all | bytes 393216 | tf_op jit(solution)/shard_map/all_to_all | solution.py:314
  176.1 0.6 reduce_sum.12
  (19 shorter events, 0.3 us)
Async XLA Ops:
  1.7 103.9 %collective-permute-start = (bf16[6144,128]{1,0:T(8,128)(2,1)}, bf16[6144,128]{1,0:T(8,128)(2,1)S(1)}, u32[]{:S(2)}, u32[]{:S(2)}) collective-permute-start(bf16[6144,128]{1,0:T(8,128)(2,1)} %param.9), channel_id=1, source_target_pairs={{0,16},{16,0},{1,17},{17,1},{2,18},{18,2},{3,19},{19,3},{4,20},{20... | collective-permute-start | bytes 4718600 | tf_op jit(solution)/shard_map/ppermute | solution.py:298
  3.6 101.9 %collective-permute-start.1 = (bf16[6144,128]{1,0:T(8,128)(2,1)}, bf16[6144,128]{1,0:T(8,128)(2,1)S(1)}, u32[]{:S(2)}, u32[]{:S(2)}) collective-permute-start(bf16[6144,128]{1,0:T(8,128)(2,1)} %param.10), channel_id=1, source_target_pairs={{0,16},{16,0},{1,17},{17,1},{2,18},{18,2},{3,19},{19,3},{4,20},{20... | collective-permute-start | bytes 4718600 | tf_op jit(solution)/shard_map/ppermute | solution.py:299
  6.1 105.8 %collective-permute-start.4 = (bf16[128,6144]{1,0:T(8,128)(2,1)}, bf16[128,6144]{1,0:T(8,128)(2,1)S(1)}, u32[]{:S(2)}, u32[]{:S(2)}) collective-permute-start(bf16[128,6144]{1,0:T(8,128)(2,1)} %down_ref.1), channel_id=1, source_target_pairs={{0,16},{16,0},{1,17},{17,1},{2,18},{18,2},{3,19},{19,3},{4,20},{20... | collective-permute-start | bytes 4718600 | tf_op jit(solution)/shard_map/ppermute | solution.py:300
  25.5 80.1 %copy-start.1 = (bf16[6144,128]{1,0:T(8,128)(2,1)S(1)}, bf16[6144,128]{1,0:T(8,128)(2,1)}, u32[]{:S(2)}) copy-start(bf16[6144,128]{1,0:T(8,128)(2,1)} %param.10) | copy-start | bytes 4718596
  25.5 80.1 %copy-start = (bf16[6144,128]{1,0:T(8,128)(2,1)S(1)}, bf16[6144,128]{1,0:T(8,128)(2,1)}, u32[]{:S(2)}) copy-start(bf16[6144,128]{1,0:T(8,128)(2,1)} %param.9) | copy-start | bytes 4718596
  94.3 16.1 %collective-permute-start.2 = (bf16[4,160,384]{2,1,0:T(8,128)(2,1)S(1)}, bf16[4,160,384]{2,1,0:T(8,128)(2,1)S(1)}, u32[]{:S(2)}, u32[]{:S(2)}) collective-permute-start(bf16[4,160,384]{2,1,0:T(8,128)(2,1)S(1)} %bitcast.20), channel_id=1, source_target_pairs={{0,1},{1,2},{2,3},{3,4},{4,5},{5,6},{6,7},{7,8},{8,9},{9,10},{10,1... | collective-permute-start | bytes 1474568 | tf_op jit(solution)/shard_map/ppermute | solution.py:302
  100.5 11.4 %collective-permute-start.3 = (bf16[4,160,384]{2,1,0:T(8,128)(2,1)S(1)}, bf16[4,160,384]{2,1,0:T(8,128)(2,1)S(1)}, u32[]{:S(2)}, u32[]{:S(2)}) collective-permute-start(bf16[4,160,384]{2,1,0:T(8,128)(2,1)S(1)} %bitcast.19), channel_id=1, source_target_pairs={{1,0},{2,1},{3,2},{4,3},{5,4},{6,5},{7,6},{8,7},{9,8},{10,9},{11,1... | collective-permute-start | bytes 1474568 | tf_op jit(solution)/shard_map/ppermute | solution.py:303
  105.6 6.3 %copy-start.2 = (bf16[128,6144]{1,0:T(8,128)(2,1)S(1)}, bf16[128,6144]{1,0:T(8,128)(2,1)}, u32[]{:S(2)}) copy-start(bf16[128,6144]{1,0:T(8,128)(2,1)} %down_ref.1) | copy-start | bytes 4718596
  113.0 12.4 %collective-permute-start.5 = (bf16[4,160,384]{2,1,0:T(8,128)(2,1)S(1)}, bf16[4,160,384]{2,1,0:T(8,128)(2,1)S(1)}, u32[]{:S(2)}, u32[]{:S(2)}) collective-permute-start(bf16[4,160,384]{2,1,0:T(8,128)(2,1)S(1)} %get-tuple-element.21), channel_id=1, source_target_pairs={{0,1},{1,2},{2,3},{3,4},{4,5},{5,6},{6,7},{7,8},{8,9},{9,10},{10,1... | collective-permute-start | bytes 1474568 | tf_op jit(solution)/shard_map/ppermute | solution.py:307
  117.2 11.1 %collective-permute-start.6 = (bf16[4,160,384]{2,1,0:T(8,128)(2,1)S(1)}, bf16[4,160,384]{2,1,0:T(8,128)(2,1)S(1)}, u32[]{:S(2)}, u32[]{:S(2)}) collective-permute-start(bf16[4,160,384]{2,1,0:T(8,128)(2,1)S(1)} %get-tuple-element.22), channel_id=1, source_target_pairs={{1,0},{2,1},{3,2},{4,3},{5,4},{6,5},{7,6},{8,7},{9,8},{10,9},{11,1... | collective-permute-start | bytes 1474568 | tf_op jit(solution)/shard_map/ppermute | solution.py:308
  129.4 3.9 %copy-start.3 = (s32[32,2]{0,1:T(2,128)S(1)}, s32[32,2]{0,1:T(2,128)}, u32[]{:S(2)}) copy-start(s32[32,2]{0,1:T(2,128)} %param.7) | copy-start | bytes 772
  129.4 4.0 %copy-start.4 = (f32[32,2]{0,1:T(2,128)S(1)}, f32[32,2]{0,1:T(2,128)}, u32[]{:S(2)}) copy-start(f32[32,2]{0,1:T(2,128)} %param.8) | copy-start | bytes 772
  129.4 23.5 %all-to-all-start.1 = ((bf16[8,80,768]{2,1,0:T(8,128)(2,1)}), bf16[8,80,768]{2,1,0:T(8,128)(2,1)S(1)}, u32[]{:S(2)}, u32[]{:S(2)}) async-start(bf16[8,80,768]{2,1,0:T(8,128)(2,1)} %join.1), calls=%async_computation.1 | async-start | bytes 1966080 | tf_op jit(solution)/shard_map/all_to_all | solution.py:310

commit v11 on v9

--- a/solution.py
+++ b/solution.py
@@ -129,7 +129,9 @@
 
 
 def side_by_side(refs, b, parity):
-    return jnp.concatenate([ref[b, parity] for ref in refs], axis=1)
+    return jnp.concatenate(
+        [ref[b, parity if ref.shape[1] > 1 else 0] for ref in refs], axis=1
+    )
 
 
 def multiply(total, tokens, refs, parity, start):
@@ -144,9 +146,12 @@
     return total
 
 
-def own_kernel(slots_ref, gate_ref, gate2_ref, up_ref, up2_ref, out_ref):
+def own_kernel(slots_ref, gate_ref, gate2_ref, up_ref, up2_ref, out_ref, rest_ref):
     refs = (gate_ref, gate2_ref, up_ref, up2_ref)
-    out_ref[...] = multiply(None, slots_ref, refs, lax.axis_index("odd"), 0)
+    parity = lax.axis_index("odd")
+    out_ref[...] = multiply(None, slots_ref, refs, parity, 0)
+    for b in range(slots_ref.shape[0]):
+        rest_ref[b, 0] = up2_ref[b, 1 - parity]
 
 
 def own_part(slots, *weights):
@@ -154,7 +159,10 @@
     width = weights[0].shape[-1]
     return pl.pallas_call(
         own_kernel,
-        out_shape=jax.ShapeDtypeStruct((rows, 4 * width), jnp.float32),
+        out_shape=(
+            jax.ShapeDtypeStruct((rows, 4 * width), jnp.float32),
+            jax.ShapeDtypeStruct((pairs, 1, depth, width), jnp.bfloat16),
+        ),
         cost_estimate=cost(2 * pairs * rows * depth * 4 * width, 4200000),
         compiler_params=pltpu.CompilerParams(vmem_limit_bytes=16 << 20),
         name="own_part",
@@ -302,18 +310,20 @@
         return lax.ppermute(value, along, [(i, (i + distance) % parts) for i in range(parts)])
 
     outgoing = dispatch(ids, tokens, chips)
-    gate, up, outgoing = lax.optimization_barrier((gate_weight, up_weight, outgoing))
+    gate, up, down, outgoing = lax.optimization_barrier(
+        (gate_weight, up_weight, down_weight, outgoing)
+    )
     incoming = lax.all_to_all(outgoing, "x", 0, 0, tiled=True)
     gate2 = lax.ppermute(gate, "core", swap)
     up2 = lax.ppermute(up, "core", swap)
+    down2 = lax.ppermute(down, "core", swap)
     own = lax.all_gather(gather_rows(incoming), ("quarter", "half"))
-    down, own = lax.optimization_barrier((down_weight, own))
-    left = shift(own[: pairs // 2], 1)
-    right = shift(own[pairs // 2 :], -1)
-    down2 = lax.ppermute(down, "core", swap)
+    left, right = shift(own[: pairs // 2], 1), shift(own[pairs // 2 :], -1)
     blocks = [w.reshape(pairs, 2, depth, w.shape[1]) for w in (gate, gate2, up, up2)]
-    total = own_part(own, *blocks)
-    hidden, to_right, to_left, to_right2, to_left2 = ffn(total, left, right, *blocks, down, down2)
+    total, rest = own_part(own, *blocks)
+    hidden, to_right, to_left, to_right2, to_left2 = ffn(
+        total, left, right, *blocks[:3], rest, down, down2
+    )
     left, right = shift(to_right, 1), shift(to_left, -1)
     left2, right2 = shift(to_right2, 2), shift(to_left2, -2)
     partial_value = join(own_down(hidden, down, down2), left, right, left2, right2, chips)

time: 186 us -> 176 us (0.946)
  waiting for transfers between devices: 39.8 us -> 25.6 us
  blocking collectives: 90.7 us -> 104 us
  starting transfers between devices: 43.6 us -> 39.2 us
  Pallas kernels: 8.47 us -> 5.49 us
    all_to_all x0 -> x1, blocking collectives: none -> 17.4 us  [on_device(): incoming = lax.all_to_all(outgoing, 'x', 0, 0, tiled=True)]
    ppermute x6, waiting for transfers between devices: 20.6 us -> 13.1 us  [shift(): lax.ppermute(value, along, [(i, (i + distance) % parts) for i in range(pa...]
    all_to_all x1 -> x0, starting transfers between devices: 7.32 us -> none  [on_device(): incoming = lax.all_to_all(outgoing, 'x', 0, 0, tiled=True)]
    all_to_all x1 -> x0, waiting for transfers between devices: 5.09 us -> none  [on_device(): incoming = lax.all_to_all(outgoing, 'x', 0, 0, tiled=True)]
    all_to_all x1, blocking collectives: 21.3 us -> 18.1 us  [on_device(): blocks = lax.all_to_all(combined, 'quarter', 0, 0, tiled=True)]
  transfers between devices with their start and end apart: 11 -> 10, of which waited for: 6 -> 5; matrix products, arithmetic and copies ran while one was open for 0% -> 0% of each run, Pallas kernels for 1% -> 1%
where the time goes in v11:
time: 176 us
  blocking collectives  104 us (59%)
  starting transfers between devices  39.2 us (22%)
  waiting for transfers between devices  25.6 us (15%)
  Pallas kernels  5.49 us (3%)
    all_gather x1, blocking collectives, on_device(): own = lax.all_gather(gather_rows(incoming), ('quarter', 'half'))  68.7 us
    ppermute x6, starting transfers between devices, shift(): lax.ppermute(value, along, [(i, (i + distance) % parts) for i in range(pa...  26.8 us
    all_to_all x1, blocking collectives, on_device(): blocks = lax.all_to_all(combined, 'quarter', 0, 0, tiled=True)  18.1 us
    all_to_all x1, blocking collectives, on_device(): incoming = lax.all_to_all(outgoing, 'x', 0, 0, tiled=True)  17.4 us
    ppermute x6, waiting for transfers between devices, shift(): lax.ppermute(value, along, [(i, (i + distance) % parts) for i in range(pa...  13.1 us
    all_to_all x1, waiting for transfers between devices, on_device(): returned = lax.all_to_all(partial_value, 'x', 0, 0, tiled=True)  12.5 us
    all_to_all x1, starting transfers between devices, on_device(): returned = lax.all_to_all(partial_value, 'x', 0, 0, tiled=True)  6.11 us
  transfers between devices with their start and end apart: 10, of which 5 were waited for; matrix products, arithmetic and copies ran while one was open for 0% of the time, Pallas kernels for 1%

profile of v11, /device:TPU:80, one launch (start us, length us, event | category | flops | bytes accessed | tf_op | source)
XLA Modules:
  0.0 175.7 jit_solution(10561375644578805076)
XLA Ops:
  0.0 1.7 dispatch.1
  1.7 1.9 %collective-permute-start = (bf16[6144,128]{1,0:T(8,128)(2,1)}, bf16[6144,128]{1,0:T(8,128)(2,1)S(1)}, u32[]{:S(2)}, u32[]{:S(2)}) collective-permute-start(bf16[6144,128]{1,0:T(8,128)(2,1)} %param.9), channel_id=1, source_target_pairs={{0,16},{16,0},{1,17},{17,1},{2,18},{18,2},{3,19},{19,3},{4,20},{20... | collective-permute-start | bytes 4718600 | tf_op jit(solution)/shard_map/ppermute | solution.py:317
  3.6 2.4 %collective-permute-start.1 = (bf16[6144,128]{1,0:T(8,128)(2,1)}, bf16[6144,128]{1,0:T(8,128)(2,1)S(1)}, u32[]{:S(2)}, u32[]{:S(2)}) collective-permute-start(bf16[6144,128]{1,0:T(8,128)(2,1)} %param.10), channel_id=1, source_target_pairs={{0,16},{16,0},{1,17},{17,1},{2,18},{18,2},{3,19},{19,3},{4,20},{20... | collective-permute-start | bytes 4718600 | tf_op jit(solution)/shard_map/ppermute | solution.py:318
  6.1 2.0 %collective-permute-start.4 = (bf16[128,6144]{1,0:T(8,128)(2,1)}, bf16[128,6144]{1,0:T(8,128)(2,1)S(1)}, u32[]{:S(2)}, u32[]{:S(2)}) collective-permute-start(bf16[128,6144]{1,0:T(8,128)(2,1)} %down_ref.1), channel_id=1, source_target_pairs={{0,16},{16,0},{1,17},{17,1},{2,18},{18,2},{3,19},{19,3},{4,20},{20... | collective-permute-start | bytes 4718600 | tf_op jit(solution)/shard_map/ppermute | solution.py:319
  8.0 17.4 %all_to_all.15.in_ref = bf16[8,20,384]{2,1,0:T(8,128)(2,1)S(1)} all-to-all(bf16[8,20,384]{2,1,0:T(8,128)(2,1)} %dispatch.1), channel_id=1, replica_groups=mesh['rep'=2,'x'=8,'core'=2,'quarter'=4,'half'=2,'odd'=2] {'x'}, dimensions={0} | all-to-all | bytes 245760 | tf_op jit(solution)/shard_map/all_to_all | solution.py:316
  25.5 68.7 %all-gather = bf16[1280,384]{1,0:T(8,128)(2,1)S(1)} all-gather(bf16[160,384]{1,0:T(8,128)(2,1)S(1)} %gather_rows.1), channel_id=2, replica_groups=mesh['rep'=2,'x'=8,'core'=2,'quarter'=4,'half'=2,'odd'=2] {'quarter','ha..., dimensions={0}, use_global_device_ids=true | all-gather | bytes 1105920 | tf_op jit(solution)/shard_map/all_gather | solution.py:320
  94.3 6.2 %collective-permute-start.2 = (bf16[4,160,384]{2,1,0:T(8,128)(2,1)S(1)}, bf16[4,160,384]{2,1,0:T(8,128)(2,1)S(1)}, u32[]{:S(2)}, u32[]{:S(2)}) collective-permute-start(bf16[4,160,384]{2,1,0:T(8,128)(2,1)S(1)} %bitcast.20), channel_id=1, source_target_pairs={{0,1},{1,2},{2,3},{3,4},{4,5},{5,6},{6,7},{7,8},{8,9},{9,10},{10,1... | collective-permute-start | bytes 1474568 | tf_op jit(solution)/shard_map/ppermute | solution.py:310
  100.5 5.1 %collective-permute-start.3 = (bf16[4,160,384]{2,1,0:T(8,128)(2,1)S(1)}, bf16[4,160,384]{2,1,0:T(8,128)(2,1)S(1)}, u32[]{:S(2)}, u32[]{:S(2)}) collective-permute-start(bf16[4,160,384]{2,1,0:T(8,128)(2,1)S(1)} %bitcast.19), channel_id=1, source_target_pairs={{0,15},{1,0},{2,1},{3,2},{4,3},{5,4},{6,5},{7,6},{8,7},{9,8},{10,9... | collective-permute-start | bytes 1474568 | tf_op jit(solution)/shard_map/ppermute | solution.py:310
  105.6 0.7 own_part.1
  106.3 4.0 %collective-permute-done.2.left_ref = bf16[4,160,384]{2,1,0:T(8,128)(2,1)S(1)} collective-permute-done((bf16[4,160,384]{2,1,0:T(8,128)(2,1)S(1)}, bf16[4,160,384]{2,1,0:T(8,128)(2,1)S(1)}, u32[]{:S(2)}, u32[]{:S(2)}) %collective-permute-start.2) | collective-permute-done | bytes 491552 | tf_op jit(solution)/shard_map/ppermute | solution.py:310
  110.4 1.5 collective-permute-done.3.right_ref
  111.9 1.2 ffn.1
  113.1 4.2 %collective-permute-start.5 = (bf16[4,160,384]{2,1,0:T(8,128)(2,1)S(1)}, bf16[4,160,384]{2,1,0:T(8,128)(2,1)S(1)}, u32[]{:S(2)}, u32[]{:S(2)}) collective-permute-start(bf16[4,160,384]{2,1,0:T(8,128)(2,1)S(1)} %get-tuple-element.23), channel_id=1, source_target_pairs={{0,1},{1,2},{2,3},{3,4},{4,5},{5,6},{6,7},{7,8},{8,9},{9,10},{10,1... | collective-permute-start | bytes 1474568 | tf_op jit(solution)/shard_map/ppermute | solution.py:310
  117.3 3.4 %collective-permute-start.6 = (bf16[4,160,384]{2,1,0:T(8,128)(2,1)S(1)}, bf16[4,160,384]{2,1,0:T(8,128)(2,1)S(1)}, u32[]{:S(2)}, u32[]{:S(2)}) collective-permute-start(bf16[4,160,384]{2,1,0:T(8,128)(2,1)S(1)} %get-tuple-element.24), channel_id=1, source_target_pairs={{0,15},{1,0},{2,1},{3,2},{4,3},{5,4},{6,5},{7,6},{8,7},{9,8},{10,9... | collective-permute-start | bytes 1474568 | tf_op jit(solution)/shard_map/ppermute | solution.py:310
  120.7 4.2 %collective-permute-start.7 = (bf16[2,160,384]{2,1,0:T(8,128)(2,1)S(1)}, bf16[2,160,384]{2,1,0:T(8,128)(2,1)S(1)}, u32[]{:S(2)}, u32[]{:S(2)}) collective-permute-start(bf16[2,160,384]{2,1,0:T(8,128)(2,1)S(1)} %get-tuple-element.25), channel_id=1, source_target_pairs={{0,2},{1,3},{2,4},{3,5},{4,6},{5,7},{6,8},{7,9},{8,10},{9,11},{10,... | collective-permute-start | bytes 737288 | tf_op jit(solution)/shard_map/ppermute | solution.py:310
  124.9 3.8 %collective-permute-start.8 = (bf16[2,160,384]{2,1,0:T(8,128)(2,1)S(1)}, bf16[2,160,384]{2,1,0:T(8,128)(2,1)S(1)}, u32[]{:S(2)}, u32[]{:S(2)}) collective-permute-start(bf16[2,160,384]{2,1,0:T(8,128)(2,1)S(1)} %get-tuple-element.26), channel_id=1, source_target_pairs={{0,14},{1,15},{2,0},{3,1},{4,2},{5,3},{6,4},{7,5},{8,6},{9,7},{10,... | collective-permute-start | bytes 737288 | tf_op jit(solution)/shard_map/ppermute | solution.py:310
  128.7 0.3 own_down.1.own_ref
  129.1 5.1 %collective-permute-done.7.left2_ref = bf16[2,160,384]{2,1,0:T(8,128)(2,1)S(1)} collective-permute-done((bf16[2,160,384]{2,1,0:T(8,128)(2,1)S(1)}, bf16[2,160,384]{2,1,0:T(8,128)(2,1)S(1)}, u32[]{:S(2)}, u32[]{:S(2)}) %collective-permute-start.7) | collective-permute-done | bytes 245792 | tf_op jit(solution)/shard_map/ppermute | solution.py:310
  134.2 2.4 %collective-permute-done.8.right2_ref = bf16[2,160,384]{2,1,0:T(8,128)(2,1)S(1)} collective-permute-done((bf16[2,160,384]{2,1,0:T(8,128)(2,1)S(1)}, bf16[2,160,384]{2,1,0:T(8,128)(2,1)S(1)}, u32[]{:S(2)}, u32[]{:S(2)}) %collective-permute-start.8) | collective-permute-done | bytes 245792 | tf_op jit(solution)/shard_map/ppermute | solution.py:310
  136.6 1.0 join.1
  137.6 6.1 %all-to-all-start.1 = ((bf16[8,80,384]{2,1,0:T(8,128)(2,1)}), bf16[8,80,384]{2,1,0:T(8,128)(2,1)S(1)}, u32[]{:S(2)}, u32[]{:S(2)}) async-start(bf16[8,80,384]{2,1,0:T(8,128)(2,1)} %join.1), calls=%async_computation.1 | async-start | bytes 983040 | tf_op jit(solution)/shard_map/all_to_all | solution.py:330
  144.1 12.5 %all-to-all-done.1 = bf16[8,80,384]{2,1,0:T(8,128)(2,1)S(1)} async-done(((bf16[8,80,384]{2,1,0:T(8,128)(2,1)}), bf16[8,80,384]{2,1,0:T(8,128)(2,1)S(1)}, u32[]{:S(2)}, u32[]{:S(2)}) %all-to-all-start.1) | async-done | bytes 491552 | tf_op jit(solution)/shard_map/all_to_all | solution.py:330
  157.0 18.1 %all_to_all.16 = bf16[4,32,384]{2,1,0:T(8,128)(2,1)S(1)} all-to-all(bf16[4,32,384]{2,1,0:T(8,128)(2,1)S(1)} %combine.1), channel_id=1, replica_groups=mesh['rep'=2,'x'=8,'core'=2,'quarter'=4,'half'=2,'odd'=2] {'quarter'}, dimensions={0} | all-to-all | bytes 196608 | tf_op jit(solution)/shard_map/all_to_all | solution.py:333
  175.1 0.6 reduce_sum.12
  (23 shorter events, 0.9 us)
Async XLA Ops:
  1.7 103.9 %collective-permute-start = (bf16[6144,128]{1,0:T(8,128)(2,1)}, bf16[6144,128]{1,0:T(8,128)(2,1)S(1)}, u32[]{:S(2)}, u32[]{:S(2)}) collective-permute-start(bf16[6144,128]{1,0:T(8,128)(2,1)} %param.9), channel_id=1, source_target_pairs={{0,16},{16,0},{1,17},{17,1},{2,18},{18,2},{3,19},{19,3},{4,20},{20... | collective-permute-start | bytes 4718600 | tf_op jit(solution)/shard_map/ppermute | solution.py:317
  3.6 101.9 %collective-permute-start.1 = (bf16[6144,128]{1,0:T(8,128)(2,1)}, bf16[6144,128]{1,0:T(8,128)(2,1)S(1)}, u32[]{:S(2)}, u32[]{:S(2)}) collective-permute-start(bf16[6144,128]{1,0:T(8,128)(2,1)} %param.10), channel_id=1, source_target_pairs={{0,16},{16,0},{1,17},{17,1},{2,18},{18,2},{3,19},{19,3},{4,20},{20... | collective-permute-start | bytes 4718600 | tf_op jit(solution)/shard_map/ppermute | solution.py:318
  6.1 105.8 %collective-permute-start.4 = (bf16[128,6144]{1,0:T(8,128)(2,1)}, bf16[128,6144]{1,0:T(8,128)(2,1)S(1)}, u32[]{:S(2)}, u32[]{:S(2)}) collective-permute-start(bf16[128,6144]{1,0:T(8,128)(2,1)} %down_ref.1), channel_id=1, source_target_pairs={{0,16},{16,0},{1,17},{17,1},{2,18},{18,2},{3,19},{19,3},{4,20},{20... | collective-permute-start | bytes 4718600 | tf_op jit(solution)/shard_map/ppermute | solution.py:319
  25.4 80.1 %copy-start.1 = (bf16[6144,128]{1,0:T(8,128)(2,1)S(1)}, bf16[6144,128]{1,0:T(8,128)(2,1)}, u32[]{:S(2)}) copy-start(bf16[6144,128]{1,0:T(8,128)(2,1)} %param.10) | copy-start | bytes 4718596
  25.5 80.1 %copy-start = (bf16[6144,128]{1,0:T(8,128)(2,1)S(1)}, bf16[6144,128]{1,0:T(8,128)(2,1)}, u32[]{:S(2)}) copy-start(bf16[6144,128]{1,0:T(8,128)(2,1)} %param.9) | copy-start | bytes 4718596
  94.3 16.1 %collective-permute-start.2 = (bf16[4,160,384]{2,1,0:T(8,128)(2,1)S(1)}, bf16[4,160,384]{2,1,0:T(8,128)(2,1)S(1)}, u32[]{:S(2)}, u32[]{:S(2)}) collective-permute-start(bf16[4,160,384]{2,1,0:T(8,128)(2,1)S(1)} %bitcast.20), channel_id=1, source_target_pairs={{0,1},{1,2},{2,3},{3,4},{4,5},{5,6},{6,7},{7,8},{8,9},{9,10},{10,1... | collective-permute-start | bytes 1474568 | tf_op jit(solution)/shard_map/ppermute | solution.py:310
  100.5 11.4 %collective-permute-start.3 = (bf16[4,160,384]{2,1,0:T(8,128)(2,1)S(1)}, bf16[4,160,384]{2,1,0:T(8,128)(2,1)S(1)}, u32[]{:S(2)}, u32[]{:S(2)}) collective-permute-start(bf16[4,160,384]{2,1,0:T(8,128)(2,1)S(1)} %bitcast.19), channel_id=1, source_target_pairs={{0,15},{1,0},{2,1},{3,2},{4,3},{5,4},{6,5},{7,6},{8,7},{9,8},{10,9... | collective-permute-start | bytes 1474568 | tf_op jit(solution)/shard_map/ppermute | solution.py:310
  105.6 6.3 %copy-start.2 = (bf16[128,6144]{1,0:T(8,128)(2,1)S(1)}, bf16[128,6144]{1,0:T(8,128)(2,1)}, u32[]{:S(2)}) copy-start(bf16[128,6144]{1,0:T(8,128)(2,1)} %down_ref.1) | copy-start | bytes 4718596
  113.1 23.5 %collective-permute-start.5 = (bf16[4,160,384]{2,1,0:T(8,128)(2,1)S(1)}, bf16[4,160,384]{2,1,0:T(8,128)(2,1)S(1)}, u32[]{:S(2)}, u32[]{:S(2)}) collective-permute-start(bf16[4,160,384]{2,1,0:T(8,128)(2,1)S(1)} %get-tuple-element.23), channel_id=1, source_target_pairs={{0,1},{1,2},{2,3},{3,4},{4,5},{5,6},{6,7},{7,8},{8,9},{9,10},{10,1... | collective-permute-start | bytes 1474568 | tf_op jit(solution)/shard_map/ppermute | solution.py:310
  117.3 19.3 %collective-permute-start.6 = (bf16[4,160,384]{2,1,0:T(8,128)(2,1)S(1)}, bf16[4,160,384]{2,1,0:T(8,128)(2,1)S(1)}, u32[]{:S(2)}, u32[]{:S(2)}) collective-permute-start(bf16[4,160,384]{2,1,0:T(8,128)(2,1)S(1)} %get-tuple-element.24), channel_id=1, source_target_pairs={{0,15},{1,0},{2,1},{3,2},{4,3},{5,4},{6,5},{7,6},{8,7},{9,8},{10,9... | collective-permute-start | bytes 1474568 | tf_op jit(solution)/shard_map/ppermute | solution.py:310
  120.7 13.5 %collective-permute-start.7 = (bf16[2,160,384]{2,1,0:T(8,128)(2,1)S(1)}, bf16[2,160,384]{2,1,0:T(8,128)(2,1)S(1)}, u32[]{:S(2)}, u32[]{:S(2)}) collective-permute-start(bf16[2,160,384]{2,1,0:T(8,128)(2,1)S(1)} %get-tuple-element.25), channel_id=1, source_target_pairs={{0,2},{1,3},{2,4},{3,5},{4,6},{5,7},{6,8},{7,9},{8,10},{9,11},{10,... | collective-permute-start | bytes 737288 | tf_op jit(solution)/shard_map/ppermute | solution.py:310
  124.9 11.7 %collective-permute-start.8 = (bf16[2,160,384]{2,1,0:T(8,128)(2,1)S(1)}, bf16[2,160,384]{2,1,0:T(8,128)(2,1)S(1)}, u32[]{:S(2)}, u32[]{:S(2)}) collective-permute-start(bf16[2,160,384]{2,1,0:T(8,128)(2,1)S(1)} %get-tuple-element.26), channel_id=1, source_target_pairs={{0,14},{1,15},{2,0},{3,1},{4,2},{5,3},{6,4},{7,5},{8,6},{9,7},{10,... | collective-permute-start | bytes 737288 | tf_op jit(solution)/shard_map/ppermute | solution.py:310
  129.0 14.7 %copy-start.3 = (s32[32,2]{0,1:T(2,128)S(1)}, s32[32,2]{0,1:T(2,128)}, u32[]{:S(2)}) copy-start(s32[32,2]{0,1:T(2,128)} %param.7) | copy-start | bytes 772
  129.0 14.8 %copy-start.4 = (f32[32,2]{0,1:T(2,128)S(1)}, f32[32,2]{0,1:T(2,128)}, u32[]{:S(2)}) copy-start(f32[32,2]{0,1:T(2,128)} %param.8) | copy-start | bytes 772
  137.6 19.0 %all-to-all-start.1 = ((bf16[8,80,384]{2,1,0:T(8,128)(2,1)}), bf16[8,80,384]{2,1,0:T(8,128)(2,1)S(1)}, u32[]{:S(2)}, u32[]{:S(2)}) async-start(bf16[8,80,384]{2,1,0:T(8,128)(2,1)} %join.1), calls=%async_computation.1 | async-start | bytes 983040 | tf_op jit(solution)/shard_map/all_to_all | solution.py:330

commit v12 on v11

--- a/solution.py
+++ b/solution.py
@@ -324,8 +324,10 @@
     hidden, to_right, to_left, to_right2, to_left2 = ffn(
         total, left, right, *blocks[:3], rest, down, down2
     )
-    left, right = shift(to_right, 1), shift(to_left, -1)
-    left2, right2 = shift(to_right2, 2), shift(to_left2, -2)
+    left2 = shift(to_right2, 2)
+    right2 = shift(to_left2, -2)
+    left = shift(to_right, 1)
+    right = shift(to_left, -1)
     partial_value = join(own_down(hidden, down, down2), left, right, left2, right2, chips)
     returned = lax.all_to_all(partial_value, "x", 0, 0, tiled=True)
     mix = mixing(ids, route_logits.T, chips)

time: 176 us -> 176 us (level)
  no operation moved by 1% of the time
where the time goes in v12:
time: 176 us
  blocking collectives  104 us (59%)
  starting transfers between devices  39.2 us (22%)
  waiting for transfers between devices  25.6 us (15%)
  Pallas kernels  5.49 us (3%)
    all_gather x1, blocking collectives, on_device(): own = lax.all_gather(gather_rows(incoming), ('quarter', 'half'))  68.7 us
    ppermute x6, starting transfers between devices, shift(): lax.ppermute(value, along, [(i, (i + distance) % parts) for i in range(pa...  26.8 us
    all_to_all x1, blocking collectives, on_device(): blocks = lax.all_to_all(combined, 'quarter', 0, 0, tiled=True)  18.1 us
    all_to_all x1, blocking collectives, on_device(): incoming = lax.all_to_all(outgoing, 'x', 0, 0, tiled=True)  17.4 us
    ppermute x6, waiting for transfers between devices, shift(): lax.ppermute(value, along, [(i, (i + distance) % parts) for i in range(pa...  13.1 us
    all_to_all x1, waiting for transfers between devices, on_device(): returned = lax.all_to_all(partial_value, 'x', 0, 0, tiled=True)  12.5 us
    all_to_all x1, starting transfers between devices, on_device(): returned = lax.all_to_all(partial_value, 'x', 0, 0, tiled=True)  6.11 us
  transfers between devices with their start and end apart: 10, of which 5 were waited for; matrix products, arithmetic and copies ran while one was open for 0% of the time, Pallas kernels for 1%

profile of v12, /device:TPU:80, one launch (start us, length us, event | category | flops | bytes accessed | tf_op | source)
XLA Modules:
  0.0 175.7 jit_solution(10561375644578805076)
XLA Ops:
  0.0 1.7 dispatch.1
  1.7 1.9 %collective-permute-start = (bf16[6144,128]{1,0:T(8,128)(2,1)}, bf16[6144,128]{1,0:T(8,128)(2,1)S(1)}, u32[]{:S(2)}, u32[]{:S(2)}) collective-permute-start(bf16[6144,128]{1,0:T(8,128)(2,1)} %param.9), channel_id=1, source_target_pairs={{0,16},{16,0},{1,17},{17,1},{2,18},{18,2},{3,19},{19,3},{4,20},{20... | collective-permute-start | bytes 4718600 | tf_op jit(solution)/shard_map/ppermute | solution.py:317
  3.6 2.4 %collective-permute-start.1 = (bf16[6144,128]{1,0:T(8,128)(2,1)}, bf16[6144,128]{1,0:T(8,128)(2,1)S(1)}, u32[]{:S(2)}, u32[]{:S(2)}) collective-permute-start(bf16[6144,128]{1,0:T(8,128)(2,1)} %param.10), channel_id=1, source_target_pairs={{0,16},{16,0},{1,17},{17,1},{2,18},{18,2},{3,19},{19,3},{4,20},{20... | collective-permute-start | bytes 4718600 | tf_op jit(solution)/shard_map/ppermute | solution.py:318
  6.1 2.0 %collective-permute-start.4 = (bf16[128,6144]{1,0:T(8,128)(2,1)}, bf16[128,6144]{1,0:T(8,128)(2,1)S(1)}, u32[]{:S(2)}, u32[]{:S(2)}) collective-permute-start(bf16[128,6144]{1,0:T(8,128)(2,1)} %down_ref.1), channel_id=1, source_target_pairs={{0,16},{16,0},{1,17},{17,1},{2,18},{18,2},{3,19},{19,3},{4,20},{20... | collective-permute-start | bytes 4718600 | tf_op jit(solution)/shard_map/ppermute | solution.py:319
  8.0 17.4 %all_to_all.15.in_ref = bf16[8,20,384]{2,1,0:T(8,128)(2,1)S(1)} all-to-all(bf16[8,20,384]{2,1,0:T(8,128)(2,1)} %dispatch.1), channel_id=1, replica_groups=mesh['rep'=2,'x'=8,'core'=2,'quarter'=4,'half'=2,'odd'=2] {'x'}, dimensions={0} | all-to-all | bytes 245760 | tf_op jit(solution)/shard_map/all_to_all | solution.py:316
  25.5 68.7 %all-gather = bf16[1280,384]{1,0:T(8,128)(2,1)S(1)} all-gather(bf16[160,384]{1,0:T(8,128)(2,1)S(1)} %gather_rows.1), channel_id=2, replica_groups=mesh['rep'=2,'x'=8,'core'=2,'quarter'=4,'half'=2,'odd'=2] {'quarter','ha..., dimensions={0}, use_global_device_ids=true | all-gather | bytes 1105920 | tf_op jit(solution)/shard_map/all_gather | solution.py:320
  94.3 6.2 %collective-permute-start.2 = (bf16[4,160,384]{2,1,0:T(8,128)(2,1)S(1)}, bf16[4,160,384]{2,1,0:T(8,128)(2,1)S(1)}, u32[]{:S(2)}, u32[]{:S(2)}) collective-permute-start(bf16[4,160,384]{2,1,0:T(8,128)(2,1)S(1)} %bitcast.20), channel_id=1, source_target_pairs={{0,1},{1,2},{2,3},{3,4},{4,5},{5,6},{6,7},{7,8},{8,9},{9,10},{10,1... | collective-permute-start | bytes 1474568 | tf_op jit(solution)/shard_map/ppermute | solution.py:310
  100.5 5.1 %collective-permute-start.3 = (bf16[4,160,384]{2,1,0:T(8,128)(2,1)S(1)}, bf16[4,160,384]{2,1,0:T(8,128)(2,1)S(1)}, u32[]{:S(2)}, u32[]{:S(2)}) collective-permute-start(bf16[4,160,384]{2,1,0:T(8,128)(2,1)S(1)} %bitcast.19), channel_id=1, source_target_pairs={{0,15},{1,0},{2,1},{3,2},{4,3},{5,4},{6,5},{7,6},{8,7},{9,8},{10,9... | collective-permute-start | bytes 1474568 | tf_op jit(solution)/shard_map/ppermute | solution.py:310
  105.6 0.7 own_part.1
  106.3 4.0 %collective-permute-done.2.left_ref = bf16[4,160,384]{2,1,0:T(8,128)(2,1)S(1)} collective-permute-done((bf16[4,160,384]{2,1,0:T(8,128)(2,1)S(1)}, bf16[4,160,384]{2,1,0:T(8,128)(2,1)S(1)}, u32[]{:S(2)}, u32[]{:S(2)}) %collective-permute-start.2) | collective-permute-done | bytes 491552 | tf_op jit(solution)/shard_map/ppermute | solution.py:310
  110.4 1.5 collective-permute-done.3.right_ref
  111.9 1.2 ffn.1
  113.1 4.2 %collective-permute-start.5 = (bf16[4,160,384]{2,1,0:T(8,128)(2,1)S(1)}, bf16[4,160,384]{2,1,0:T(8,128)(2,1)S(1)}, u32[]{:S(2)}, u32[]{:S(2)}) collective-permute-start(bf16[4,160,384]{2,1,0:T(8,128)(2,1)S(1)} %get-tuple-element.23), channel_id=1, source_target_pairs={{0,1},{1,2},{2,3},{3,4},{4,5},{5,6},{6,7},{7,8},{8,9},{9,10},{10,1... | collective-permute-start | bytes 1474568 | tf_op jit(solution)/shard_map/ppermute | solution.py:310
  117.3 3.4 %collective-permute-start.6 = (bf16[4,160,384]{2,1,0:T(8,128)(2,1)S(1)}, bf16[4,160,384]{2,1,0:T(8,128)(2,1)S(1)}, u32[]{:S(2)}, u32[]{:S(2)}) collective-permute-start(bf16[4,160,384]{2,1,0:T(8,128)(2,1)S(1)} %get-tuple-element.24), channel_id=1, source_target_pairs={{0,15},{1,0},{2,1},{3,2},{4,3},{5,4},{6,5},{7,6},{8,7},{9,8},{10,9... | collective-permute-start | bytes 1474568 | tf_op jit(solution)/shard_map/ppermute | solution.py:310
  120.7 4.2 %collective-permute-start.7 = (bf16[2,160,384]{2,1,0:T(8,128)(2,1)S(1)}, bf16[2,160,384]{2,1,0:T(8,128)(2,1)S(1)}, u32[]{:S(2)}, u32[]{:S(2)}) collective-permute-start(bf16[2,160,384]{2,1,0:T(8,128)(2,1)S(1)} %get-tuple-element.25), channel_id=1, source_target_pairs={{0,2},{1,3},{2,4},{3,5},{4,6},{5,7},{6,8},{7,9},{8,10},{9,11},{10,... | collective-permute-start | bytes 737288 | tf_op jit(solution)/shard_map/ppermute | solution.py:310
  124.9 3.8 %collective-permute-start.8 = (bf16[2,160,384]{2,1,0:T(8,128)(2,1)S(1)}, bf16[2,160,384]{2,1,0:T(8,128)(2,1)S(1)}, u32[]{:S(2)}, u32[]{:S(2)}) collective-permute-start(bf16[2,160,384]{2,1,0:T(8,128)(2,1)S(1)} %get-tuple-element.26), channel_id=1, source_target_pairs={{0,14},{1,15},{2,0},{3,1},{4,2},{5,3},{6,4},{7,5},{8,6},{9,7},{10,... | collective-permute-start | bytes 737288 | tf_op jit(solution)/shard_map/ppermute | solution.py:310
  128.7 0.3 own_down.1.own_ref
  129.1 5.1 %collective-permute-done.7.left2_ref = bf16[2,160,384]{2,1,0:T(8,128)(2,1)S(1)} collective-permute-done((bf16[2,160,384]{2,1,0:T(8,128)(2,1)S(1)}, bf16[2,160,384]{2,1,0:T(8,128)(2,1)S(1)}, u32[]{:S(2)}, u32[]{:S(2)}) %collective-permute-start.7) | collective-permute-done | bytes 245792 | tf_op jit(solution)/shard_map/ppermute | solution.py:310
  134.2 2.4 %collective-permute-done.8.right2_ref = bf16[2,160,384]{2,1,0:T(8,128)(2,1)S(1)} collective-permute-done((bf16[2,160,384]{2,1,0:T(8,128)(2,1)S(1)}, bf16[2,160,384]{2,1,0:T(8,128)(2,1)S(1)}, u32[]{:S(2)}, u32[]{:S(2)}) %collective-permute-start.8) | collective-permute-done | bytes 245792 | tf_op jit(solution)/shard_map/ppermute | solution.py:310
  136.6 1.0 join.1
  137.6 6.1 %all-to-all-start.1 = ((bf16[8,80,384]{2,1,0:T(8,128)(2,1)}), bf16[8,80,384]{2,1,0:T(8,128)(2,1)S(1)}, u32[]{:S(2)}, u32[]{:S(2)}) async-start(bf16[8,80,384]{2,1,0:T(8,128)(2,1)} %join.1), calls=%async_computation.1 | async-start | bytes 983040 | tf_op jit(solution)/shard_map/all_to_all | solution.py:332
  144.1 12.5 %all-to-all-done.1 = bf16[8,80,384]{2,1,0:T(8,128)(2,1)S(1)} async-done(((bf16[8,80,384]{2,1,0:T(8,128)(2,1)}), bf16[8,80,384]{2,1,0:T(8,128)(2,1)S(1)}, u32[]{:S(2)}, u32[]{:S(2)}) %all-to-all-start.1) | async-done | bytes 491552 | tf_op jit(solution)/shard_map/all_to_all | solution.py:332
  157.0 18.1 %all_to_all.16 = bf16[4,32,384]{2,1,0:T(8,128)(2,1)S(1)} all-to-all(bf16[4,32,384]{2,1,0:T(8,128)(2,1)S(1)} %combine.1), channel_id=1, replica_groups=mesh['rep'=2,'x'=8,'core'=2,'quarter'=4,'half'=2,'odd'=2] {'quarter'}, dimensions={0} | all-to-all | bytes 196608 | tf_op jit(solution)/shard_map/all_to_all | solution.py:335
  175.1 0.6 reduce_sum.12
  (23 shorter events, 0.9 us)
Async XLA Ops:
  1.7 103.9 %collective-permute-start = (bf16[6144,128]{1,0:T(8,128)(2,1)}, bf16[6144,128]{1,0:T(8,128)(2,1)S(1)}, u32[]{:S(2)}, u32[]{:S(2)}) collective-permute-start(bf16[6144,128]{1,0:T(8,128)(2,1)} %param.9), channel_id=1, source_target_pairs={{0,16},{16,0},{1,17},{17,1},{2,18},{18,2},{3,19},{19,3},{4,20},{20... | collective-permute-start | bytes 4718600 | tf_op jit(solution)/shard_map/ppermute | solution.py:317
  3.6 101.9 %collective-permute-start.1 = (bf16[6144,128]{1,0:T(8,128)(2,1)}, bf16[6144,128]{1,0:T(8,128)(2,1)S(1)}, u32[]{:S(2)}, u32[]{:S(2)}) collective-permute-start(bf16[6144,128]{1,0:T(8,128)(2,1)} %param.10), channel_id=1, source_target_pairs={{0,16},{16,0},{1,17},{17,1},{2,18},{18,2},{3,19},{19,3},{4,20},{20... | collective-permute-start | bytes 4718600 | tf_op jit(solution)/shard_map/ppermute | solution.py:318
  6.1 105.8 %collective-permute-start.4 = (bf16[128,6144]{1,0:T(8,128)(2,1)}, bf16[128,6144]{1,0:T(8,128)(2,1)S(1)}, u32[]{:S(2)}, u32[]{:S(2)}) collective-permute-start(bf16[128,6144]{1,0:T(8,128)(2,1)} %down_ref.1), channel_id=1, source_target_pairs={{0,16},{16,0},{1,17},{17,1},{2,18},{18,2},{3,19},{19,3},{4,20},{20... | collective-permute-start | bytes 4718600 | tf_op jit(solution)/shard_map/ppermute | solution.py:319
  25.4 80.1 %copy-start.1 = (bf16[6144,128]{1,0:T(8,128)(2,1)S(1)}, bf16[6144,128]{1,0:T(8,128)(2,1)}, u32[]{:S(2)}) copy-start(bf16[6144,128]{1,0:T(8,128)(2,1)} %param.10) | copy-start | bytes 4718596
  25.5 80.1 %copy-start = (bf16[6144,128]{1,0:T(8,128)(2,1)S(1)}, bf16[6144,128]{1,0:T(8,128)(2,1)}, u32[]{:S(2)}) copy-start(bf16[6144,128]{1,0:T(8,128)(2,1)} %param.9) | copy-start | bytes 4718596
  94.3 16.1 %collective-permute-start.2 = (bf16[4,160,384]{2,1,0:T(8,128)(2,1)S(1)}, bf16[4,160,384]{2,1,0:T(8,128)(2,1)S(1)}, u32[]{:S(2)}, u32[]{:S(2)}) collective-permute-start(bf16[4,160,384]{2,1,0:T(8,128)(2,1)S(1)} %bitcast.20), channel_id=1, source_target_pairs={{0,1},{1,2},{2,3},{3,4},{4,5},{5,6},{6,7},{7,8},{8,9},{9,10},{10,1... | collective-permute-start | bytes 1474568 | tf_op jit(solution)/shard_map/ppermute | solution.py:310
  100.5 11.4 %collective-permute-start.3 = (bf16[4,160,384]{2,1,0:T(8,128)(2,1)S(1)}, bf16[4,160,384]{2,1,0:T(8,128)(2,1)S(1)}, u32[]{:S(2)}, u32[]{:S(2)}) collective-permute-start(bf16[4,160,384]{2,1,0:T(8,128)(2,1)S(1)} %bitcast.19), channel_id=1, source_target_pairs={{0,15},{1,0},{2,1},{3,2},{4,3},{5,4},{6,5},{7,6},{8,7},{9,8},{10,9... | collective-permute-start | bytes 1474568 | tf_op jit(solution)/shard_map/ppermute | solution.py:310
  105.6 6.3 %copy-start.2 = (bf16[128,6144]{1,0:T(8,128)(2,1)S(1)}, bf16[128,6144]{1,0:T(8,128)(2,1)}, u32[]{:S(2)}) copy-start(bf16[128,6144]{1,0:T(8,128)(2,1)} %down_ref.1) | copy-start | bytes 4718596
  113.1 23.5 %collective-permute-start.5 = (bf16[4,160,384]{2,1,0:T(8,128)(2,1)S(1)}, bf16[4,160,384]{2,1,0:T(8,128)(2,1)S(1)}, u32[]{:S(2)}, u32[]{:S(2)}) collective-permute-start(bf16[4,160,384]{2,1,0:T(8,128)(2,1)S(1)} %get-tuple-element.23), channel_id=1, source_target_pairs={{0,1},{1,2},{2,3},{3,4},{4,5},{5,6},{6,7},{7,8},{8,9},{9,10},{10,1... | collective-permute-start | bytes 1474568 | tf_op jit(solution)/shard_map/ppermute | solution.py:310
  117.3 19.3 %collective-permute-start.6 = (bf16[4,160,384]{2,1,0:T(8,128)(2,1)S(1)}, bf16[4,160,384]{2,1,0:T(8,128)(2,1)S(1)}, u32[]{:S(2)}, u32[]{:S(2)}) collective-permute-start(bf16[4,160,384]{2,1,0:T(8,128)(2,1)S(1)} %get-tuple-element.24), channel_id=1, source_target_pairs={{0,15},{1,0},{2,1},{3,2},{4,3},{5,4},{6,5},{7,6},{8,7},{9,8},{10,9... | collective-permute-start | bytes 1474568 | tf_op jit(solution)/shard_map/ppermute | solution.py:310
  120.7 13.5 %collective-permute-start.7 = (bf16[2,160,384]{2,1,0:T(8,128)(2,1)S(1)}, bf16[2,160,384]{2,1,0:T(8,128)(2,1)S(1)}, u32[]{:S(2)}, u32[]{:S(2)}) collective-permute-start(bf16[2,160,384]{2,1,0:T(8,128)(2,1)S(1)} %get-tuple-element.25), channel_id=1, source_target_pairs={{0,2},{1,3},{2,4},{3,5},{4,6},{5,7},{6,8},{7,9},{8,10},{9,11},{10,... | collective-permute-start | bytes 737288 | tf_op jit(solution)/shard_map/ppermute | solution.py:310
  124.9 11.7 %collective-permute-start.8 = (bf16[2,160,384]{2,1,0:T(8,128)(2,1)S(1)}, bf16[2,160,384]{2,1,0:T(8,128)(2,1)S(1)}, u32[]{:S(2)}, u32[]{:S(2)}) collective-permute-start(bf16[2,160,384]{2,1,0:T(8,128)(2,1)S(1)} %get-tuple-element.26), channel_id=1, source_target_pairs={{0,14},{1,15},{2,0},{3,1},{4,2},{5,3},{6,4},{7,5},{8,6},{9,7},{10,... | collective-permute-start | bytes 737288 | tf_op jit(solution)/shard_map/ppermute | solution.py:310
  129.0 14.7 %copy-start.3 = (s32[32,2]{0,1:T(2,128)S(1)}, s32[32,2]{0,1:T(2,128)}, u32[]{:S(2)}) copy-start(s32[32,2]{0,1:T(2,128)} %param.7) | copy-start | bytes 772
  129.0 14.8 %copy-start.4 = (f32[32,2]{0,1:T(2,128)S(1)}, f32[32,2]{0,1:T(2,128)}, u32[]{:S(2)}) copy-start(f32[32,2]{0,1:T(2,128)} %param.8) | copy-start | bytes 772
  137.6 19.0 %all-to-all-start.1 = ((bf16[8,80,384]{2,1,0:T(8,128)(2,1)}), bf16[8,80,384]{2,1,0:T(8,128)(2,1)S(1)}, u32[]{:S(2)}, u32[]{:S(2)}) async-start(bf16[8,80,384]{2,1,0:T(8,128)(2,1)} %join.1), calls=%async_computation.1 | async-start | bytes 983040 | tf_op jit(solution)/shard_map/all_to_all | solution.py:332

commit v13 on v11

--- a/solution.py
+++ b/solution.py
@@ -225,15 +225,16 @@
     )(total, left, right, *weights)
 
 
-def own_down_kernel(hidden_ref, down_ref, down2_ref, out_ref):
+def own_down_kernel(hidden_ref, down_ref, down2_ref, left_ref, right_ref, out_ref):
     blocks, _, depth = out_ref.shape
     for b in range(0, blocks, 2):
         partial = down_pair(hidden_ref[...], (down_ref, down2_ref), b, class_at(0), depth)
-        out_ref[b] = partial[:, :depth]
-        out_ref[b + 1] = partial[:, depth:]
-
-
-def own_down(hidden, down, down2):
+        for i, own in ((b, partial[:, :depth]), (b + 1, partial[:, depth:])):
+            near = left_ref[i].astype(jnp.float32) + right_ref[i].astype(jnp.float32)
+            out_ref[i] = own + near
+
+
+def own_down(hidden, down, down2, left, right):
     rows = hidden.shape[0]
     width, model = down.shape
     depth = model // (CLASSES * QUARTERS)
@@ -243,17 +244,16 @@
         cost_estimate=cost(rows * model * width, 4000000),
         compiler_params=pltpu.CompilerParams(vmem_limit_bytes=16 << 20),
         name="own_down",
-    )(hidden, down, down2)
-
-
-def join_kernel(own_ref, left_ref, right_ref, left2_ref, right2_ref, out_ref):
-    blocks = own_ref.shape[0]
+    )(hidden, down, down2, left, right)
+
+
+def join_kernel(near_ref, left2_ref, right2_ref, out_ref):
+    blocks = near_ref.shape[0]
     chips = out_ref.shape[0]
     half = blocks // 2
     for q in range(blocks):
-        both = own_ref[q] + left_ref[q].astype(jnp.float32) + right_ref[q].astype(jnp.float32)
         third = left2_ref[q] if q < half else right2_ref[q - half]
-        both = (both + third.astype(jnp.float32)).astype(jnp.bfloat16)
+        both = (near_ref[q] + third.astype(jnp.float32)).astype(jnp.bfloat16)
         at = QUARTERS * MAIN + q * TAIL
         for chip in range(chips):
             tail = chips * MAIN + chip * TAIL
@@ -261,15 +261,15 @@
             out_ref[chip, at : at + TAIL] = both[tail : tail + TAIL]
 
 
-def join(own, left, right, left2, right2, chips):
-    blocks, rows, depth = own.shape
+def join(near, left2, right2, chips):
+    blocks, rows, depth = near.shape
     return pl.pallas_call(
         join_kernel,
         out_shape=jax.ShapeDtypeStruct((chips, blocks * CAP, depth), jnp.bfloat16),
         cost_estimate=cost(blocks * rows * depth, 12 * blocks * rows * depth),
         compiler_params=pltpu.CompilerParams(vmem_limit_bytes=16 << 20),
         name="join",
-    )(own, left, right, left2, right2)
+    )(near, left2, right2)
 
 
 def combine_kernel(mix_ref, back_ref, out_ref):
@@ -326,7 +326,7 @@
     )
     left, right = shift(to_right, 1), shift(to_left, -1)
     left2, right2 = shift(to_right2, 2), shift(to_left2, -2)
-    partial_value = join(own_down(hidden, down, down2), left, right, left2, right2, chips)
+    partial_value = join(own_down(hidden, down, down2, left, right), left2, right2, chips)
     returned = lax.all_to_all(partial_value, "x", 0, 0, tiled=True)
     mix = mixing(ids, route_logits.T, chips)
     combined = combine(mix, returned.reshape(chips * QUARTERS * CAP, depth), count, QUARTERS)

time: 176 us -> 176 us (level)
  transfers between devices with their start and end apart: 10 -> 10, of which waited for: 5 -> 6; matrix products, arithmetic and copies ran while one was open for 0% -> 0% of each run, Pallas kernels for 1% -> 1%
where the time goes in v13:
time: 176 us
  blocking collectives  104 us (59%)
  starting transfers between devices  39.2 us (22%)
  waiting for transfers between devices  25.6 us (15%)
  Pallas kernels  5.35 us (3%)
    all_gather x1, blocking collectives, on_device(): own = lax.all_gather(gather_rows(incoming), ('quarter', 'half'))  68.7 us
    ppermute x6, starting transfers between devices, shift(): lax.ppermute(value, along, [(i, (i + distance) % parts) for i in range(pa...  26.8 us
    all_to_all x1, blocking collectives, on_device(): blocks = lax.all_to_all(combined, 'quarter', 0, 0, tiled=True)  18.1 us
    all_to_all x1, blocking collectives, on_device(): incoming = lax.all_to_all(outgoing, 'x', 0, 0, tiled=True)  17.4 us
    ppermute x6, waiting for transfers between devices, shift(): lax.ppermute(value, along, [(i, (i + distance) % parts) for i in range(pa...  13.1 us
    all_to_all x1, waiting for transfers between devices, on_device(): returned = lax.all_to_all(partial_value, 'x', 0, 0, tiled=True)  12.5 us
    all_to_all x1, starting transfers between devices, on_device(): returned = lax.all_to_all(partial_value, 'x', 0, 0, tiled=True)  6.11 us
  transfers between devices with their start and end apart: 10, of which 6 were waited for; matrix products, arithmetic and copies ran while one was open for 0% of the time, Pallas kernels for 1%

profile of v13, /device:TPU:80, one launch (start us, length us, event | category | flops | bytes accessed | tf_op | source)
XLA Modules:
  0.0 175.6 jit_solution(3535696724462509129)
XLA Ops:
  0.0 1.7 dispatch.1
  1.7 1.9 %collective-permute-start = (bf16[6144,128]{1,0:T(8,128)(2,1)}, bf16[6144,128]{1,0:T(8,128)(2,1)S(1)}, u32[]{:S(2)}, u32[]{:S(2)}) collective-permute-start(bf16[6144,128]{1,0:T(8,128)(2,1)} %param.9), channel_id=1, source_target_pairs={{0,16},{16,0},{1,17},{17,1},{2,18},{18,2},{3,19},{19,3},{4,20},{20... | collective-permute-start | bytes 4718600 | tf_op jit(solution)/shard_map/ppermute | solution.py:317
  3.6 2.4 %collective-permute-start.1 = (bf16[6144,128]{1,0:T(8,128)(2,1)}, bf16[6144,128]{1,0:T(8,128)(2,1)S(1)}, u32[]{:S(2)}, u32[]{:S(2)}) collective-permute-start(bf16[6144,128]{1,0:T(8,128)(2,1)} %param.10), channel_id=1, source_target_pairs={{0,16},{16,0},{1,17},{17,1},{2,18},{18,2},{3,19},{19,3},{4,20},{20... | collective-permute-start | bytes 4718600 | tf_op jit(solution)/shard_map/ppermute | solution.py:318
  6.1 2.0 %collective-permute-start.4 = (bf16[128,6144]{1,0:T(8,128)(2,1)}, bf16[128,6144]{1,0:T(8,128)(2,1)S(1)}, u32[]{:S(2)}, u32[]{:S(2)}) collective-permute-start(bf16[128,6144]{1,0:T(8,128)(2,1)} %down_ref.1), channel_id=1, source_target_pairs={{0,16},{16,0},{1,17},{17,1},{2,18},{18,2},{3,19},{19,3},{4,20},{20... | collective-permute-start | bytes 4718600 | tf_op jit(solution)/shard_map/ppermute | solution.py:319
  8.0 17.4 %all_to_all.15.in_ref = bf16[8,20,384]{2,1,0:T(8,128)(2,1)S(1)} all-to-all(bf16[8,20,384]{2,1,0:T(8,128)(2,1)} %dispatch.1), channel_id=1, replica_groups=mesh['rep'=2,'x'=8,'core'=2,'quarter'=4,'half'=2,'odd'=2] {'x'}, dimensions={0} | all-to-all | bytes 245760 | tf_op jit(solution)/shard_map/all_to_all | solution.py:316
  25.5 68.7 %all-gather = bf16[1280,384]{1,0:T(8,128)(2,1)S(1)} all-gather(bf16[160,384]{1,0:T(8,128)(2,1)S(1)} %gather_rows.1), channel_id=2, replica_groups=mesh['rep'=2,'x'=8,'core'=2,'quarter'=4,'half'=2,'odd'=2] {'quarter','ha..., dimensions={0}, use_global_device_ids=true | all-gather | bytes 1105920 | tf_op jit(solution)/shard_map/all_gather | solution.py:320
  94.3 6.2 %collective-permute-start.2 = (bf16[4,160,384]{2,1,0:T(8,128)(2,1)S(1)}, bf16[4,160,384]{2,1,0:T(8,128)(2,1)S(1)}, u32[]{:S(2)}, u32[]{:S(2)}) collective-permute-start(bf16[4,160,384]{2,1,0:T(8,128)(2,1)S(1)} %bitcast.20), channel_id=1, source_target_pairs={{0,1},{1,2},{2,3},{3,4},{4,5},{5,6},{6,7},{7,8},{8,9},{9,10},{10,1... | collective-permute-start | bytes 1474568 | tf_op jit(solution)/shard_map/ppermute | solution.py:310
  100.5 5.1 %collective-permute-start.3 = (bf16[4,160,384]{2,1,0:T(8,128)(2,1)S(1)}, bf16[4,160,384]{2,1,0:T(8,128)(2,1)S(1)}, u32[]{:S(2)}, u32[]{:S(2)}) collective-permute-start(bf16[4,160,384]{2,1,0:T(8,128)(2,1)S(1)} %bitcast.19), channel_id=1, source_target_pairs={{0,15},{1,0},{2,1},{3,2},{4,3},{5,4},{6,5},{7,6},{8,7},{9,8},{10,9... | collective-permute-start | bytes 1474568 | tf_op jit(solution)/shard_map/ppermute | solution.py:310
  105.6 0.7 own_part.1
  106.3 4.0 %collective-permute-done.2.left_ref = bf16[4,160,384]{2,1,0:T(8,128)(2,1)S(1)} collective-permute-done((bf16[4,160,384]{2,1,0:T(8,128)(2,1)S(1)}, bf16[4,160,384]{2,1,0:T(8,128)(2,1)S(1)}, u32[]{:S(2)}, u32[]{:S(2)}) %collective-permute-start.2) | collective-permute-done | bytes 491552 | tf_op jit(solution)/shard_map/ppermute | solution.py:310
  110.4 1.5 collective-permute-done.3.right_ref
  111.9 1.2 ffn.1
  113.1 4.2 %collective-permute-start.5 = (bf16[4,160,384]{2,1,0:T(8,128)(2,1)S(1)}, bf16[4,160,384]{2,1,0:T(8,128)(2,1)S(1)}, u32[]{:S(2)}, u32[]{:S(2)}) collective-permute-start(bf16[4,160,384]{2,1,0:T(8,128)(2,1)S(1)} %get-tuple-element.23), channel_id=1, source_target_pairs={{0,1},{1,2},{2,3},{3,4},{4,5},{5,6},{6,7},{7,8},{8,9},{9,10},{10,1... | collective-permute-start | bytes 1474568 | tf_op jit(solution)/shard_map/ppermute | solution.py:310
  117.3 3.4 %collective-permute-start.6 = (bf16[4,160,384]{2,1,0:T(8,128)(2,1)S(1)}, bf16[4,160,384]{2,1,0:T(8,128)(2,1)S(1)}, u32[]{:S(2)}, u32[]{:S(2)}) collective-permute-start(bf16[4,160,384]{2,1,0:T(8,128)(2,1)S(1)} %get-tuple-element.24), channel_id=1, source_target_pairs={{0,15},{1,0},{2,1},{3,2},{4,3},{5,4},{6,5},{7,6},{8,7},{9,8},{10,9... | collective-permute-start | bytes 1474568 | tf_op jit(solution)/shard_map/ppermute | solution.py:310
  120.7 4.2 %collective-permute-start.7 = (bf16[2,160,384]{2,1,0:T(8,128)(2,1)S(1)}, bf16[2,160,384]{2,1,0:T(8,128)(2,1)S(1)}, u32[]{:S(2)}, u32[]{:S(2)}) collective-permute-start(bf16[2,160,384]{2,1,0:T(8,128)(2,1)S(1)} %get-tuple-element.25), channel_id=1, source_target_pairs={{0,2},{1,3},{2,4},{3,5},{4,6},{5,7},{6,8},{7,9},{8,10},{9,11},{10,... | collective-permute-start | bytes 737288 | tf_op jit(solution)/shard_map/ppermute | solution.py:310
  124.9 3.8 %collective-permute-start.8 = (bf16[2,160,384]{2,1,0:T(8,128)(2,1)S(1)}, bf16[2,160,384]{2,1,0:T(8,128)(2,1)S(1)}, u32[]{:S(2)}, u32[]{:S(2)}) collective-permute-start(bf16[2,160,384]{2,1,0:T(8,128)(2,1)S(1)} %get-tuple-element.26), channel_id=1, source_target_pairs={{0,14},{1,15},{2,0},{3,1},{4,2},{5,3},{6,4},{7,5},{8,6},{9,7},{10,... | collective-permute-start | bytes 737288 | tf_op jit(solution)/shard_map/ppermute | solution.py:310
  128.7 2.3 %collective-permute-done.6.right_ref = bf16[4,160,384]{2,1,0:T(8,128)(2,1)S(1)} collective-permute-done((bf16[4,160,384]{2,1,0:T(8,128)(2,1)S(1)}, bf16[4,160,384]{2,1,0:T(8,128)(2,1)S(1)}, u32[]{:S(2)}, u32[]{:S(2)}) %collective-permute-start.6) | collective-permute-done | bytes 491552 | tf_op jit(solution)/shard_map/ppermute | solution.py:310
  131.4 2.8 %collective-permute-done.7.left2_ref = bf16[2,160,384]{2,1,0:T(8,128)(2,1)S(1)} collective-permute-done((bf16[2,160,384]{2,1,0:T(8,128)(2,1)S(1)}, bf16[2,160,384]{2,1,0:T(8,128)(2,1)S(1)}, u32[]{:S(2)}, u32[]{:S(2)}) %collective-permute-start.7) | collective-permute-done | bytes 245792 | tf_op jit(solution)/shard_map/ppermute | solution.py:310
  134.2 2.4 %collective-permute-done.8.right2_ref = bf16[2,160,384]{2,1,0:T(8,128)(2,1)S(1)} collective-permute-done((bf16[2,160,384]{2,1,0:T(8,128)(2,1)S(1)}, bf16[2,160,384]{2,1,0:T(8,128)(2,1)S(1)}, u32[]{:S(2)}, u32[]{:S(2)}) %collective-permute-start.8) | collective-permute-done | bytes 245792 | tf_op jit(solution)/shard_map/ppermute | solution.py:310
  136.6 0.9 join.1
  137.5 6.1 %all-to-all-start.1 = ((bf16[8,80,384]{2,1,0:T(8,128)(2,1)}), bf16[8,80,384]{2,1,0:T(8,128)(2,1)S(1)}, u32[]{:S(2)}, u32[]{:S(2)}) async-start(bf16[8,80,384]{2,1,0:T(8,128)(2,1)} %join.1), calls=%async_computation.1 | async-start | bytes 983040 | tf_op jit(solution)/shard_map/all_to_all | solution.py:330
  144.0 12.5 %all-to-all-done.1 = bf16[8,80,384]{2,1,0:T(8,128)(2,1)S(1)} async-done(((bf16[8,80,384]{2,1,0:T(8,128)(2,1)}), bf16[8,80,384]{2,1,0:T(8,128)(2,1)S(1)}, u32[]{:S(2)}, u32[]{:S(2)}) %all-to-all-start.1) | async-done | bytes 491552 | tf_op jit(solution)/shard_map/all_to_all | solution.py:330
  156.8 18.1 %all_to_all.16 = bf16[4,32,384]{2,1,0:T(8,128)(2,1)S(1)} all-to-all(bf16[4,32,384]{2,1,0:T(8,128)(2,1)S(1)} %combine.1), channel_id=1, replica_groups=mesh['rep'=2,'x'=8,'core'=2,'quarter'=4,'half'=2,'odd'=2] {'quarter'}, dimensions={0} | all-to-all | bytes 196608 | tf_op jit(solution)/shard_map/all_to_all | solution.py:333
  174.9 0.6 reduce_sum.12
  (23 shorter events, 1.2 us)
Async XLA Ops:
  1.7 103.9 %collective-permute-start = (bf16[6144,128]{1,0:T(8,128)(2,1)}, bf16[6144,128]{1,0:T(8,128)(2,1)S(1)}, u32[]{:S(2)}, u32[]{:S(2)}) collective-permute-start(bf16[6144,128]{1,0:T(8,128)(2,1)} %param.9), channel_id=1, source_target_pairs={{0,16},{16,0},{1,17},{17,1},{2,18},{18,2},{3,19},{19,3},{4,20},{20... | collective-permute-start | bytes 4718600 | tf_op jit(solution)/shard_map/ppermute | solution.py:317
  3.6 101.9 %collective-permute-start.1 = (bf16[6144,128]{1,0:T(8,128)(2,1)}, bf16[6144,128]{1,0:T(8,128)(2,1)S(1)}, u32[]{:S(2)}, u32[]{:S(2)}) collective-permute-start(bf16[6144,128]{1,0:T(8,128)(2,1)} %param.10), channel_id=1, source_target_pairs={{0,16},{16,0},{1,17},{17,1},{2,18},{18,2},{3,19},{19,3},{4,20},{20... | collective-permute-start | bytes 4718600 | tf_op jit(solution)/shard_map/ppermute | solution.py:318
  6.1 105.8 %collective-permute-start.4 = (bf16[128,6144]{1,0:T(8,128)(2,1)}, bf16[128,6144]{1,0:T(8,128)(2,1)S(1)}, u32[]{:S(2)}, u32[]{:S(2)}) collective-permute-start(bf16[128,6144]{1,0:T(8,128)(2,1)} %down_ref.1), channel_id=1, source_target_pairs={{0,16},{16,0},{1,17},{17,1},{2,18},{18,2},{3,19},{19,3},{4,20},{20... | collective-permute-start | bytes 4718600 | tf_op jit(solution)/shard_map/ppermute | solution.py:319
  25.4 80.1 %copy-start.1 = (bf16[6144,128]{1,0:T(8,128)(2,1)S(1)}, bf16[6144,128]{1,0:T(8,128)(2,1)}, u32[]{:S(2)}) copy-start(bf16[6144,128]{1,0:T(8,128)(2,1)} %param.10) | copy-start | bytes 4718596
  25.5 80.1 %copy-start = (bf16[6144,128]{1,0:T(8,128)(2,1)S(1)}, bf16[6144,128]{1,0:T(8,128)(2,1)}, u32[]{:S(2)}) copy-start(bf16[6144,128]{1,0:T(8,128)(2,1)} %param.9) | copy-start | bytes 4718596
  94.3 16.1 %collective-permute-start.2 = (bf16[4,160,384]{2,1,0:T(8,128)(2,1)S(1)}, bf16[4,160,384]{2,1,0:T(8,128)(2,1)S(1)}, u32[]{:S(2)}, u32[]{:S(2)}) collective-permute-start(bf16[4,160,384]{2,1,0:T(8,128)(2,1)S(1)} %bitcast.20), channel_id=1, source_target_pairs={{0,1},{1,2},{2,3},{3,4},{4,5},{5,6},{6,7},{7,8},{8,9},{9,10},{10,1... | collective-permute-start | bytes 1474568 | tf_op jit(solution)/shard_map/ppermute | solution.py:310
  100.5 11.4 %collective-permute-start.3 = (bf16[4,160,384]{2,1,0:T(8,128)(2,1)S(1)}, bf16[4,160,384]{2,1,0:T(8,128)(2,1)S(1)}, u32[]{:S(2)}, u32[]{:S(2)}) collective-permute-start(bf16[4,160,384]{2,1,0:T(8,128)(2,1)S(1)} %bitcast.19), channel_id=1, source_target_pairs={{0,15},{1,0},{2,1},{3,2},{4,3},{5,4},{6,5},{7,6},{8,7},{9,8},{10,9... | collective-permute-start | bytes 1474568 | tf_op jit(solution)/shard_map/ppermute | solution.py:310
  105.6 6.3 %copy-start.2 = (bf16[128,6144]{1,0:T(8,128)(2,1)S(1)}, bf16[128,6144]{1,0:T(8,128)(2,1)}, u32[]{:S(2)}) copy-start(bf16[128,6144]{1,0:T(8,128)(2,1)} %down_ref.1) | copy-start | bytes 4718596
  113.1 15.6 %collective-permute-start.5 = (bf16[4,160,384]{2,1,0:T(8,128)(2,1)S(1)}, bf16[4,160,384]{2,1,0:T(8,128)(2,1)S(1)}, u32[]{:S(2)}, u32[]{:S(2)}) collective-permute-start(bf16[4,160,384]{2,1,0:T(8,128)(2,1)S(1)} %get-tuple-element.23), channel_id=1, source_target_pairs={{0,1},{1,2},{2,3},{3,4},{4,5},{5,6},{6,7},{7,8},{8,9},{9,10},{10,1... | collective-permute-start | bytes 1474568 | tf_op jit(solution)/shard_map/ppermute | solution.py:310
  117.3 13.7 %collective-permute-start.6 = (bf16[4,160,384]{2,1,0:T(8,128)(2,1)S(1)}, bf16[4,160,384]{2,1,0:T(8,128)(2,1)S(1)}, u32[]{:S(2)}, u32[]{:S(2)}) collective-permute-start(bf16[4,160,384]{2,1,0:T(8,128)(2,1)S(1)} %get-tuple-element.24), channel_id=1, source_target_pairs={{0,15},{1,0},{2,1},{3,2},{4,3},{5,4},{6,5},{7,6},{8,7},{9,8},{10,9... | collective-permute-start | bytes 1474568 | tf_op jit(solution)/shard_map/ppermute | solution.py:310
  120.7 13.5 %collective-permute-start.7 = (bf16[2,160,384]{2,1,0:T(8,128)(2,1)S(1)}, bf16[2,160,384]{2,1,0:T(8,128)(2,1)S(1)}, u32[]{:S(2)}, u32[]{:S(2)}) collective-permute-start(bf16[2,160,384]{2,1,0:T(8,128)(2,1)S(1)} %get-tuple-element.25), channel_id=1, source_target_pairs={{0,2},{1,3},{2,4},{3,5},{4,6},{5,7},{6,8},{7,9},{8,10},{9,11},{10,... | collective-permute-start | bytes 737288 | tf_op jit(solution)/shard_map/ppermute | solution.py:310
  124.9 11.7 %collective-permute-start.8 = (bf16[2,160,384]{2,1,0:T(8,128)(2,1)S(1)}, bf16[2,160,384]{2,1,0:T(8,128)(2,1)S(1)}, u32[]{:S(2)}, u32[]{:S(2)}) collective-permute-start(bf16[2,160,384]{2,1,0:T(8,128)(2,1)S(1)} %get-tuple-element.26), channel_id=1, source_target_pairs={{0,14},{1,15},{2,0},{3,1},{4,2},{5,3},{6,4},{7,5},{8,6},{9,7},{10,... | collective-permute-start | bytes 737288 | tf_op jit(solution)/shard_map/ppermute | solution.py:310
  131.4 12.2 %copy-start.3 = (s32[32,2]{0,1:T(2,128)S(1)}, s32[32,2]{0,1:T(2,128)}, u32[]{:S(2)}) copy-start(s32[32,2]{0,1:T(2,128)} %param.7) | copy-start | bytes 772
  131.4 12.3 %copy-start.4 = (f32[32,2]{0,1:T(2,128)S(1)}, f32[32,2]{0,1:T(2,128)}, u32[]{:S(2)}) copy-start(f32[32,2]{0,1:T(2,128)} %param.8) | copy-start | bytes 772
  137.5 19.0 %all-to-all-start.1 = ((bf16[8,80,384]{2,1,0:T(8,128)(2,1)}), bf16[8,80,384]{2,1,0:T(8,128)(2,1)S(1)}, u32[]{:S(2)}, u32[]{:S(2)}) async-start(bf16[8,80,384]{2,1,0:T(8,128)(2,1)} %join.1), calls=%async_computation.1 | async-start | bytes 983040 | tf_op jit(solution)/shard_map/all_to_all | solution.py:330
